TPU v7x, 128 devices: a whole 4x4x4 slice. The times are simulated.
128 devices in a mesh: wide: 16 (over z, y), deep: 8 (over x, core).
Axes of the slice: x: 4, y: 4, z: 4, core: 2. Of those that a mesh axis runs over, the one named last changes fastest.
Arguments:
- coarse_density: float32 [128, 8, 960], P('wide', None, 'deep'), may hold values from 0.8 to 1.6
- coarse_velocity: float32 [3, 128, 8, 960], P(None, 'wide', None, 'deep'), may hold values from -0.4 to 0.4
- coarse_pressure: float32 [128, 8, 960], P('wide', None, 'deep'), may hold values from 0.8 to 1.6
- fine_density: float32 [8, 64, 16, 256], P('deep', 'wide'), may hold values from 0.8 to 1.6
- fine_velocity: float32 [8, 64, 3, 16, 256], P('deep', 'wide'), may hold values from -0.4 to 0.4
- fine_pressure: float32 [8, 64, 16, 256], P('deep', 'wide'), may hold values from 0.8 to 1.6
- patch_count: int32 [8, 16], P('deep'), may hold values from 1 to 4, 32 in all within a row
- region_start: int32 [8], P('deep'), may hold values from 0 to 207
Outputs:
- coarse_state: float32 [5, 128, 8, 960], P(None, 'wide', None, 'deep')
- fine_state: float32 [8, 64, 5, 16, 256], P('deep', 'wide')
Inputs may be any that keep to these rules, and one draw needn't show every extreme that they name: `patch_count`: each deep row's counts sum to 32, and some device of every row holds 4 patches.
All inputs are finite; a program needn't handle non-finite values.
Results may differ from a plain program's by a relative error of at most 0.0003.
Values sent between devices are 32-bit elements; how exact they have to be, the bound alone decides.
No kernel may reach another device: no remote copies, remote signals or barrier semaphores. Data moves between devices by JAX's collectives and lax.ppermute only.
A program may use at most 192 MiB of HBM per device.

v0:
```python
import jax
import jax.numpy as jnp
from jax import lax
from jax.experimental import pallas as pl
from jax.experimental.pallas import tpu as pltpu
from jax.sharding import PartitionSpec as P


f32 = jnp.float32
i32 = jnp.int32
HIGH = lax.Precision.HIGHEST
PLACES = 13
WIDE = 16
DEEP = 8
LIVE_Z = 120
FILL = (1.0, 0.0, 0.0, 0.0, 2.5)


def lanes():
    return lax.broadcasted_iota(i32, (8, 128), 1)


def subs():
    return lax.broadcasted_iota(i32, (8, 128), 0)


def roll(v, shift, axis):
    size = v.shape[axis]
    shift = shift % size
    return v if shift == 0 else pltpu.roll(v, shift, axis)


def y_shift(v, k):
    y = lanes() & 15
    if k > 0:
        return jnp.where(y < 16 - k, roll(v, -k, 1), roll(v, 16 - k, 1))
    return jnp.where(y >= -k, roll(v, -k, 1), roll(v, -k - 16, 1))


def sub_shift(v, k):
    return roll(v, -k, 0)


def lane_shift(v, k):
    return roll(v, -k, 1)


def prims_of(u):
    inv = 1.0 / u[0]
    vx, vy, vz = u[1] * inv, u[2] * inv, u[3] * inv
    kinetic = 0.5 * u[0] * (vx * vx + vy * vy + vz * vz)
    return [u[0], vx, vy, vz, 0.4 * (u[4] - kinetic)]


def cons_of(p):
    kinetic = 0.5 * p[0] * (p[1] * p[1] + p[2] * p[2] + p[3] * p[3])
    return [p[0], p[0] * p[1], p[0] * p[2], p[0] * p[3], p[4] / 0.4 + kinetic]


def recon(a, b, c, d, e):
    da, db, dc, dd = b - a, c - b, d - c, e - d
    ga, gb, gc = db - da, dc - db, dd - dc
    db2, dc2 = db + db, dc + dc
    ta, tb, tc = ga + db2, db + dc, gc - dc2
    k = 13.0 / 3.0
    sa = (k * ga) * ga + (ta * ta + 4e-6)
    sb = (k * gb) * gb + (tb * tb + 4e-6)
    sc = (k * gc) * gc + (tc * tc + 4e-6)
    pa, pb, pc = sa * sa, (sb * sb) * (1.0 / 6.0), sc * sc
    bc, ac, ab = pb * pc, pa * pc, pa * pb
    ab3, bc3 = 3.0 * ab, 3.0 * bc
    db4, dc4 = db2 + db2, dc2 + dc2
    left = bc * (db4 + db - (da + da)) + ac * (db + dc2) + ab3 * (dc4 - dd)
    right = ab * (dc4 + dc - (dd + dd)) + ac * (dc + db2) + bc3 * (db4 - da)
    left = left / (6.0 * (bc + ac + ab3))
    right = right / (6.0 * (ab + ac + bc3))
    return c + left, c - right


def hllc(lt, rt, n):
    o1, o2 = [k for k in (1, 2, 3) if k != n]
    dl, ul, pl_ = lt[0], lt[n], lt[4]
    dr, ur, pr = rt[0], rt[n], rt[4]
    il, ir = 1.0 / dl, 1.0 / dr
    cl = jnp.sqrt(1.4 * pl_ * il)
    cr = jnp.sqrt(1.4 * pr * ir)
    slow = jnp.minimum(ul - cl, ur - cr)
    fast = jnp.maximum(ul + cl, ur + cr)
    ml = dl * (slow - ul)
    mr = dr * (fast - ur)
    mid = (pr - pl_ + ml * ul - mr * ur) / (ml - mr)
    use = (slow >= 0.0) | (mid >= 0.0)
    d = jnp.where(use, dl, dr)
    u = jnp.where(use, ul, ur)
    t1 = jnp.where(use, lt[o1], rt[o1])
    t2 = jnp.where(use, lt[o2], rt[o2])
    p = jnp.where(use, pl_, pr)
    inv = jnp.where(use, il, ir)
    mass = jnp.where(use, ml, mr)
    wave = jnp.where(use, slow, fast)
    star = (use & (slow < 0.0)) | (jnp.logical_not(use) & (fast > 0.0))
    energy = 2.5 * p + 0.5 * d * (u * u + t1 * t1 + t2 * t2)
    du = d * u
    factor = mass / (wave - mid)
    e_star = energy * inv + (mid - u) * (mid + p / mass)
    out = [None] * 5
    flux = {0: du, n: du * u + p, o1: du * t1, o2: du * t2, 4: u * (energy + p)}
    state = {0: d, n: du, o1: d * t1, o2: d * t2, 4: energy}
    goal = {0: factor, n: factor * mid, o1: factor * t1, o2: factor * t2, 4: factor * e_star}
    for c in range(5):
        out[c] = jnp.where(star, flux[c] + wave * (goal[c] - state[c]), flux[c])
    return out


def repeat(count, unroll, body):
    turns = count // unroll

    def turn(t, carry):
        for j in range(unroll):
            body(t * unroll + j)
        return carry

    if turns > 0:
        lax.fori_loop(0, turns, turn, 0)
    for j in range(turns * unroll, count):
        body(j)


UNROLL_CELLS, UNROLL_FACES, UNROLL_ROLLS = 2, 9, 4


def major_pass(q, sl, sr, fx, n, count=10):
    def cells(m):
        for c in range(5):
            l, r = recon(*[q[c, m + k] for k in range(5)])
            sl[c, m] = l
            sr[c, m] = r

    repeat(count, UNROLL_CELLS, cells)

    def faces(f):
        out = hllc([sl[c, f] for c in range(5)], [sr[c, f + 1] for c in range(5)], n)
        for c in range(5):
            fx[c, f] = out[c]

    repeat(count - 1, UNROLL_FACES, faces)


def roll_pass(q, d, shift, n, count=8, keep=None, at=3):
    def cells(m):
        left, right = [], []
        for c in range(5):
            v = q[c, m + at]
            l, r = recon(shift(v, -2), shift(v, -1), v, shift(v, 1), shift(v, 2))
            left.append(shift(l, -1))
            right.append(r)
        out = hllc(left, right, n)
        for c in range(5):
            d[c, m] = d[c, m] + (shift(out[c], 1) - out[c])
            if keep is not None:
                keep[c, m] = out[c]

    repeat(count, UNROLL_ROLLS, cells)


def swap_groups(v):
    lane = lanes()
    for b in range(3):
        bit = ((lane >> (4 + b)) & 1) == 1
        step = 16 << b
        w = list(v)
        for m in range(8):
            if not (m >> b) & 1:
                lo, hi = v[m], v[m | (1 << b)]
                w[m] = jnp.where(bit, roll(hi, step, 1), lo)
                w[m | (1 << b)] = jnp.where(bit, hi, roll(lo, -step, 1))
        v = w
    return v


Z0, OWNER, COL, COUNT, ADJ, MATCH = 0, 2, 4, 8, 9, 10


def column_places(column, anchor):
    d = (column - anchor) & 15
    bad = 2 - lax.rem(d, 3)
    off_a = d + 16 * jnp.where(bad == 0, 1, 0)
    off_b = d + 16 * jnp.where(bad == 2, 1, 2)

    def ident(off):
        place = anchor + off
        return jnp.where(place >= WIDE * PLACES, place - WIDE * PLACES, place)

    swap = ident(off_b) < ident(off_a)
    first = jnp.where(swap, off_b, off_a)
    second = jnp.where(swap, off_a, off_b)
    heights = [ident(first) >> 4, ident(second) >> 4]
    ranks = [2 * lax.div(o, 3) + lax.rem(o, 3) for o in (first, second)]
    return heights, ranks


def info_kernel(counts, start, here, info):
    me = here[0]
    anchor = start[0]
    h, ranks = column_places(me, anchor)
    low, _ = column_places((me + 15) & 15, anchor)
    high, _ = column_places((me + 1) & 15, anchor)
    total = jnp.int32(0)
    begin = jnp.int32(0)
    mine = jnp.int32(0)
    owner = [jnp.int32(0), jnp.int32(0)]
    for w in range(WIDE):
        n = counts[0, w]
        begin = jnp.where(me == w, total, begin)
        mine = jnp.where(me == w, n, mine)
        total = total + n
        for p in range(2):
            owner[p] = owner[p] + jnp.where(ranks[p] >= total, 1, 0)
    for p in range(2):
        info[Z0 + p] = 8 * (h[p] + 1)
        info[OWNER + p] = jnp.minimum(owner[p], WIDE - 1)
        for side, other in enumerate((low, high)):
            info[MATCH + 2 * side + p] = jnp.where(
                other[0] == h[p], 0, jnp.where(other[1] == h[p], 1, 2)
            )
    for s in range(4):
        serial = begin + s
        place = anchor + 3 * (serial >> 1) + (serial & 1)
        info[COL + s] = place & 15
    info[COUNT] = mine
    info[ADJ] = jnp.where(h[1] == h[0] + 1, 1, 0)
    info[14] = 0
    info[15] = 0


def send_kernel(info, dens, vel, pres, out, sem):
    for s in range(4):

        @pl.when(s < info[COUNT])
        def _():
            copies = slot_copies(info, dens, vel, pres, out, sem, s)
            for cp in copies:
                cp.start()

    for s in range(4):

        @pl.when(s < info[COUNT])
        def _():
            for cp in slot_copies(info, dens, vel, pres, out, sem, s):
                cp.wait()


def slot_copies(info, dens, vel, pres, out, sem, s):
    to = info[COL + s]
    copies = []
    for xh in range(2):
        for zh in range(2):
            rows, cols = pl.ds(8 * xh, 8), pl.ds(128 * zh, 128)
            goal = pl.ds(16 * xh + 8 * zh, 8)
            k = 2 * xh + zh
            copies.append(
                pltpu.make_async_copy(
                    dens.at[0, s, rows, cols], out.at[to, 0, goal, :], sem.at[s, 3 * k]
                )
            )
            copies.append(
                pltpu.make_async_copy(
                    vel.at[0, s, :, rows, cols],
                    out.at[to, pl.ds(1, 3), goal, :],
                    sem.at[s, 3 * k + 1],
                )
            )
            copies.append(
                pltpu.make_async_copy(
                    pres.at[0, s, rows, cols], out.at[to, 4, goal, :], sem.at[s, 3 * k + 2]
                )
            )
    return copies


def patch_copies(info, far, near, sem, out):
    copies = []
    for p in range(2):
        for xh in range(2):
            there = far.at[info[OWNER + p], :, pl.ds(16 * xh, 16), :]
            here = near.at[:, pl.ds((4 * xh + 2 * p) * 8, 16), :]
            a, b = (here, there) if out else (there, here)
            copies.append(pltpu.make_async_copy(a, b, sem.at[2 * p + xh]))
    return copies


def take_kernel(info, far, s, lo, hi, near, sem):
    copies = patch_copies(info, far, near, sem, False)
    for cp in copies:
        cp.start()
    for cp in copies:
        cp.wait()
    for m in range(8):
        u = cons_of([near[c, pl.ds(m, 8, stride=8), :] for c in range(5)])
        for c in range(5):
            s[c, m] = u[c]
    lo[...] = s[:, 0:3, 0:4, :]
    hi[...] = s[:, 5:8, 4:8, :]


def give_kernel(info, s, far, near, sem):
    for m in range(8):
        for c in range(5):
            near[c, pl.ds(m, 8, stride=8), :] = s[c, m]
    copies = patch_copies(info, far, near, sem, True)
    for cp in copies:
        cp.start()
    for cp in copies:
        cp.wait()


def home_copies(info, far, out, sem, s):
    copies = []
    for xh in range(2):
        for zh in range(2):
            copies.append(
                pltpu.make_async_copy(
                    far.at[info[COL + s], :, pl.ds(16 * xh + 8 * zh, 8), :],
                    out.at[0, s, :, pl.ds(8 * xh, 8), pl.ds(128 * zh, 128)],
                    sem.at[s, 2 * xh + zh],
                )
            )
    return copies


def home_kernel(info, far, initial, out, sem):
    for s in range(4):

        @pl.when(s < info[COUNT])
        def _():
            for cp in home_copies(info, far, out, sem, s):
                cp.start()

    for s in range(4):

        @pl.when(s < info[COUNT])
        def _():
            for cp in home_copies(info, far, out, sem, s):
                cp.wait()


def pack_edge(u, first):
    lane = lanes()
    out = jnp.zeros((8, 128), f32)
    for c in range(5):
        for x in range(8):
            k = 3 * (8 * c + x)
            out = jnp.where((lane >= k) & (lane < k + 3), roll(u[c][x], k - first, 1), out)
    return out


def prep_kernel(dens_far, vel_far, pres_far, u, plo, phi, dens, vel, pres, sem):
    pairs = ((dens_far, dens), (vel_far, vel), (pres_far, pres))
    copies = [pltpu.make_async_copy(a, b, sem.at[k]) for k, (a, b) in enumerate(pairs)]
    for cp in copies:
        cp.start()
    for cp in copies:
        cp.wait()
    state = cons_of([dens[...], vel[0], vel[1], vel[2], pres[...]])
    for c in range(5):
        u[c] = jnp.full((8, 8, 128), FILL[c], f32)
        u[c, :, :, pl.ds(0, LIVE_Z)] = state[c]
    plo[...] = pack_edge([[u[c, x] for x in range(8)] for c in range(5)], 0)
    phi[...] = pack_edge([[u[c, x] for x in range(8)] for c in range(5)], LIVE_Z - 3)


def with_halo(v, below, above, k):
    lane = lanes()
    v = jnp.where(lane >= 125, roll(below, 125 - k, 1), v)
    return jnp.where((lane >= 120) & (lane < 123), roll(above, 120 - k, 1), v)


def halo_kernel(u, zl, zh, out):
    below, above = zl[...], zh[...]
    for c in range(5):
        for x in range(8):
            out[c, x] = with_halo(u[c, x], below, above, 3 * (8 * c + x))


def coarse_rates(layers, own, zl, zh, q, sl, sr, fx, d, keep):
    count = len(layers)
    for i, layer in enumerate(layers):
        state = [layer(c) for c in range(5)]
        if own is not None and 0 <= i - own < 8:
            state = [
                with_halo(state[c], zl[...], zh[...], 3 * (8 * c + i - own)) for c in range(5)
            ]
        p = prims_of(state)
        for c in range(5):
            q[c, i] = p[c]
    major_pass(q, sl, sr, fx, 1, count - 4)
    for c in range(5):
        for m in range(count - 6):
            d[c, m] = fx[c, m + 1] - fx[c, m]
    roll_pass(q, d, sub_shift, 2, count - 6)
    roll_pass(q, d, lane_shift, 3, count - 6, keep)


def take_layer(ref, x):
    return lambda c: ref[c, x]


def coarse_one(u, ul, ur, mid, plo, phi, fa, fz, q, sl, sr, fx, d, keep):
    refs = [take_layer(ref, x) for ref in (ul, u, ur) for x in range(8)]
    coarse_rates(refs, None, None, None, q, sl, sr, fx, d, keep)
    live = lanes() < LIVE_Z
    for c in range(5):
        fa[c, 0] = fx[c, 5]
        fa[c, 1] = fx[c, 13]
        for m in range(18):
            mid[c, m] = jnp.where(live, refs[m + 3](c) - 0.2 * d[c, m], FILL[c])
        for m in range(8):
            fz[c, m] = keep[c, m + 5]
    plo[...] = pack_edge([[mid[c, x + 5] for x in range(8)] for c in range(5)], 0)
    phi[...] = pack_edge([[mid[c, x + 5] for x in range(8)] for c in range(5)], LIVE_Z - 3)


def coarse_two(u0, ul, ur, fa, fza, u, zl, zh, new, mx, mz, q, sl, sr, fx, d, keep):
    refs = [take_layer(ref, x) for ref in (ul, u0, ur) for x in range(8)]
    coarse_rates([take_layer(u, m) for m in range(18)], 5, zl, zh, q, sl, sr, fx, d, keep)
    live = lanes() < LIVE_Z
    for c in range(5):
        mx[c, 0] = 0.5 * (fa[c, 0] + fx[c, 2])
        mx[c, 1] = 0.5 * (fa[c, 1] + fx[c, 10])
        for m in range(8):
            mz[c, m] = 0.5 * (fza[c, m] + keep[c, m + 2])
        for m in range(12):
            new[c, m] = jnp.where(
                live, 0.5 * (refs[m + 6](c) + u[c, m + 3]) - 0.1 * d[c, m], FILL[c]
            )


def dot(a, b):
    return jnp.dot(a, b, precision=HIGH, preferred_element_type=f32)


def dot_nt(a, b):
    return lax.dot_general(
        a, b, (((1,), (1,)), ((), ())), precision=HIGH, preferred_element_type=f32
    )


def iota2(shape, axis):
    return lax.broadcasted_iota(i32, shape, axis)


def pick(cond):
    return jnp.where(cond, 1.0, 0.0).astype(f32)


def rim_kernel(info, *refs, late):
    gx, gz = refs[-2:]
    if late:
        new = refs[0]
        low, high = [take_layer(new, 0), take_layer(new, 1)], [take_layer(new, 10), take_layer(new, 11)]
        own = lambda c: new[c, 2:10]
    else:
        u, ul, ur = refs[:3]
        low, high = [take_layer(ul, 6), take_layer(ul, 7)], [take_layer(ur, 0), take_layer(ur, 1)]
        own = lambda c: u[c]
    z = iota2((128, 128), 0)
    l = iota2((128, 128), 1)
    y8 = iota2((32, 128), 0) & 7
    ymask = pick(y8 == ((iota2((32, 128), 1) & 15) >> 1))
    layers = []
    for c in range(5):
        layers += [low[0](c), low[1](c), high[0](c), high[1](c)]
    rows = jnp.concatenate(layers, axis=0)
    parts = []
    for pz in range(4):
        start = info[Z0 + pz // 2] + 4 * (pz % 2)
        parts.append(dot(rows, pick(z == start + (l >> 5))))
    r = iota2((24, 128), 0)
    k = iota2((24, 128), 1)
    g, s = r >> 3, r & 7
    layer = jnp.where(s < 4, jnp.where(g == 0, 0, 1), jnp.where(g == 2, 3, 2))
    left = pick(((s & 3) == (k >> 5)) & (layer == ((k >> 3) & 3)))
    for c in range(5):
        stack = jnp.concatenate([part[32 * c : 32 * c + 32] * ymask for part in parts], axis=0)
        gx[c] = dot(left, stack).reshape(3, 8, 128)
    pnum = (s >> 1) & 1
    start = jnp.where(pnum == 0, info[Z0], info[Z0 + 1])
    off = jnp.where((s & 1) == 0, jnp.where(g == 0, -2, -1), jnp.where(g == 2, 9, 8))
    choose = pick(k == start + off)
    er = iota2((64, 256), 0)
    ec = iota2((64, 256), 1)
    spread = pick(((er >> 3) == (ec >> 5)) & ((er & 7) == ((ec & 15) >> 1)))
    for c in range(5):
        cols = dot_nt(choose, own(c).reshape(64, 128))
        both = dot(cols, spread)
        gz[c] = jnp.where(s < 4, both[:, :128], both[:, 128:]).reshape(3, 8, 128)


def blend(old, new, theta, c, g):
    if theta == 0.0:
        return old[c, g]
    if theta == 1.0:
        return new[c, g]
    return 0.5 * old[c, g] + 0.5 * new[c, g]


def split_refs(refs, flags):
    return [refs.pop(0) if flag else None for flag in flags]


def places_of_rows():
    sub = subs()
    return sub >= 4, (sub & 2) != 0, (sub & 1) != 0


THETA = (0.0, 0.5, 0.5, 1.0)


def yz_kernel(*refs, stage):
    theta = THETA[stage]
    refs = list(refs)
    info, s, old, new, reg = split_refs(refs, (1, 1, theta < 1.0, theta > 0.0, stage))
    pr, d, rz, q, sl, sr, fx = refs
    _, second, upper_z = places_of_rows()
    for m in range(8):
        p = prims_of([s[c, m] for c in range(5)])
        for c in range(5):
            pr[c, m] = p[c]
    adjacent = info[ADJ] == 1
    inner_low = upper_z | (second & adjacent)
    inner_high = jnp.logical_not(upper_z) | (jnp.logical_not(second) & adjacent)
    for c in range(5):
        t = swap_groups([pr[c, m] for m in range(8)])
        for m in range(8):
            q[c, m + 3] = t[m]
    for g in range(3):
        p = prims_of([blend(old, new, theta, c, g) for c in range(5)])
        for c in range(5):
            q[c, g] = jnp.where(inner_low, roll(q[c, g + 8], 1, 0), p[c])
            q[c, g + 11] = jnp.where(inner_high, roll(q[c, g + 3], -1, 0), p[c])
    major_pass(q, sl, sr, fx, 3)
    for c in range(5):
        face = jnp.where(upper_z, fx[c, 8], fx[c, 0])
        rz[c] = face if reg is None else reg[c] + face
        t = swap_groups([fx[c, m + 1] - fx[c, m] for m in range(8)])
        for m in range(8):
            d[c, m] = t[m]
    roll_pass(pr, d, y_shift, 2, at=0)


def x_kernel(*refs, stage):
    theta = THETA[stage]
    refs = list(refs)
    info, s, rl, rh, pr, d, old, new, base, reg = split_refs(
        refs, (1,) * 6 + (theta < 1.0, theta > 0.0, stage % 2, stage)
    )
    out, rx, lo, hi = split_refs(refs, (1, 1, stage < 3, stage < 3))
    q, sl, sr, fx, near = refs
    upper_x, second, _ = places_of_rows()
    near[:, :, 0:4, :] = rl[...]
    near[:, :, 4:8, :] = rh[...]
    code = jnp.where(
        upper_x,
        jnp.where(second, info[MATCH + 3], info[MATCH + 2]),
        jnp.where(second, info[MATCH + 1], info[MATCH]),
    )
    none = code == 2
    same = code == jnp.where(second, 1, 0)
    for c in range(5):
        for m in range(8):
            q[c, m + 3] = pr[c, m]
    for g in range(3):
        state = []
        for c in range(5):
            v = near[c, g]
            other = jnp.where(second, roll(v, 2, 0), roll(v, -2, 0))
            state.append(
                jnp.where(none, blend(old, new, theta, c, g), jnp.where(same, v, other))
            )
        p = prims_of(state)
        for c in range(5):
            q[c, g] = jnp.where(upper_x, roll(pr[c, g + 5], 4, 0), p[c])
            q[c, g + 11] = jnp.where(upper_x, p[c], roll(pr[c, g], 4, 0))
    major_pass(q, sl, sr, fx, 1)
    for c in range(5):
        face = jnp.where(upper_x, fx[c, 8], fx[c, 0])
        rx[c] = face if reg is None else reg[c] + face
        for m in range(8):
            change = d[c, m] + (fx[c, m + 1] - fx[c, m])
            if base is None:
                out[c, m] = s[c, m] - 0.2 * change
            else:
                out[c, m] = 0.5 * (base[c, m] + s[c, m]) - 0.1 * change
    if stage < 3:
        lo[...] = out[:, 0:3, 0:4, :]
        hi[...] = out[:, 5:8, 4:8, :]


def sync_kernel(info, s, rx, rz, new, mx, mz, out, low, high):
    lane = lanes()
    y = pick(subs() == ((lane & 15) >> 1))
    z0 = [info[Z0], info[Z0 + 1]]
    lr = iota2((128, 128), 0)
    zc = iota2((128, 128), 1)
    spread = [pick(zc == z0[pz // 2] + 4 * (pz % 2) + (lr >> 5)) for pz in range(4)]
    mean = None
    for pz in range(4):
        rows = []
        for c in range(5):
            for x in range(8):
                m, at = 2 * (x % 4), 4 * (x // 4) + pz
                v = s[c, m] + s[c, m + 1]
                rows.append(jnp.broadcast_to(v[at : at + 1], (8, 128)) * y)
        term = dot(jnp.concatenate(rows, axis=0), spread[pz])
        mean = term if mean is None else mean + term
    edge = [[info[MATCH + 2 * side + p] == 2 for p in range(2)] for side in range(2)]
    inside = [(lane >= z0[p]) & (lane < z0[p] + 8) for p in range(2)]
    placed = None
    for pz in range(4):
        rows = []
        for side in range(2):
            for c in range(5):
                v = rx[c]
                at = 4 * side + pz
                rows.append(jnp.broadcast_to(v[at : at + 1], (8, 128)) * y)
        term = dot(jnp.concatenate(rows, axis=0), spread[pz])
        placed = term if placed is None else placed + term
    for side, goal in ((0, low), (1, high)):
        keep = (inside[0] & edge[side][0]) | (inside[1] & edge[side][1])
        for c in range(5):
            at = 8 * (5 * side + c)
            delta = 0.2 * mx[c, side] - 0.0125 * placed[at : at + 8]
            goal[c] = jnp.where(keep, delta if side == 0 else -delta, 0.0)
    adjacent = info[ADJ] == 1
    apart = jnp.logical_not(adjacent)
    at_low = (lane == z0[0] - 1) | ((lane == z0[1] - 1) & apart)
    at_high = (lane == z0[1] + 8) | ((lane == z0[0] + 8) & apart)
    sub = subs()
    is_second = (sub & 2) != 0
    is_high = (sub & 1) != 0
    where_z = jnp.where(is_second, z0[1], z0[0]) + jnp.where(is_high, 8, -1)
    gone = adjacent & (is_second != is_high)
    sign = jnp.where(is_high, 0.0125, -0.0125)
    put = jnp.where((lane == where_z) & jnp.logical_not(gone), sign, 0.0)
    er = iota2((64, 128), 0)
    el = iota2((64, 128), 1)
    group = [
        pick(((er >> 3) == 4 * xh + (el >> 5)) & ((er & 7) == ((el & 15) >> 1)))
        for xh in range(2)
    ]
    covered = inside[0] | inside[1]
    for c in range(5):
        v = rz[c]
        n = dot_nt(group[0], jnp.where(sub < 4, v, 0.0))
        n = n + dot_nt(group[1], jnp.where(sub < 4, 0.0, v))
        fix = dot(n, put)
        for x in range(8):
            f = 0.2 * mz[c, x]
            w = new[c, x + 2] + fix[8 * x : 8 * x + 8]
            w = w + jnp.where(at_low, roll(f, -1, 1), 0.0)
            w = w - jnp.where(at_high, f, 0.0)
            at = 8 * (8 * c + x)
            out[c, x] = jnp.where(covered, 0.125 * mean[at : at + 8], w)


def last_kernel(info, w, left, right, out):
    lane = lanes()
    z0 = [info[Z0], info[Z0 + 1]]
    inside = [(lane >= z0[p]) & (lane < z0[p] + 8) for p in range(2)]
    covered = inside[0] | inside[1]
    for c in range(5):
        first = w[c, 0] + jnp.where(covered, 0.0, left[c])
        final = w[c, 7] + jnp.where(covered, 0.0, right[c])
        out[c, 0] = first[:, :LIVE_Z]
        out[c, 7] = final[:, :LIVE_Z]
        for x in range(1, 7):
            out[c, x] = w[c, x, :, pl.ds(0, LIVE_Z)]


VM = pl.BlockSpec(memory_space=pltpu.VMEM)
SM = pl.BlockSpec(memory_space=pltpu.SMEM)
LIMIT = 8 << 20
ANY = pl.BlockSpec(memory_space=pl.ANY)
HBM = pl.BlockSpec(memory_space=pltpu.HBM)


def call(kernel, ins, outs, scratch, args, alias=None):
    shapes = [jax.ShapeDtypeStruct(shape, dtype) for shape, dtype, _ in outs]
    return pl.pallas_call(
        kernel,
        in_specs=ins,
        out_specs=[spec for _, _, spec in outs],
        out_shape=shapes,
        scratch_shapes=scratch,
        input_output_aliases=alias or {},
        compiler_params=pltpu.CompilerParams(vmem_limit_bytes=LIMIT),
    )(*args)


def vm(*shape):
    return (shape, f32, VM)


def buf(*shape):
    return pltpu.VMEM(shape, f32)


FIELD = (5, 8, 8, 128)
WIDE_PASS = [buf(5, 24, 8, 128)] + [buf(5, 20, 8, 128)] * 2 + [buf(5, 19, 8, 128)] + [buf(5, 18, 8, 128)] * 2
PASS = [buf(5, 14, 8, 128), buf(5, 10, 8, 128), buf(5, 10, 8, 128), buf(5, 9, 8, 128)]


def ring(axis, up):
    count = DEEP if axis == "deep" else WIDE
    pairs = [(i, (i + 1) % count) for i in range(count)]
    return pairs if up else [(j, i) for i, j in pairs]


def swap(lo, hi, axis):
    below = lax.ppermute(hi, axis, ring(axis, True))
    return below, lax.ppermute(lo, axis, ring(axis, False))


def local(dens, vel, pres, fdens, fvel, fpres, counts, start):
    here = lax.axis_index("wide").astype(i32).reshape(1)
    (info,) = call(info_kernel, [SM] * 3, [((16,), i32, SM)], [], (counts, start, here))
    dma = pltpu.SemaphoreType.DMA
    moved = (WIDE, 5, 32, 128)
    (sent,) = call(
        send_kernel,
        [SM, ANY, ANY, ANY],
        [(moved, f32, ANY)],
        [dma((4, 12))],
        (info, fdens, fvel, fpres),
    )
    came = lax.all_to_all(sent, "wide", split_axis=0, concat_axis=0, tiled=True)

    edge = vm(8, 128)
    side = vm(5, 3, 8, 128)
    u0, plo, phi = call(
        prep_kernel,
        [HBM] * 3,
        [vm(*FIELD), edge, edge],
        [buf(8, 8, LIVE_Z), buf(3, 8, 8, LIVE_Z), buf(8, 8, LIVE_Z), dma((3,))],
        [pltpu.with_memory_space_constraint(x, pltpu.HBM) for x in (dens, vel, pres)],
    )
    zl0, zh0 = swap(plo, phi, "deep")
    (u0,) = call(halo_kernel, [VM] * 3, [vm(*FIELD)], [], (u0, zl0, zh0))
    ul, ur = swap(u0, u0, "wide")
    mid, plo, phi, fa, fza = call(
        coarse_one,
        [VM] * 3,
        [vm(5, 18, 8, 128), edge, edge, vm(5, 2, 8, 128), vm(*FIELD)],
        WIDE_PASS,
        (u0, ul, ur),
    )
    zl1, zh1 = swap(plo, phi, "deep")
    new, mx, mz = call(
        coarse_two,
        [VM] * 8,
        [vm(5, 12, 8, 128), vm(5, 2, 8, 128), vm(*FIELD)],
        WIDE_PASS,
        (u0, ul, ur, fa, fza, mid, zl1, zh1),
    )

    def rims(args, late):
        return call(
            lambda *refs: rim_kernel(*refs, late=late),
            [SM] + [VM] * len(args),
            [side, side],
            [],
            (info, *args),
        )

    old = rims((u0, ul, ur), False)
    late = rims((new,), True)

    strip = vm(5, 3, 4, 128)
    near = buf(5, 64, 128)
    s, flo, fhi = call(
        take_kernel, [SM, ANY], [vm(*FIELD), strip, strip], [near, dma((4,))], (info, came)
    )
    rx = rz = base = None
    for stage in range(4):
        theta = THETA[stage]
        rl, rh = swap(flo, fhi, "wide")
        gx = [old[0]] * (theta < 1.0) + [late[0]] * (theta > 0.0)
        gz = [old[1]] * (theta < 1.0) + [late[1]] * (theta > 0.0)
        args = [info, s] + gz + ([rz] if stage else [])
        pr, d, rz = call(
            lambda *refs, stage=stage: yz_kernel(*refs, stage=stage),
            [SM] + [VM] * (len(args) - 1),
            [vm(*FIELD), vm(*FIELD), vm(5, 8, 128)],
            PASS,
            args,
        )
        args = [info, s, rl, rh, pr, d] + gx
        args += ([base] if stage % 2 else []) + ([rx] if stage else [])
        if stage % 2 == 0:
            base = s
        got = call(
            lambda *refs, stage=stage: x_kernel(*refs, stage=stage),
            [SM] + [VM] * (len(args) - 1),
            [vm(*FIELD), vm(5, 8, 128)] + ([strip, strip] if stage < 3 else []),
            PASS + [buf(5, 3, 8, 128)],
            args,
        )
        s, rx = got[:2]
        if stage < 3:
            flo, fhi = got[2:]
    regs = (rx, rz)
    (gone,) = call(give_kernel, [SM, VM], [(moved, f32, ANY)], [near, dma((4,))], (info, s))
    home = lax.all_to_all(gone, "wide", split_axis=0, concat_axis=0, tiled=True)
    plane = vm(5, 8, 128)
    w, low, high = call(
        sync_kernel,
        [SM] + [VM] * 6,
        [vm(*FIELD), plane, plane],
        [],
        (info, s, regs[0], regs[1], new, mx, mz),
    )
    from_left, from_right = swap(low, high, "wide")
    (coarse_out,) = call(
        last_kernel, [SM] + [VM] * 3, [vm(5, 8, 8, LIVE_Z)], [], (info, w, from_left, from_right)
    )
    initial = jnp.stack(
        cons_of([fdens, fvel[:, :, 0], fvel[:, :, 1], fvel[:, :, 2], fpres]), axis=2
    )
    (fine_out,) = call(
        home_kernel,
        [SM, ANY, ANY],
        [(initial.shape, f32, ANY)],
        [dma((4, 4))],
        (info, home, initial),
        alias={2: 0},
    )
    return coarse_out, fine_out


def solution(mesh):
    return jax.shard_map(
        local,
        mesh=mesh,
        in_specs=(
            P("wide", None, "deep"),
            P(None, "wide", None, "deep"),
            P("wide", None, "deep"),
            P("deep", "wide", None, None),
            P("deep", "wide", None, None, None),
            P("deep", "wide", None, None),
            P("deep", None),
            P("deep"),
        ),
        out_specs=(P(None, "wide", None, "deep"), P("deep", "wide", None, None, None)),
        check_vma=False,
    )
```

profile of v0, /device:TPU:0, one launch (start us, length us, event | category | flops | bytes accessed | tf_op | source)
XLA Modules:
  0.0 120.5 jit_solution(9414482112182565649)
XLA Ops:
  1.3 0.6 copy-done.6
  1.9 1.3 %shard_map.95.info.refs_0_ = s32[16]{0:T(128)S(1)} custom-call(s32[1,16]{1,0:T(1,128)S(1)} %copy-done.6, s32[1]{0:T(128)S(6)} %copy.25.start, s32[1]{0:T(128)} %bitcast.here), custom_call_target="tpu_custom_call" | custom-call | tf_op jit(solution)/shard_map/pallas_call | solution.py:689
  3.2 0.8 copy-done
  4.0 0.9 copy-done.2
  5.0 0.8 copy-done.4
  5.8 1.6 %shard_map.96 = f32[16,5,32,128]{3,2,1,0:T(8,128)} custom-call(s32[16]{0:T(128)S(1)} %shard_map.95.info.refs_0_, f32[1,4,16,256]{3,2,1,0:T(8,128)S(1)} %copy-done, f32[1,4,3,16,256]{4,3,2,1,0:T(8,128)S(1)} %copy-done.2, f32[1,4,16,256]{3,2,1,0:T(8,128)S(1)} %copy-done.4), custom_call_target="tpu_custom_call" | custom-call | tf_op jit(solution)/shard_map/pallas_call | solution.py:689
  7.5 8.2 %all-to-all-start = ((f32[16,5,32,128]{3,2,1,0:T(8,128)}), f32[16,5,32,128]{3,2,1,0:T(8,128)S(1)}, u32[]{:S(2)}, u32[]{:S(2)}) async-start(f32[16,5,32,128]{3,2,1,0:T(8,128)} %shard_map.96), calls=%async_computation | async-start | bytes 2621440 | tf_op jit(solution)/shard_map/all_to_all | solution.py:736
  15.7 1.1 shard_map.98
  16.8 2.9 %collective-permute-start.3 = (f32[8,128]{1,0:T(8,128)S(1)}, f32[8,128]{1,0:T(8,128)S(1)}, u32[]{:S(2)}, u32[]{:S(2)}) collective-permute-start(f32[8,128]{1,0:T(8,128)S(1)} %get-tuple-element.54), channel_id=1, source_target_pairs={{1,0},{2,1},{3,2},{4,3},{5,4},{6,5},{7,6},{0,7},{9,8},{10,9},{11,1... | collective-permute-start | bytes 12296 | tf_op jit(solution)/shard_map/ppermute | solution.py:721
  19.8 1.3 %collective-permute-done.2.zl = f32[8,128]{1,0:T(8,128)S(1)} collective-permute-done((f32[8,128]{1,0:T(8,128)S(1)}, f32[8,128]{1,0:T(8,128)S(1)}, u32[]{:S(2)}, u32[]{:S(2)}) %collective-permute-start.2) | collective-permute-done | bytes 4128 | tf_op jit(solution)/shard_map/ppermute | solution.py:720
  21.0 0.0 collective-permute-done.3.zh
  21.1 0.1 shard_map.99.refs_1_.u.u0
  21.2 2.0 %collective-permute-start.4 = (f32[5,8,8,128]{3,2,1,0:T(8,128)S(1)}, f32[5,8,8,128]{3,2,1,0:T(8,128)S(1)}, u32[]{:S(2)}, u32[]{:S(2)}) collective-permute-start(f32[5,8,8,128]{3,2,1,0:T(8,128)S(1)} %shard_map.99.refs_1_.u.u0), channel_id=1, source_target_pairs={{0,8},{8,16},{16,24},{24,32},{32,40},{40,48},{48,56},{56,64},{64,7... | collective-permute-start | bytes 491528 | tf_op jit(solution)/shard_map/ppermute | solution.py:720
  23.2 3.4 %collective-permute-start.5 = (f32[5,8,8,128]{3,2,1,0:T(8,128)S(1)}, f32[5,8,8,128]{3,2,1,0:T(8,128)S(1)}, u32[]{:S(2)}, u32[]{:S(2)}) collective-permute-start(f32[5,8,8,128]{3,2,1,0:T(8,128)S(1)} %shard_map.99.refs_1_.u.u0), channel_id=1, source_target_pairs={{8,0},{16,8},{24,16},{32,24},{40,32},{48,40},{56,48},{64,56},{72,6... | collective-permute-start | bytes 491528 | tf_op jit(solution)/shard_map/ppermute | solution.py:721
  26.7 10.8 %all-to-all-done.far = f32[16,5,32,128]{3,2,1,0:T(8,128)S(1)} async-done(((f32[16,5,32,128]{3,2,1,0:T(8,128)}), f32[16,5,32,128]{3,2,1,0:T(8,128)S(1)}, u32[]{:S(2)}, u32[]{:S(2)}) %all-to-all-start) | async-done | bytes 1310752 | tf_op jit(solution)/shard_map/all_to_all | solution.py:736
  37.5 0.7 shard_map.97
  38.1 0.2 collective-permute-start
  38.3 5.2 %collective-permute-start.1 = (f32[5,3,4,128]{3,2,1,0:T(4,128)S(1)}, f32[5,3,4,128]{3,2,1,0:T(4,128)S(1)}, u32[]{:S(2)}, u32[]{:S(2)}) collective-permute-start(f32[5,3,4,128]{3,2,1,0:T(4,128)S(1)} %get-tuple-element.51), channel_id=1, source_target_pairs={{8,0},{16,8},{24,16},{32,24},{40,32},{48,40},{56,48},{64,56},{72,6... | collective-permute-start | bytes 92168 | tf_op jit(solution)/shard_map/ppermute | solution.py:721
  43.6 2.4 %shard_map.100 = (f32[5,3,8,128]{3,2,1,0:T(8,128)S(1)}, f32[5,3,8,128]{3,2,1,0:T(8,128)S(1)}) custom-call(s32[16]{0:T(128)S(1)} %shard_map.95.info.refs_0_, f32[5,8,8,128]{3,2,1,0:T(8,128)S(1)} %shard_map.99.refs_1_.u.u0, f32[5,8,8,128]{3,2,1,0:T(8,128)S(1)} %collective-permute-done.4.refs_2_.ul, f32[5,8,8,128]{3,2,1,0:T(8,128)S(1)} %collective-permute-done.5.refs_3_.ur), custom_call_target="tpu_custom_call" | custom-call | tf_op jit(solution)/shard_map/pallas_call | solution.py:689
  46.0 2.7 %shard_map.101 = (f32[5,8,8,128]{3,2,1,0:T(8,128)S(1)}, f32[5,8,8,128]{3,2,1,0:T(8,128)S(1)}, f32[5,8,128]{2,1,0:T(8,128)S(1)}) custom-call(s32[16]{0:T(128)S(1)} %shard_map.95.info.refs_0_, f32[5,8,8,128]{3,2,1,0:T(8,128)S(1)} %get-tuple-element.49.refs_1_.refs_8_, f32[5,3,8,128]{3,2,1,0:T(8,128)S(1)} %get-tuple-element.55.refs_2_), custom_call_target="tpu_custom_call" | custom-call | tf_op jit(solution)/shard_map/pallas_call | solution.py:689
  48.7 1.2 %shard_map.102 = (f32[5,8,8,128]{3,2,1,0:T(8,128)S(1)}, f32[5,8,128]{2,1,0:T(8,128)S(1)}, f32[5,3,4,128]{3,2,1,0:T(4,128)S(1)}, f32[5,3,4,128]{3,2,1,0:T(4,128)S(1)}) custom-call(s32[16]{0:T(128)S(1)} %shard_map.95.info.refs_0_, f32[5,8,8,128]{3,2,1,0:T(8,128)S(1)} %get-tuple-element.49.refs_1_.refs_8_, f32[5,3,4,128]{3,2,1,0:T(4,128)S(1)} %collective-permute-done.refs_2_, ...), custom_call_target="tpu_custom_call" | custom-call | tf_op jit(solution)/shard_map/pallas_call | solution.py:689
  49.9 0.1 collective-permute-start.6
  50.0 5.3 %collective-permute-start.7 = (f32[5,3,4,128]{3,2,1,0:T(4,128)S(1)}, f32[5,3,4,128]{3,2,1,0:T(4,128)S(1)}, u32[]{:S(2)}, u32[]{:S(2)}) collective-permute-start(f32[5,3,4,128]{3,2,1,0:T(4,128)S(1)} %get-tuple-element.61), channel_id=1, source_target_pairs={{8,0},{16,8},{24,16},{32,24},{40,32},{48,40},{56,48},{64,56},{72,6... | collective-permute-start | bytes 92168 | tf_op jit(solution)/shard_map/ppermute | solution.py:721
  55.3 4.5 %shard_map.103 = (f32[5,18,8,128]{3,2,1,0:T(8,128)S(1)}, f32[8,128]{1,0:T(8,128)S(1)}, f32[8,128]{1,0:T(8,128)S(1)}, f32[5,2,8,128]{3,2,1,0:T(8,128)S(1)}, f32[5,8,8,128]{3,2,1,0:T(8,128)S(1)}) custom-call(f32[5,8,8,128]{3,2,1,0:T(8,128)S(1)} %shard_map.99.refs_1_.u.u0, f32[5,8,8,128]{3,2,1,0:T(8,128)S(1)} %collective-permute-done.4.refs_2_.ul, ...), custom_call_target="tpu_custom_call" | custom-call | tf_op jit(solution)/shard_map/pallas_call | solution.py:689
  59.9 2.9 %collective-permute-start.9 = (f32[8,128]{1,0:T(8,128)S(1)}, f32[8,128]{1,0:T(8,128)S(1)}, u32[]{:S(2)}, u32[]{:S(2)}) collective-permute-start(f32[8,128]{1,0:T(8,128)S(1)} %get-tuple-element.66), channel_id=1, source_target_pairs={{1,0},{2,1},{3,2},{4,3},{5,4},{6,5},{7,6},{0,7},{9,8},{10,9},{11,1... | collective-permute-start | bytes 12296 | tf_op jit(solution)/shard_map/ppermute | solution.py:721
  62.8 1.3 %collective-permute-done.8.zl = f32[8,128]{1,0:T(8,128)S(1)} collective-permute-done((f32[8,128]{1,0:T(8,128)S(1)}, f32[8,128]{1,0:T(8,128)S(1)}, u32[]{:S(2)}, u32[]{:S(2)}) %collective-permute-start.8) | collective-permute-done | bytes 4128 | tf_op jit(solution)/shard_map/ppermute | solution.py:720
  64.1 0.0 collective-permute-done.9.zh
  64.1 3.1 %shard_map.104 = (f32[5,12,8,128]{3,2,1,0:T(8,128)S(1)}, f32[5,2,8,128]{3,2,1,0:T(8,128)S(1)}, f32[5,8,8,128]{3,2,1,0:T(8,128)S(1)}) custom-call(f32[5,8,8,128]{3,2,1,0:T(8,128)S(1)} %shard_map.99.refs_1_.u.u0, f32[5,8,8,128]{3,2,1,0:T(8,128)S(1)} %collective-permute-done.4.refs_2_.ul, f32[5,8,8,128]{3,2,1,0:T(8,128)S(1)} %collective-permute-done.5.refs_3_.ur, ...), custom_call_target="tpu_custom_call" | custom-call | tf_op jit(solution)/shard_map/pallas_call | solution.py:689
  67.2 2.4 %shard_map.105 = (f32[5,3,8,128]{3,2,1,0:T(8,128)S(1)}, f32[5,3,8,128]{3,2,1,0:T(8,128)S(1)}) custom-call(s32[16]{0:T(128)S(1)} %shard_map.95.info.refs_0_, f32[5,12,8,128]{3,2,1,0:T(8,128)S(1)} %get-tuple-element.67.refs_1_.new), custom_call_target="tpu_custom_call" | custom-call | tf_op jit(solution)/shard_map/pallas_call | solution.py:689
  69.7 2.6 %shard_map.106 = (f32[5,8,8,128]{3,2,1,0:T(8,128)S(1)}, f32[5,8,8,128]{3,2,1,0:T(8,128)S(1)}, f32[5,8,128]{2,1,0:T(8,128)S(1)}) custom-call(s32[16]{0:T(128)S(1)} %shard_map.95.info.refs_0_, f32[5,8,8,128]{3,2,1,0:T(8,128)S(1)} %get-tuple-element.59.refs_1_, f32[5,3,8,128]{3,2,1,0:T(8,128)S(1)} %get-tuple-element.55.refs_2_, ...), custom_call_target="tpu_custom_call" | custom-call | tf_op jit(solution)/shard_map/pallas_call | solution.py:689
  72.3 1.3 %shard_map.107 = (f32[5,8,8,128]{3,2,1,0:T(8,128)S(1)}, f32[5,8,128]{2,1,0:T(8,128)S(1)}, f32[5,3,4,128]{3,2,1,0:T(4,128)S(1)}, f32[5,3,4,128]{3,2,1,0:T(4,128)S(1)}) custom-call(s32[16]{0:T(128)S(1)} %shard_map.95.info.refs_0_, f32[5,8,8,128]{3,2,1,0:T(8,128)S(1)} %get-tuple-element.59.refs_1_, f32[5,3,4,128]{3,2,1,0:T(4,128)S(1)} %collective-permute-done.6.refs_2_, ...), custom_call_target="tpu_custom_call" | custom-call | tf_op jit(solution)/shard_map/pallas_call | solution.py:689
  73.6 0.1 collective-permute-start.10
  73.7 5.3 %collective-permute-start.11 = (f32[5,3,4,128]{3,2,1,0:T(4,128)S(1)}, f32[5,3,4,128]{3,2,1,0:T(4,128)S(1)}, u32[]{:S(2)}, u32[]{:S(2)}) collective-permute-start(f32[5,3,4,128]{3,2,1,0:T(4,128)S(1)} %get-tuple-element.76), channel_id=1, source_target_pairs={{8,0},{16,8},{24,16},{32,24},{40,32},{48,40},{56,48},{64,56},{72,6... | collective-permute-start | bytes 92168 | tf_op jit(solution)/shard_map/ppermute | solution.py:721
  79.0 2.6 %shard_map.108 = (f32[5,8,8,128]{3,2,1,0:T(8,128)S(1)}, f32[5,8,8,128]{3,2,1,0:T(8,128)S(1)}, f32[5,8,128]{2,1,0:T(8,128)S(1)}) custom-call(s32[16]{0:T(128)S(1)} %shard_map.95.info.refs_0_, f32[5,8,8,128]{3,2,1,0:T(8,128)S(1)} %get-tuple-element.74.refs_1_.refs_7_, f32[5,3,8,128]{3,2,1,0:T(8,128)S(1)} %get-tuple-element.55.refs_2_, ...), custom_call_target="tpu_custom_call" | custom-call | tf_op jit(solution)/shard_map/pallas_call | solution.py:689
  81.7 1.2 %shard_map.109 = (f32[5,8,8,128]{3,2,1,0:T(8,128)S(1)}, f32[5,8,128]{2,1,0:T(8,128)S(1)}, f32[5,3,4,128]{3,2,1,0:T(4,128)S(1)}, f32[5,3,4,128]{3,2,1,0:T(4,128)S(1)}) custom-call(s32[16]{0:T(128)S(1)} %shard_map.95.info.refs_0_, f32[5,8,8,128]{3,2,1,0:T(8,128)S(1)} %get-tuple-element.74.refs_1_.refs_7_, ...), custom_call_target="tpu_custom_call" | custom-call | tf_op jit(solution)/shard_map/pallas_call | solution.py:689
  83.0 0.1 collective-permute-start.12
  83.0 5.3 %collective-permute-start.13 = (f32[5,3,4,128]{3,2,1,0:T(4,128)S(1)}, f32[5,3,4,128]{3,2,1,0:T(4,128)S(1)}, u32[]{:S(2)}, u32[]{:S(2)}) collective-permute-start(f32[5,3,4,128]{3,2,1,0:T(4,128)S(1)} %get-tuple-element.83), channel_id=1, source_target_pairs={{8,0},{16,8},{24,16},{32,24},{40,32},{48,40},{56,48},{64,56},{72,6... | collective-permute-start | bytes 92168 | tf_op jit(solution)/shard_map/ppermute | solution.py:721
  88.4 2.6 %shard_map.110 = (f32[5,8,8,128]{3,2,1,0:T(8,128)S(1)}, f32[5,8,8,128]{3,2,1,0:T(8,128)S(1)}, f32[5,8,128]{2,1,0:T(8,128)S(1)}) custom-call(s32[16]{0:T(128)S(1)} %shard_map.95.info.refs_0_, f32[5,8,8,128]{3,2,1,0:T(8,128)S(1)} %get-tuple-element.81.refs_1_, f32[5,3,8,128]{3,2,1,0:T(8,128)S(1)} %get-tuple-element.68.refs_3_.refs_2_, ...), custom_call_target="tpu_custom_call" | custom-call | tf_op jit(solution)/shard_map/pallas_call | solution.py:689
  91.0 1.3 %shard_map.111 = (f32[5,8,8,128]{3,2,1,0:T(8,128)S(1)}, f32[5,8,128]{2,1,0:T(8,128)S(1)}) custom-call(s32[16]{0:T(128)S(1)} %shard_map.95.info.refs_0_, f32[5,8,8,128]{3,2,1,0:T(8,128)S(1)} %get-tuple-element.81.refs_1_, f32[5,3,4,128]{3,2,1,0:T(4,128)S(1)} %collective-permute-done.12.refs_2_, f32[5,3,4,128]{3,2,1,0:T(4,128)S(1)} %collective-permute-done.13.refs_3_, ...), custom_call_target="tpu_custom_call" | custom-call | tf_op jit(solution)/shard_map/pallas_call | solution.py:689
  92.3 1.3 %shard_map.114 = f32[16,5,32,128]{3,2,1,0:T(8,128)} custom-call(s32[16]{0:T(128)S(1)} %shard_map.95.info.refs_0_, f32[5,8,8,128]{3,2,1,0:T(8,128)S(1)} %get-tuple-element.88.s), custom_call_target="tpu_custom_call" | custom-call | tf_op jit(solution)/shard_map/pallas_call | solution.py:689
  93.6 6.1 %all-to-all-start.1 = ((f32[16,5,32,128]{3,2,1,0:T(8,128)}), f32[16,5,32,128]{3,2,1,0:T(8,128)S(1)}, u32[]{:S(2)}, u32[]{:S(2)}) async-start(f32[16,5,32,128]{3,2,1,0:T(8,128)} %shard_map.114), calls=%async_computation.1 | async-start | bytes 2621440 | tf_op jit(solution)/shard_map/all_to_all | solution.py:813
  99.8 2.9 %shard_map.112 = (f32[5,8,8,128]{3,2,1,0:T(8,128)S(1)}, f32[5,8,128]{2,1,0:T(8,128)S(1)}, f32[5,8,128]{2,1,0:T(8,128)S(1)}) custom-call(s32[16]{0:T(128)S(1)} %shard_map.95.info.refs_0_, f32[5,8,8,128]{3,2,1,0:T(8,128)S(1)} %get-tuple-element.88.s, f32[5,8,128]{2,1,0:T(8,128)S(1)} %get-tuple-element.89.rx, f32[5,8,128]{2,1,0:T(8,128)S(1)} %get-tuple-element.90.rz, ...), custom_call_target="tpu_custom_call" | custom-call | tf_op jit(solution)/shard_map/pallas_call | solution.py:689
  102.7 2.0 %collective-permute-start.14 = (f32[5,8,128]{2,1,0:T(8,128)S(1)}, f32[5,8,128]{2,1,0:T(8,128)S(1)}, u32[]{:S(2)}, u32[]{:S(2)}) collective-permute-start(f32[5,8,128]{2,1,0:T(8,128)S(1)} %get-tuple-element.94), channel_id=1, source_target_pairs={{0,8},{8,16},{16,24},{24,32},{32,40},{40,48},{48,56},{56,64},{64,7... | collective-permute-start | bytes 61448 | tf_op jit(solution)/shard_map/ppermute | solution.py:720
  104.7 3.4 %collective-permute-start.15 = (f32[5,8,128]{2,1,0:T(8,128)S(1)}, f32[5,8,128]{2,1,0:T(8,128)S(1)}, u32[]{:S(2)}, u32[]{:S(2)}) collective-permute-start(f32[5,8,128]{2,1,0:T(8,128)S(1)} %get-tuple-element.95), channel_id=1, source_target_pairs={{8,0},{16,8},{24,16},{32,24},{40,32},{48,40},{56,48},{64,56},{72,6... | collective-permute-start | bytes 61448 | tf_op jit(solution)/shard_map/ppermute | solution.py:721
  108.2 9.2 %collective-permute-done.14.left = f32[5,8,128]{2,1,0:T(8,128)S(1)} collective-permute-done((f32[5,8,128]{2,1,0:T(8,128)S(1)}, f32[5,8,128]{2,1,0:T(8,128)S(1)}, u32[]{:S(2)}, u32[]{:S(2)}) %collective-permute-start.14) | collective-permute-done | bytes 20512 | tf_op jit(solution)/shard_map/ppermute | solution.py:720
  117.4 1.2 %shard_map.113 = f32[5,8,8,120]{3,2,1,0:T(8,128)} custom-call(s32[16]{0:T(128)S(1)} %shard_map.95.info.refs_0_, f32[5,8,8,128]{3,2,1,0:T(8,128)S(1)} %get-tuple-element.93.w, f32[5,8,128]{2,1,0:T(8,128)S(1)} %collective-permute-done.14.left, f32[5,8,128]{2,1,0:T(8,128)S(1)} %collective-permute-done.15.right), custom_call_target="tpu_custom_call" | custom-call | tf_op jit(solution)/shard_map/pallas_call | solution.py:689
  118.6 0.4 all-to-all-done.1.far
  119.0 1.3 %shard_map.115 = f32[1,4,5,16,256]{4,3,2,1,0:T(8,128)} custom-call(s32[16]{0:T(128)S(1)} %shard_map.95.info.refs_0_, f32[16,5,32,128]{3,2,1,0:T(8,128)S(1)} %all-to-all-done.1.far, f32[1,4,5,16,256]{4,3,2,1,0:T(8,128)} %copy-done.7), custom_call_target="tpu_custom_call", output_to_operand_aliasing={{}: (2, {})} | custom-call | tf_op jit(solution)/shard_map/pallas_call | solution.py:689
  (30 shorter events, 0.2 us)
Async XLA Ops:
  1.3 0.7 copy-start.6
  3.2 0.8 copy-start
  4.0 0.9 copy-start.2
  5.0 0.8 copy-start.4
  7.5 30.0 %all-to-all-start = ((f32[16,5,32,128]{3,2,1,0:T(8,128)}), f32[16,5,32,128]{3,2,1,0:T(8,128)S(1)}, u32[]{:S(2)}, u32[]{:S(2)}) async-start(f32[16,5,32,128]{3,2,1,0:T(8,128)} %shard_map.96), calls=%async_computation | async-start | bytes 2621440 | tf_op jit(solution)/shard_map/all_to_all | solution.py:736
  16.8 4.3 %collective-permute-start.2 = (f32[8,128]{1,0:T(8,128)S(1)}, f32[8,128]{1,0:T(8,128)S(1)}, u32[]{:S(2)}, u32[]{:S(2)}) collective-permute-start(f32[8,128]{1,0:T(8,128)S(1)} %get-tuple-element.53), channel_id=1, source_target_pairs={{0,1},{1,2},{2,3},{3,4},{4,5},{5,6},{6,7},{7,0},{8,9},{9,10},{10,1... | collective-permute-start | bytes 12296 | tf_op jit(solution)/shard_map/ppermute | solution.py:720
  16.8 4.3 %collective-permute-start.3 = (f32[8,128]{1,0:T(8,128)S(1)}, f32[8,128]{1,0:T(8,128)S(1)}, u32[]{:S(2)}, u32[]{:S(2)}) collective-permute-start(f32[8,128]{1,0:T(8,128)S(1)} %get-tuple-element.54), channel_id=1, source_target_pairs={{1,0},{2,1},{3,2},{4,3},{5,4},{6,5},{7,6},{0,7},{9,8},{10,9},{11,1... | collective-permute-start | bytes 12296 | tf_op jit(solution)/shard_map/ppermute | solution.py:721
  21.2 22.3 %collective-permute-start.4 = (f32[5,8,8,128]{3,2,1,0:T(8,128)S(1)}, f32[5,8,8,128]{3,2,1,0:T(8,128)S(1)}, u32[]{:S(2)}, u32[]{:S(2)}) collective-permute-start(f32[5,8,8,128]{3,2,1,0:T(8,128)S(1)} %shard_map.99.refs_1_.u.u0), channel_id=1, source_target_pairs={{0,8},{8,16},{16,24},{24,32},{32,40},{40,48},{48,56},{56,64},{64,7... | collective-permute-start | bytes 491528 | tf_op jit(solution)/shard_map/ppermute | solution.py:720
  23.2 20.3 %collective-permute-start.5 = (f32[5,8,8,128]{3,2,1,0:T(8,128)S(1)}, f32[5,8,8,128]{3,2,1,0:T(8,128)S(1)}, u32[]{:S(2)}, u32[]{:S(2)}) collective-permute-start(f32[5,8,8,128]{3,2,1,0:T(8,128)S(1)} %shard_map.99.refs_1_.u.u0), channel_id=1, source_target_pairs={{8,0},{16,8},{24,16},{32,24},{40,32},{48,40},{56,48},{64,56},{72,6... | collective-permute-start | bytes 491528 | tf_op jit(solution)/shard_map/ppermute | solution.py:721
  38.1 10.5 %collective-permute-start = (f32[5,3,4,128]{3,2,1,0:T(4,128)S(1)}, f32[5,3,4,128]{3,2,1,0:T(4,128)S(1)}, u32[]{:S(2)}, u32[]{:S(2)}) collective-permute-start(f32[5,3,4,128]{3,2,1,0:T(4,128)S(1)} %get-tuple-element.50), channel_id=1, source_target_pairs={{0,8},{8,16},{16,24},{24,32},{32,40},{40,48},{48,56},{56,64},{64,7... | collective-permute-start | bytes 92168 | tf_op jit(solution)/shard_map/ppermute | solution.py:720
  38.3 10.3 %collective-permute-start.1 = (f32[5,3,4,128]{3,2,1,0:T(4,128)S(1)}, f32[5,3,4,128]{3,2,1,0:T(4,128)S(1)}, u32[]{:S(2)}, u32[]{:S(2)}) collective-permute-start(f32[5,3,4,128]{3,2,1,0:T(4,128)S(1)} %get-tuple-element.51), channel_id=1, source_target_pairs={{8,0},{16,8},{24,16},{32,24},{40,32},{48,40},{56,48},{64,56},{72,6... | collective-permute-start | bytes 92168 | tf_op jit(solution)/shard_map/ppermute | solution.py:721
  49.9 22.4 %collective-permute-start.6 = (f32[5,3,4,128]{3,2,1,0:T(4,128)S(1)}, f32[5,3,4,128]{3,2,1,0:T(4,128)S(1)}, u32[]{:S(2)}, u32[]{:S(2)}) collective-permute-start(f32[5,3,4,128]{3,2,1,0:T(4,128)S(1)} %get-tuple-element.60), channel_id=1, source_target_pairs={{0,8},{8,16},{16,24},{24,32},{32,40},{40,48},{48,56},{56,64},{64,7... | collective-permute-start | bytes 92168 | tf_op jit(solution)/shard_map/ppermute | solution.py:720
  50.0 22.3 %collective-permute-start.7 = (f32[5,3,4,128]{3,2,1,0:T(4,128)S(1)}, f32[5,3,4,128]{3,2,1,0:T(4,128)S(1)}, u32[]{:S(2)}, u32[]{:S(2)}) collective-permute-start(f32[5,3,4,128]{3,2,1,0:T(4,128)S(1)} %get-tuple-element.61), channel_id=1, source_target_pairs={{8,0},{16,8},{24,16},{32,24},{40,32},{48,40},{56,48},{64,56},{72,6... | collective-permute-start | bytes 92168 | tf_op jit(solution)/shard_map/ppermute | solution.py:721
  59.8 4.3 %collective-permute-start.8 = (f32[8,128]{1,0:T(8,128)S(1)}, f32[8,128]{1,0:T(8,128)S(1)}, u32[]{:S(2)}, u32[]{:S(2)}) collective-permute-start(f32[8,128]{1,0:T(8,128)S(1)} %get-tuple-element.65), channel_id=1, source_target_pairs={{0,1},{1,2},{2,3},{3,4},{4,5},{5,6},{6,7},{7,0},{8,9},{9,10},{10,1... | collective-permute-start | bytes 12296 | tf_op jit(solution)/shard_map/ppermute | solution.py:720
  59.9 4.3 %collective-permute-start.9 = (f32[8,128]{1,0:T(8,128)S(1)}, f32[8,128]{1,0:T(8,128)S(1)}, u32[]{:S(2)}, u32[]{:S(2)}) collective-permute-start(f32[8,128]{1,0:T(8,128)S(1)} %get-tuple-element.66), channel_id=1, source_target_pairs={{1,0},{2,1},{3,2},{4,3},{5,4},{6,5},{7,6},{0,7},{9,8},{10,9},{11,1... | collective-permute-start | bytes 12296 | tf_op jit(solution)/shard_map/ppermute | solution.py:721
  73.6 8.1 %collective-permute-start.10 = (f32[5,3,4,128]{3,2,1,0:T(4,128)S(1)}, f32[5,3,4,128]{3,2,1,0:T(4,128)S(1)}, u32[]{:S(2)}, u32[]{:S(2)}) collective-permute-start(f32[5,3,4,128]{3,2,1,0:T(4,128)S(1)} %get-tuple-element.75), channel_id=1, source_target_pairs={{0,8},{8,16},{16,24},{24,32},{32,40},{40,48},{48,56},{56,64},{64,7... | collective-permute-start | bytes 92168 | tf_op jit(solution)/shard_map/ppermute | solution.py:720
  73.7 8.0 %collective-permute-start.11 = (f32[5,3,4,128]{3,2,1,0:T(4,128)S(1)}, f32[5,3,4,128]{3,2,1,0:T(4,128)S(1)}, u32[]{:S(2)}, u32[]{:S(2)}) collective-permute-start(f32[5,3,4,128]{3,2,1,0:T(4,128)S(1)} %get-tuple-element.76), channel_id=1, source_target_pairs={{8,0},{16,8},{24,16},{32,24},{40,32},{48,40},{56,48},{64,56},{72,6... | collective-permute-start | bytes 92168 | tf_op jit(solution)/shard_map/ppermute | solution.py:721
  83.0 8.1 %collective-permute-start.12 = (f32[5,3,4,128]{3,2,1,0:T(4,128)S(1)}, f32[5,3,4,128]{3,2,1,0:T(4,128)S(1)}, u32[]{:S(2)}, u32[]{:S(2)}) collective-permute-start(f32[5,3,4,128]{3,2,1,0:T(4,128)S(1)} %get-tuple-element.82), channel_id=1, source_target_pairs={{0,8},{8,16},{16,24},{24,32},{32,40},{40,48},{48,56},{56,64},{64,7... | collective-permute-start | bytes 92168 | tf_op jit(solution)/shard_map/ppermute | solution.py:720
  83.0 8.0 %collective-permute-start.13 = (f32[5,3,4,128]{3,2,1,0:T(4,128)S(1)}, f32[5,3,4,128]{3,2,1,0:T(4,128)S(1)}, u32[]{:S(2)}, u32[]{:S(2)}) collective-permute-start(f32[5,3,4,128]{3,2,1,0:T(4,128)S(1)} %get-tuple-element.83), channel_id=1, source_target_pairs={{8,0},{16,8},{24,16},{32,24},{40,32},{48,40},{56,48},{64,56},{72,6... | collective-permute-start | bytes 92168 | tf_op jit(solution)/shard_map/ppermute | solution.py:721
  93.6 6.1 %copy-start.1 = (f32[1,4,16,256]{3,2,1,0:T(8,128)S(1)}, f32[1,4,16,256]{3,2,1,0:T(8,128)}, u32[]{:S(2)}) copy-start(f32[1,4,16,256]{3,2,1,0:T(8,128)} %dens.1) | copy-start | bytes 196612
  93.6 6.1 %copy-start.3 = (f32[1,4,3,16,256]{4,3,2,1,0:T(8,128)S(1)}, f32[1,4,3,16,256]{4,3,2,1,0:T(8,128)}, u32[]{:S(2)}) copy-start(f32[1,4,3,16,256]{4,3,2,1,0:T(8,128)} %vel.1) | copy-start | bytes 589828
  93.6 25.4 %all-to-all-start.1 = ((f32[16,5,32,128]{3,2,1,0:T(8,128)}), f32[16,5,32,128]{3,2,1,0:T(8,128)S(1)}, u32[]{:S(2)}, u32[]{:S(2)}) async-start(f32[16,5,32,128]{3,2,1,0:T(8,128)} %shard_map.114), calls=%async_computation.1 | async-start | bytes 2621440 | tf_op jit(solution)/shard_map/all_to_all | solution.py:813
  99.7 8.5 %copy-start.5 = (f32[1,4,16,256]{3,2,1,0:T(8,128)S(1)}, f32[1,4,16,256]{3,2,1,0:T(8,128)}, u32[]{:S(2)}) copy-start(f32[1,4,16,256]{3,2,1,0:T(8,128)} %pres.1) | copy-start | bytes 196612
  102.7 14.7 %collective-permute-start.14 = (f32[5,8,128]{2,1,0:T(8,128)S(1)}, f32[5,8,128]{2,1,0:T(8,128)S(1)}, u32[]{:S(2)}, u32[]{:S(2)}) collective-permute-start(f32[5,8,128]{2,1,0:T(8,128)S(1)} %get-tuple-element.94), channel_id=1, source_target_pairs={{0,8},{8,16},{16,24},{24,32},{32,40},{40,48},{48,56},{56,64},{64,7... | collective-permute-start | bytes 61448 | tf_op jit(solution)/shard_map/ppermute | solution.py:720
  104.7 12.7 %collective-permute-start.15 = (f32[5,8,128]{2,1,0:T(8,128)S(1)}, f32[5,8,128]{2,1,0:T(8,128)S(1)}, u32[]{:S(2)}, u32[]{:S(2)}) collective-permute-start(f32[5,8,128]{2,1,0:T(8,128)S(1)} %get-tuple-element.95), channel_id=1, source_target_pairs={{8,0},{16,8},{24,16},{32,24},{40,32},{48,40},{56,48},{64,56},{72,6... | collective-permute-start | bytes 61448 | tf_op jit(solution)/shard_map/ppermute | solution.py:721
  108.2 10.9 %copy-start.7 = (f32[1,4,5,16,256]{4,3,2,1,0:T(8,128)}, f32[1,4,5,16,256]{4,3,2,1,0:T(8,128)S(1)}, u32[]{:S(2)}) copy-start(f32[1,4,5,16,256]{4,3,2,1,0:T(8,128)S(1)} %fusion.6.initial) | copy-start | bytes 983044
where the time goes:
time: 122 us; the launch traced here: 121 us
  starting transfers between devices  52.7 us (43%)
  Pallas kernels  39.6 us (32%)
  waiting for transfers between devices  23.1 us (19%)
  local copies, waits for them, and re-layouts  3.28 us (3%)
  between operations  1.79 us (1%)
    pallas_call x21, Pallas kernels, call(): pl.pallas_call(kernel, in_specs=ins, out_specs=[spec for _, _, spec in ou...  39.6 us
    ppermute x8, starting transfers between devices, swap(): return (below, lax.ppermute(lo, axis, ring(axis, False)))  34 us
    ppermute x8, waiting for transfers between devices, swap(): below = lax.ppermute(hi, axis, ring(axis, True))  11.8 us
    all_to_all x1, waiting for transfers between devices, local(): came = lax.all_to_all(sent, 'wide', split_axis=0, concat_axis=0, tiled=True)  10.8 us
    all_to_all x1, starting transfers between devices, local(): came = lax.all_to_all(sent, 'wide', split_axis=0, concat_axis=0, tiled=True)  8.21 us
    all_to_all x1, starting transfers between devices, local(): home = lax.all_to_all(gone, 'wide', split_axis=0, concat_axis=0, tiled=True)  6.07 us
    ppermute x8, starting transfers between devices, swap(): below = lax.ppermute(hi, axis, ring(axis, True))  4.41 us
    unnamed x17, local copies, waits for them, and re-layouts  3.28 us
  transfers between devices with their start and end apart: 18, of which 5 were waited for; matrix products, arithmetic and copies ran while one was open for 0% of the time, Pallas kernels for 24%

commit v1 on v0

--- a/solution.py
+++ b/solution.py
@@ -178,7 +178,12 @@
     return v
 
 
-Z0, OWNER, COL, COUNT, ADJ, MATCH = 0, 2, 4, 8, 9, 10
+Z0, OWNER, COL, COUNT, ADJ, MATCH, PARITY = 0, 2, 4, 8, 9, 10, 14
+
+
+def by_parity(info, first, second):
+    odd = info[PARITY] == 1
+    return jnp.where(odd, first, second), jnp.where(odd, second, first)
 
 
 def column_places(column, anchor):
@@ -229,17 +234,22 @@
         info[COL + s] = place & 15
     info[COUNT] = mine
     info[ADJ] = jnp.where(h[1] == h[0] + 1, 1, 0)
-    info[14] = 0
+    info[PARITY] = me & 1
     info[15] = 0
 
 
-def send_kernel(info, dens, vel, pres, out, sem):
+def send_kernel(info, dens_far, vel_far, pres_far, out, dens, vel, pres, sem, load):
+    pairs = ((dens_far, dens), (vel_far, vel), (pres_far, pres))
+    loads = [pltpu.make_async_copy(a, b, load.at[k]) for k, (a, b) in enumerate(pairs)]
+    for cp in loads:
+        cp.start()
+    for cp in loads:
+        cp.wait()
     for s in range(4):
 
         @pl.when(s < info[COUNT])
         def _():
-            copies = slot_copies(info, dens, vel, pres, out, sem, s)
-            for cp in copies:
+            for cp in slot_copies(info, dens, vel, pres, out, sem, s):
                 cp.start()
 
     for s in range(4):
@@ -289,7 +299,7 @@
     return copies
 
 
-def take_kernel(info, far, s, lo, hi, near, sem):
+def take_kernel(info, far, s, near_side, far_side, near, sem):
     copies = patch_copies(info, far, near, sem, False)
     for cp in copies:
         cp.start()
@@ -299,8 +309,13 @@
         u = cons_of([near[c, pl.ds(m, 8, stride=8), :] for c in range(5)])
         for c in range(5):
             s[c, m] = u[c]
-    lo[...] = s[:, 0:3, 0:4, :]
-    hi[...] = s[:, 5:8, 4:8, :]
+    sides(info, s, near_side, far_side)
+
+
+def sides(info, s, near_side, far_side):
+    for c in range(5):
+        for g in range(3):
+            near_side[c, g], far_side[c, g] = by_parity(info, s[c, g, 0:4, :], s[c, g + 5, 4:8, :])
 
 
 def give_kernel(info, s, far, near, sem):
@@ -328,22 +343,6 @@
     return copies
 
 
-def home_kernel(info, far, initial, out, sem):
-    for s in range(4):
-
-        @pl.when(s < info[COUNT])
-        def _():
-            for cp in home_copies(info, far, out, sem, s):
-                cp.start()
-
-    for s in range(4):
-
-        @pl.when(s < info[COUNT])
-        def _():
-            for cp in home_copies(info, far, out, sem, s):
-                cp.wait()
-
-
 def pack_edge(u, first):
     lane = lanes()
     out = jnp.zeros((8, 128), f32)
@@ -405,8 +404,16 @@
     return lambda c: ref[c, x]
 
 
-def coarse_one(u, ul, ur, mid, plo, phi, fa, fz, q, sl, sr, fx, d, keep):
-    refs = [take_layer(ref, x) for ref in (ul, u, ur) for x in range(8)]
+def side_layers(info, ra, rb, side):
+    def layer(x):
+        return lambda c: by_parity(info, ra[c, x], rb[c, x])[side]
+
+    return [layer(x) for x in range(8)]
+
+
+def coarse_one(info, u, ra, rb, mid, plo, phi, fa, fz, q, sl, sr, fx, d, keep):
+    refs = side_layers(info, ra, rb, 0) + [take_layer(u, x) for x in range(8)]
+    refs += side_layers(info, ra, rb, 1)
     coarse_rates(refs, None, None, None, q, sl, sr, fx, d, keep)
     live = lanes() < LIVE_Z
     for c in range(5):
@@ -420,8 +427,9 @@
     phi[...] = pack_edge([[mid[c, x + 5] for x in range(8)] for c in range(5)], LIVE_Z - 3)
 
 
-def coarse_two(u0, ul, ur, fa, fza, u, zl, zh, new, mx, mz, q, sl, sr, fx, d, keep):
-    refs = [take_layer(ref, x) for ref in (ul, u0, ur) for x in range(8)]
+def coarse_two(info, u0, ra, rb, fa, fza, u, zl, zh, new, mx, mz, q, sl, sr, fx, d, keep):
+    refs = side_layers(info, ra, rb, 0) + [take_layer(u0, x) for x in range(8)]
+    refs += side_layers(info, ra, rb, 1)
     coarse_rates([take_layer(u, m) for m in range(18)], 5, zl, zh, q, sl, sr, fx, d, keep)
     live = lanes() < LIVE_Z
     for c in range(5):
@@ -460,8 +468,8 @@
         low, high = [take_layer(new, 0), take_layer(new, 1)], [take_layer(new, 10), take_layer(new, 11)]
         own = lambda c: new[c, 2:10]
     else:
-        u, ul, ur = refs[:3]
-        low, high = [take_layer(ul, 6), take_layer(ul, 7)], [take_layer(ur, 0), take_layer(ur, 1)]
+        u, ra, rb = refs[:3]
+        low, high = side_layers(info, ra, rb, 0)[6:], side_layers(info, ra, rb, 1)[:2]
         own = lambda c: u[c]
     z = iota2((128, 128), 0)
     l = iota2((128, 128), 1)
@@ -551,14 +559,15 @@
 def x_kernel(*refs, stage):
     theta = THETA[stage]
     refs = list(refs)
-    info, s, rl, rh, pr, d, old, new, base, reg = split_refs(
+    info, s, ra, rb, pr, d, old, new, base, reg = split_refs(
         refs, (1,) * 6 + (theta < 1.0, theta > 0.0, stage % 2, stage)
     )
-    out, rx, lo, hi = split_refs(refs, (1, 1, stage < 3, stage < 3))
+    out, rx, near_side, far_side = split_refs(refs, (1, 1, stage < 3, stage < 3))
     q, sl, sr, fx, near = refs
     upper_x, second, _ = places_of_rows()
-    near[:, :, 0:4, :] = rl[...]
-    near[:, :, 4:8, :] = rh[...]
+    for c in range(5):
+        for g in range(3):
+            near[c, g, 0:4, :], near[c, g, 4:8, :] = by_parity(info, ra[c, g], rb[c, g])
     code = jnp.where(
         upper_x,
         jnp.where(second, info[MATCH + 3], info[MATCH + 2]),
@@ -592,11 +601,10 @@
             else:
                 out[c, m] = 0.5 * (base[c, m] + s[c, m]) - 0.1 * change
     if stage < 3:
-        lo[...] = out[:, 0:3, 0:4, :]
-        hi[...] = out[:, 5:8, 4:8, :]
-
-
-def sync_kernel(info, s, rx, rz, new, mx, mz, out, low, high):
+        sides(info, out, near_side, far_side)
+
+
+def sync_kernel(info, s, rx, rz, new, mx, mz, out, near_side, far_side):
     lane = lanes()
     y = pick(subs() == ((lane & 15) >> 1))
     z0 = [info[Z0], info[Z0 + 1]]
@@ -625,12 +633,15 @@
                 rows.append(jnp.broadcast_to(v[at : at + 1], (8, 128)) * y)
         term = dot(jnp.concatenate(rows, axis=0), spread[pz])
         placed = term if placed is None else placed + term
-    for side, goal in ((0, low), (1, high)):
+    planes = []
+    for side in range(2):
         keep = (inside[0] & edge[side][0]) | (inside[1] & edge[side][1])
         for c in range(5):
             at = 8 * (5 * side + c)
             delta = 0.2 * mx[c, side] - 0.0125 * placed[at : at + 8]
-            goal[c] = jnp.where(keep, delta if side == 0 else -delta, 0.0)
+            planes.append(jnp.where(keep, delta if side == 0 else -delta, 0.0))
+    for c in range(5):
+        near_side[c], far_side[c] = by_parity(info, planes[c], planes[5 + c])
     adjacent = info[ADJ] == 1
     apart = jnp.logical_not(adjacent)
     at_low = (lane == z0[0] - 1) | ((lane == z0[1] - 1) & apart)
@@ -663,18 +674,33 @@
             out[c, x] = jnp.where(covered, 0.125 * mean[at : at + 8], w)
 
 
-def last_kernel(info, w, left, right, out):
+def last_kernel(info, far, initial, w, ra, rb, coarse, fine, sem):
+    for s in range(4):
+
+        @pl.when(s < info[COUNT])
+        def _():
+            for cp in home_copies(info, far, fine, sem, s):
+                cp.start()
+
     lane = lanes()
     z0 = [info[Z0], info[Z0 + 1]]
     inside = [(lane >= z0[p]) & (lane < z0[p] + 8) for p in range(2)]
     covered = inside[0] | inside[1]
     for c in range(5):
-        first = w[c, 0] + jnp.where(covered, 0.0, left[c])
-        final = w[c, 7] + jnp.where(covered, 0.0, right[c])
-        out[c, 0] = first[:, :LIVE_Z]
-        out[c, 7] = final[:, :LIVE_Z]
+        left, right = by_parity(info, ra[c], rb[c])
+        first = w[c, 0] + jnp.where(covered, 0.0, left)
+        final = w[c, 7] + jnp.where(covered, 0.0, right)
+        coarse[c, 0] = first[:, :LIVE_Z]
+        coarse[c, 7] = final[:, :LIVE_Z]
         for x in range(1, 7):
-            out[c, x] = w[c, x, :, pl.ds(0, LIVE_Z)]
+            coarse[c, x] = w[c, x, :, pl.ds(0, LIVE_Z)]
+
+    for s in range(4):
+
+        @pl.when(s < info[COUNT])
+        def _():
+            for cp in home_copies(info, far, fine, sem, s):
+                cp.wait()
 
 
 VM = pl.BlockSpec(memory_space=pltpu.VMEM)
@@ -721,6 +747,15 @@
     return below, lax.ppermute(lo, axis, ring(axis, False))
 
 
+def trade(near_side, far_side):
+    far_pairs = [(i + 1, (i + 2) % WIDE) for i in range(0, WIDE, 2)]
+    near_pairs = [(i, i + 1) for i in range(0, WIDE, 2)]
+    got = []
+    for value, pairs in ((far_side, far_pairs), (near_side, near_pairs)):
+        got.append(lax.ppermute(value, "wide", pairs + [(j, i) for i, j in pairs]))
+    return got[1], got[0]
+
+
 def local(dens, vel, pres, fdens, fvel, fpres, counts, start):
     here = lax.axis_index("wide").astype(i32).reshape(1)
     (info,) = call(info_kernel, [SM] * 3, [((16,), i32, SM)], [], (counts, start, here))
@@ -728,10 +763,10 @@
     moved = (WIDE, 5, 32, 128)
     (sent,) = call(
         send_kernel,
-        [SM, ANY, ANY, ANY],
+        [SM, HBM, HBM, HBM],
         [(moved, f32, ANY)],
-        [dma((4, 12))],
-        (info, fdens, fvel, fpres),
+        [buf(*x.shape) for x in (fdens, fvel, fpres)] + [dma((4, 12)), dma((3,))],
+        [info] + [pltpu.with_memory_space_constraint(x, pltpu.HBM) for x in (fdens, fvel, fpres)],
     )
     came = lax.all_to_all(sent, "wide", split_axis=0, concat_axis=0, tiled=True)
 
@@ -746,21 +781,21 @@
     )
     zl0, zh0 = swap(plo, phi, "deep")
     (u0,) = call(halo_kernel, [VM] * 3, [vm(*FIELD)], [], (u0, zl0, zh0))
-    ul, ur = swap(u0, u0, "wide")
+    ra, rb = trade(u0, u0)
     mid, plo, phi, fa, fza = call(
         coarse_one,
-        [VM] * 3,
+        [SM] + [VM] * 3,
         [vm(5, 18, 8, 128), edge, edge, vm(5, 2, 8, 128), vm(*FIELD)],
         WIDE_PASS,
-        (u0, ul, ur),
+        (info, u0, ra, rb),
     )
     zl1, zh1 = swap(plo, phi, "deep")
     new, mx, mz = call(
         coarse_two,
-        [VM] * 8,
+        [SM] + [VM] * 8,
         [vm(5, 12, 8, 128), vm(5, 2, 8, 128), vm(*FIELD)],
         WIDE_PASS,
-        (u0, ul, ur, fa, fza, mid, zl1, zh1),
+        (info, u0, ra, rb, fa, fza, mid, zl1, zh1),
     )
 
     def rims(args, late):
@@ -772,18 +807,18 @@
             (info, *args),
         )
 
-    old = rims((u0, ul, ur), False)
+    old = rims((u0, ra, rb), False)
     late = rims((new,), True)
 
     strip = vm(5, 3, 4, 128)
     near = buf(5, 64, 128)
-    s, flo, fhi = call(
+    s, near_side, far_side = call(
         take_kernel, [SM, ANY], [vm(*FIELD), strip, strip], [near, dma((4,))], (info, came)
     )
     rx = rz = base = None
     for stage in range(4):
         theta = THETA[stage]
-        rl, rh = swap(flo, fhi, "wide")
+        ga, gb = trade(near_side, far_side)
         gx = [old[0]] * (theta < 1.0) + [late[0]] * (theta > 0.0)
         gz = [old[1]] * (theta < 1.0) + [late[1]] * (theta > 0.0)
         args = [info, s] + gz + ([rz] if stage else [])
@@ -794,7 +829,7 @@
             PASS,
             args,
         )
-        args = [info, s, rl, rh, pr, d] + gx
+        args = [info, s, ga, gb, pr, d] + gx
         args += ([base] if stage % 2 else []) + ([rx] if stage else [])
         if stage % 2 == 0:
             base = s
@@ -807,32 +842,29 @@
         )
         s, rx = got[:2]
         if stage < 3:
-            flo, fhi = got[2:]
+            near_side, far_side = got[2:]
     regs = (rx, rz)
     (gone,) = call(give_kernel, [SM, VM], [(moved, f32, ANY)], [near, dma((4,))], (info, s))
     home = lax.all_to_all(gone, "wide", split_axis=0, concat_axis=0, tiled=True)
     plane = vm(5, 8, 128)
-    w, low, high = call(
+    w, near_side, far_side = call(
         sync_kernel,
         [SM] + [VM] * 6,
         [vm(*FIELD), plane, plane],
         [],
         (info, s, regs[0], regs[1], new, mx, mz),
     )
-    from_left, from_right = swap(low, high, "wide")
-    (coarse_out,) = call(
-        last_kernel, [SM] + [VM] * 3, [vm(5, 8, 8, LIVE_Z)], [], (info, w, from_left, from_right)
-    )
+    ra, rb = trade(near_side, far_side)
     initial = jnp.stack(
         cons_of([fdens, fvel[:, :, 0], fvel[:, :, 1], fvel[:, :, 2], fpres]), axis=2
     )
-    (fine_out,) = call(
-        home_kernel,
-        [SM, ANY, ANY],
-        [(initial.shape, f32, ANY)],
+    coarse_out, fine_out = call(
+        last_kernel,
+        [SM, ANY, ANY] + [VM] * 3,
+        [vm(5, 8, 8, LIVE_Z), (initial.shape, f32, ANY)],
         [dma((4, 4))],
-        (info, home, initial),
-        alias={2: 0},
+        (info, home, initial, w, ra, rb),
+        alias={2: 1},
     )
     return coarse_out, fine_out
 

time: 122 us -> 112 us (0.918); the launches traced: 121 us -> 112 us
  starting transfers between devices: 52.7 us -> 39.9 us
  waiting for transfers between devices: 23.1 us -> 28.5 us
  local copies, waits for them, and re-layouts: 3.28 us -> 0.68 us
  Pallas kernels: 39.6 us -> 41.1 us
    ppermute x8 -> x2, starting transfers between devices: 34 us -> 5.89 us  [swap(): return (below, lax.ppermute(lo, axis, ring(axis, False)))]
    ppermute x0 -> x12, starting transfers between devices: none -> 21.9 us  [trade(): got.append(lax.ppermute(value, 'wide', pairs + [(j, i) for i, j in pairs]))]
    ppermute x0 -> x12, waiting for transfers between devices: none -> 14.2 us  [trade(): got.append(lax.ppermute(value, 'wide', pairs + [(j, i) for i, j in pairs]))]
    ppermute x8 -> x2, waiting for transfers between devices: 11.8 us -> 2.57 us  [swap(): below = lax.ppermute(hi, axis, ring(axis, True))]
    ppermute x8 -> x2, starting transfers between devices: 4.41 us -> 0.03 us  [swap(): below = lax.ppermute(hi, axis, ring(axis, True))]
    unnamed x17 -> x11, local copies, waits for them, and re-layouts: 3.28 us -> 0.68 us
    all_to_all x1, starting transfers between devices: 6.07 us -> 3.84 us  [local(): home = lax.all_to_all(gone, 'wide', split_axis=0, concat_axis=0, tiled=True)]
    pallas_call x21 -> x20, Pallas kernels: 39.6 us -> 41.1 us  [call(): pl.pallas_call(kernel, in_specs=ins, out_specs=[spec for _, _, spec in ou...]
  transfers between devices with their start and end apart: 18 -> 18, of which waited for: 5 -> 9; matrix products, arithmetic and copies ran while one was open for 0% -> 0% of each run, Pallas kernels for 24% -> 26%
where the time goes in v1:
time: 112 us
  Pallas kernels  41.1 us (37%)
  starting transfers between devices  39.9 us (36%)
  waiting for transfers between devices  28.5 us (25%)
  between operations  1.75 us (2%)
    pallas_call x20, Pallas kernels, call(): pl.pallas_call(kernel, in_specs=ins, out_specs=[spec for _, _, spec in ou...  41.1 us
    ppermute x12, starting transfers between devices, trade(): got.append(lax.ppermute(value, 'wide', pairs + [(j, i) for i, j in pairs]))  21.9 us
    ppermute x12, waiting for transfers between devices, trade(): got.append(lax.ppermute(value, 'wide', pairs + [(j, i) for i, j in pairs]))  14.2 us
    all_to_all x1, waiting for transfers between devices, local(): came = lax.all_to_all(sent, 'wide', split_axis=0, concat_axis=0, tiled=True)  10 us
    all_to_all x1, starting transfers between devices, local(): came = lax.all_to_all(sent, 'wide', split_axis=0, concat_axis=0, tiled=True)  8.22 us
    ppermute x2, starting transfers between devices, swap(): return (below, lax.ppermute(lo, axis, ring(axis, False)))  5.89 us
    all_to_all x1, starting transfers between devices, local(): home = lax.all_to_all(gone, 'wide', split_axis=0, concat_axis=0, tiled=True)  3.84 us
    ppermute x2, waiting for transfers between devices, swap(): below = lax.ppermute(hi, axis, ring(axis, True))  2.57 us
  transfers between devices with their start and end apart: 18, of which 9 were waited for; matrix products, arithmetic and copies ran while one was open for 0% of the time, Pallas kernels for 26%

profile of v1, /device:TPU:0, one launch (start us, length us, event | category | flops | bytes accessed | tf_op | source)
XLA Modules:
  0.0 112.0 jit_solution(3429408055937096144)
XLA Ops:
  1.3 0.6 copy-done
  1.9 1.3 %shard_map.95.info.refs_0_ = s32[16]{0:T(128)S(1)} custom-call(s32[1,16]{1,0:T(1,128)S(1)} %copy-done, s32[1]{0:T(128)S(6)} %copy.25.start, s32[1]{0:T(128)} %bitcast.here), custom_call_target="tpu_custom_call" | custom-call | tf_op jit(solution)/shard_map/pallas_call | solution.py:715
  3.2 2.6 %shard_map.96 = f32[16,5,32,128]{3,2,1,0:T(8,128)} custom-call(s32[16]{0:T(128)S(1)} %shard_map.95.info.refs_0_, f32[1,4,16,256]{3,2,1,0:T(8,128)} %dens_far.2, f32[1,4,3,16,256]{4,3,2,1,0:T(8,128)} %vel_far.2, f32[1,4,16,256]{3,2,1,0:T(8,128)} %pres_far.2), custom_call_target="tpu_custom_call" | custom-call | tf_op jit(solution)/shard_map/pallas_call | solution.py:715
  5.8 8.2 %all-to-all-start = ((f32[16,5,32,128]{3,2,1,0:T(8,128)}), f32[16,5,32,128]{3,2,1,0:T(8,128)S(1)}, u32[]{:S(2)}, u32[]{:S(2)}) async-start(f32[16,5,32,128]{3,2,1,0:T(8,128)} %shard_map.96), calls=%async_computation | async-start | bytes 2621440 | tf_op jit(solution)/shard_map/all_to_all | solution.py:771
  14.1 1.1 shard_map.98
  15.2 2.9 %collective-permute-start.3 = (f32[8,128]{1,0:T(8,128)S(1)}, f32[8,128]{1,0:T(8,128)S(1)}, u32[]{:S(2)}, u32[]{:S(2)}) collective-permute-start(f32[8,128]{1,0:T(8,128)S(1)} %get-tuple-element.54), channel_id=1, source_target_pairs={{1,0},{2,1},{3,2},{4,3},{5,4},{6,5},{7,6},{0,7},{9,8},{10,9},{11,1... | collective-permute-start | bytes 12296 | tf_op jit(solution)/shard_map/ppermute | solution.py:747
  18.1 1.3 %collective-permute-done.2.zl = f32[8,128]{1,0:T(8,128)S(1)} collective-permute-done((f32[8,128]{1,0:T(8,128)S(1)}, f32[8,128]{1,0:T(8,128)S(1)}, u32[]{:S(2)}, u32[]{:S(2)}) %collective-permute-start.2) | collective-permute-done | bytes 4128 | tf_op jit(solution)/shard_map/ppermute | solution.py:746
  19.4 0.0 collective-permute-done.3.zh
  19.5 0.1 shard_map.99.refs_1_.u.u0
  19.6 2.0 %collective-permute-start.4 = (f32[5,8,8,128]{3,2,1,0:T(8,128)S(1)}, f32[5,8,8,128]{3,2,1,0:T(8,128)S(1)}, u32[]{:S(2)}, u32[]{:S(2)}) collective-permute-start(f32[5,8,8,128]{3,2,1,0:T(8,128)S(1)} %shard_map.99.refs_1_.u.u0), channel_id=1, source_target_pairs={{0,8},{16,24},{32,40},{48,56},{64,72},{80,88},{96,104},{112,120},{... | collective-permute-start | bytes 491528 | tf_op jit(solution)/shard_map/ppermute | solution.py:755
  21.6 4.2 %collective-permute-start.5 = (f32[5,8,8,128]{3,2,1,0:T(8,128)S(1)}, f32[5,8,8,128]{3,2,1,0:T(8,128)S(1)}, u32[]{:S(2)}, u32[]{:S(2)}) collective-permute-start(f32[5,8,8,128]{3,2,1,0:T(8,128)S(1)} %shard_map.99.refs_1_.u.u0), channel_id=1, source_target_pairs={{8,16},{24,32},{40,48},{56,64},{72,80},{88,96},{104,112},{120,0},{... | collective-permute-start | bytes 491528 | tf_op jit(solution)/shard_map/ppermute | solution.py:755
  25.8 10.0 %all-to-all-done.far = f32[16,5,32,128]{3,2,1,0:T(8,128)S(1)} async-done(((f32[16,5,32,128]{3,2,1,0:T(8,128)}), f32[16,5,32,128]{3,2,1,0:T(8,128)S(1)}, u32[]{:S(2)}, u32[]{:S(2)}) %all-to-all-start) | async-done | bytes 1310752 | tf_op jit(solution)/shard_map/all_to_all | solution.py:771
  35.8 0.7 shard_map.97
  36.5 0.2 collective-permute-start
  36.7 1.2 %collective-permute-start.1 = (f32[5,3,4,128]{3,2,1,0:T(4,128)S(1)}, f32[5,3,4,128]{3,2,1,0:T(4,128)S(1)}, u32[]{:S(2)}, u32[]{:S(2)}) collective-permute-start(f32[5,3,4,128]{3,2,1,0:T(4,128)S(1)} %get-tuple-element.51), channel_id=1, source_target_pairs={{8,16},{24,32},{40,48},{56,64},{72,80},{88,96},{104,112},{120,0},{... | collective-permute-start | bytes 92168 | tf_op jit(solution)/shard_map/ppermute | solution.py:755
  38.0 2.4 %shard_map.100 = (f32[5,3,8,128]{3,2,1,0:T(8,128)S(1)}, f32[5,3,8,128]{3,2,1,0:T(8,128)S(1)}) custom-call(s32[16]{0:T(128)S(1)} %shard_map.95.info.refs_0_, f32[5,8,8,128]{3,2,1,0:T(8,128)S(1)} %shard_map.99.refs_1_.u.u0, f32[5,8,8,128]{3,2,1,0:T(8,128)S(1)} %collective-permute-done.4.refs_2_.ra, f32[5,8,8,128]{3,2,1,0:T(8,128)S(1)} %collective-permute-done.5.refs_3_.rb), custom_call_target="tpu_custom_call" | custom-call | tf_op jit(solution)/shard_map/pallas_call | solution.py:715
  40.4 2.7 %shard_map.101 = (f32[5,8,8,128]{3,2,1,0:T(8,128)S(1)}, f32[5,8,8,128]{3,2,1,0:T(8,128)S(1)}, f32[5,8,128]{2,1,0:T(8,128)S(1)}) custom-call(s32[16]{0:T(128)S(1)} %shard_map.95.info.refs_0_, f32[5,8,8,128]{3,2,1,0:T(8,128)S(1)} %get-tuple-element.49.refs_1_.refs_8_, f32[5,3,8,128]{3,2,1,0:T(8,128)S(1)} %get-tuple-element.55.refs_2_), custom_call_target="tpu_custom_call" | custom-call | tf_op jit(solution)/shard_map/pallas_call | solution.py:715
  43.1 0.9 collective-permute-done.1.refs_3_
  43.9 1.2 %shard_map.102 = (f32[5,8,8,128]{3,2,1,0:T(8,128)S(1)}, f32[5,8,128]{2,1,0:T(8,128)S(1)}, f32[5,3,4,128]{3,2,1,0:T(4,128)S(1)}, f32[5,3,4,128]{3,2,1,0:T(4,128)S(1)}) custom-call(s32[16]{0:T(128)S(1)} %shard_map.95.info.refs_0_, f32[5,8,8,128]{3,2,1,0:T(8,128)S(1)} %get-tuple-element.49.refs_1_.refs_8_, f32[5,3,4,128]{3,2,1,0:T(4,128)S(1)} %collective-permute-done.refs_2_, ...), custom_call_target="tpu_custom_call" | custom-call | tf_op jit(solution)/shard_map/pallas_call | solution.py:715
  45.2 0.1 collective-permute-start.6
  45.3 3.3 %collective-permute-start.7 = (f32[5,3,4,128]{3,2,1,0:T(4,128)S(1)}, f32[5,3,4,128]{3,2,1,0:T(4,128)S(1)}, u32[]{:S(2)}, u32[]{:S(2)}) collective-permute-start(f32[5,3,4,128]{3,2,1,0:T(4,128)S(1)} %get-tuple-element.61), channel_id=1, source_target_pairs={{8,16},{24,32},{40,48},{56,64},{72,80},{88,96},{104,112},{120,0},{... | collective-permute-start | bytes 92168 | tf_op jit(solution)/shard_map/ppermute | solution.py:755
  48.6 5.1 %shard_map.103 = (f32[5,18,8,128]{3,2,1,0:T(8,128)S(1)}, f32[8,128]{1,0:T(8,128)S(1)}, f32[8,128]{1,0:T(8,128)S(1)}, f32[5,2,8,128]{3,2,1,0:T(8,128)S(1)}, f32[5,8,8,128]{3,2,1,0:T(8,128)S(1)}) custom-call(s32[16]{0:T(128)S(1)} %shard_map.95.info.refs_0_, f32[5,8,8,128]{3,2,1,0:T(8,128)S(1)} %shard_map.99.refs_1_.u.u0, ...), custom_call_target="tpu_custom_call" | custom-call | tf_op jit(solution)/shard_map/pallas_call | solution.py:715
  53.7 2.9 %collective-permute-start.9 = (f32[8,128]{1,0:T(8,128)S(1)}, f32[8,128]{1,0:T(8,128)S(1)}, u32[]{:S(2)}, u32[]{:S(2)}) collective-permute-start(f32[8,128]{1,0:T(8,128)S(1)} %get-tuple-element.66), channel_id=1, source_target_pairs={{1,0},{2,1},{3,2},{4,3},{5,4},{6,5},{7,6},{0,7},{9,8},{10,9},{11,1... | collective-permute-start | bytes 12296 | tf_op jit(solution)/shard_map/ppermute | solution.py:747
  56.6 1.3 %collective-permute-done.8.zl = f32[8,128]{1,0:T(8,128)S(1)} collective-permute-done((f32[8,128]{1,0:T(8,128)S(1)}, f32[8,128]{1,0:T(8,128)S(1)}, u32[]{:S(2)}, u32[]{:S(2)}) %collective-permute-start.8) | collective-permute-done | bytes 4128 | tf_op jit(solution)/shard_map/ppermute | solution.py:746
  57.9 0.0 collective-permute-done.9.zh
  58.0 3.7 %shard_map.104 = (f32[5,12,8,128]{3,2,1,0:T(8,128)S(1)}, f32[5,2,8,128]{3,2,1,0:T(8,128)S(1)}, f32[5,8,8,128]{3,2,1,0:T(8,128)S(1)}) custom-call(s32[16]{0:T(128)S(1)} %shard_map.95.info.refs_0_, f32[5,8,8,128]{3,2,1,0:T(8,128)S(1)} %shard_map.99.refs_1_.u.u0, f32[5,8,8,128]{3,2,1,0:T(8,128)S(1)} %collective-permute-done.4.refs_2_.ra, ...), custom_call_target="tpu_custom_call" | custom-call | tf_op jit(solution)/shard_map/pallas_call | solution.py:715
  61.6 2.4 %shard_map.105 = (f32[5,3,8,128]{3,2,1,0:T(8,128)S(1)}, f32[5,3,8,128]{3,2,1,0:T(8,128)S(1)}) custom-call(s32[16]{0:T(128)S(1)} %shard_map.95.info.refs_0_, f32[5,12,8,128]{3,2,1,0:T(8,128)S(1)} %get-tuple-element.67.refs_1_.new), custom_call_target="tpu_custom_call" | custom-call | tf_op jit(solution)/shard_map/pallas_call | solution.py:715
  64.0 2.6 %shard_map.106 = (f32[5,8,8,128]{3,2,1,0:T(8,128)S(1)}, f32[5,8,8,128]{3,2,1,0:T(8,128)S(1)}, f32[5,8,128]{2,1,0:T(8,128)S(1)}) custom-call(s32[16]{0:T(128)S(1)} %shard_map.95.info.refs_0_, f32[5,8,8,128]{3,2,1,0:T(8,128)S(1)} %get-tuple-element.59.refs_1_, f32[5,3,8,128]{3,2,1,0:T(8,128)S(1)} %get-tuple-element.55.refs_2_, ...), custom_call_target="tpu_custom_call" | custom-call | tf_op jit(solution)/shard_map/pallas_call | solution.py:715
  66.7 1.3 %shard_map.107 = (f32[5,8,8,128]{3,2,1,0:T(8,128)S(1)}, f32[5,8,128]{2,1,0:T(8,128)S(1)}, f32[5,3,4,128]{3,2,1,0:T(4,128)S(1)}, f32[5,3,4,128]{3,2,1,0:T(4,128)S(1)}) custom-call(s32[16]{0:T(128)S(1)} %shard_map.95.info.refs_0_, f32[5,8,8,128]{3,2,1,0:T(8,128)S(1)} %get-tuple-element.59.refs_1_, f32[5,3,4,128]{3,2,1,0:T(4,128)S(1)} %collective-permute-done.6.refs_2_, ...), custom_call_target="tpu_custom_call" | custom-call | tf_op jit(solution)/shard_map/pallas_call | solution.py:715
  68.0 0.1 collective-permute-start.10
  68.1 2.4 %collective-permute-start.11 = (f32[5,3,4,128]{3,2,1,0:T(4,128)S(1)}, f32[5,3,4,128]{3,2,1,0:T(4,128)S(1)}, u32[]{:S(2)}, u32[]{:S(2)}) collective-permute-start(f32[5,3,4,128]{3,2,1,0:T(4,128)S(1)} %get-tuple-element.76), channel_id=1, source_target_pairs={{8,16},{24,32},{40,48},{56,64},{72,80},{88,96},{104,112},{120,0},{... | collective-permute-start | bytes 92168 | tf_op jit(solution)/shard_map/ppermute | solution.py:755
  70.4 2.6 %shard_map.108 = (f32[5,8,8,128]{3,2,1,0:T(8,128)S(1)}, f32[5,8,8,128]{3,2,1,0:T(8,128)S(1)}, f32[5,8,128]{2,1,0:T(8,128)S(1)}) custom-call(s32[16]{0:T(128)S(1)} %shard_map.95.info.refs_0_, f32[5,8,8,128]{3,2,1,0:T(8,128)S(1)} %get-tuple-element.74.refs_1_.refs_7_, f32[5,3,8,128]{3,2,1,0:T(8,128)S(1)} %get-tuple-element.55.refs_2_, ...), custom_call_target="tpu_custom_call" | custom-call | tf_op jit(solution)/shard_map/pallas_call | solution.py:715
  73.1 2.5 %collective-permute-done.11.refs_3_ = f32[5,3,4,128]{3,2,1,0:T(4,128)S(1)} collective-permute-done((f32[5,3,4,128]{3,2,1,0:T(4,128)S(1)}, f32[5,3,4,128]{3,2,1,0:T(4,128)S(1)}, u32[]{:S(2)}, u32[]{:S(2)}) %collective-permute-start.11) | collective-permute-done | bytes 30752 | tf_op jit(solution)/shard_map/ppermute | solution.py:755
  75.6 1.2 %shard_map.109 = (f32[5,8,8,128]{3,2,1,0:T(8,128)S(1)}, f32[5,8,128]{2,1,0:T(8,128)S(1)}, f32[5,3,4,128]{3,2,1,0:T(4,128)S(1)}, f32[5,3,4,128]{3,2,1,0:T(4,128)S(1)}) custom-call(s32[16]{0:T(128)S(1)} %shard_map.95.info.refs_0_, f32[5,8,8,128]{3,2,1,0:T(8,128)S(1)} %get-tuple-element.74.refs_1_.refs_7_, ...), custom_call_target="tpu_custom_call" | custom-call | tf_op jit(solution)/shard_map/pallas_call | solution.py:715
  76.8 0.1 collective-permute-start.12
  76.9 2.2 %collective-permute-start.13 = (f32[5,3,4,128]{3,2,1,0:T(4,128)S(1)}, f32[5,3,4,128]{3,2,1,0:T(4,128)S(1)}, u32[]{:S(2)}, u32[]{:S(2)}) collective-permute-start(f32[5,3,4,128]{3,2,1,0:T(4,128)S(1)} %get-tuple-element.83), channel_id=1, source_target_pairs={{8,16},{24,32},{40,48},{56,64},{72,80},{88,96},{104,112},{120,0},{... | collective-permute-start | bytes 92168 | tf_op jit(solution)/shard_map/ppermute | solution.py:755
  79.1 2.6 %shard_map.110 = (f32[5,8,8,128]{3,2,1,0:T(8,128)S(1)}, f32[5,8,8,128]{3,2,1,0:T(8,128)S(1)}, f32[5,8,128]{2,1,0:T(8,128)S(1)}) custom-call(s32[16]{0:T(128)S(1)} %shard_map.95.info.refs_0_, f32[5,8,8,128]{3,2,1,0:T(8,128)S(1)} %get-tuple-element.81.refs_1_, f32[5,3,8,128]{3,2,1,0:T(8,128)S(1)} %get-tuple-element.68.refs_3_.refs_2_, ...), custom_call_target="tpu_custom_call" | custom-call | tf_op jit(solution)/shard_map/pallas_call | solution.py:715
  81.7 2.5 %collective-permute-done.13.refs_3_ = f32[5,3,4,128]{3,2,1,0:T(4,128)S(1)} collective-permute-done((f32[5,3,4,128]{3,2,1,0:T(4,128)S(1)}, f32[5,3,4,128]{3,2,1,0:T(4,128)S(1)}, u32[]{:S(2)}, u32[]{:S(2)}) %collective-permute-start.13) | collective-permute-done | bytes 30752 | tf_op jit(solution)/shard_map/ppermute | solution.py:755
  84.2 1.2 %shard_map.111 = (f32[5,8,8,128]{3,2,1,0:T(8,128)S(1)}, f32[5,8,128]{2,1,0:T(8,128)S(1)}) custom-call(s32[16]{0:T(128)S(1)} %shard_map.95.info.refs_0_, f32[5,8,8,128]{3,2,1,0:T(8,128)S(1)} %get-tuple-element.81.refs_1_, f32[5,3,4,128]{3,2,1,0:T(4,128)S(1)} %collective-permute-done.12.refs_2_, f32[5,3,4,128]{3,2,1,0:T(4,128)S(1)} %collective-permute-done.13.refs_3_, ...), custom_call_target="tpu_custom_call" | custom-call | tf_op jit(solution)/shard_map/pallas_call | solution.py:715
  85.4 1.3 %shard_map.112 = f32[16,5,32,128]{3,2,1,0:T(8,128)} custom-call(s32[16]{0:T(128)S(1)} %shard_map.95.info.refs_0_, f32[5,8,8,128]{3,2,1,0:T(8,128)S(1)} %get-tuple-element.88.s), custom_call_target="tpu_custom_call" | custom-call | tf_op jit(solution)/shard_map/pallas_call | solution.py:715
  86.7 3.8 %all-to-all-start.1 = ((f32[16,5,32,128]{3,2,1,0:T(8,128)}), f32[16,5,32,128]{3,2,1,0:T(8,128)S(1)}, u32[]{:S(2)}, u32[]{:S(2)}) async-start(f32[16,5,32,128]{3,2,1,0:T(8,128)} %shard_map.112), calls=%async_computation.1 | async-start | bytes 2621440 | tf_op jit(solution)/shard_map/all_to_all | solution.py:848
  90.7 2.9 %shard_map.113 = (f32[5,8,8,128]{3,2,1,0:T(8,128)S(1)}, f32[5,8,128]{2,1,0:T(8,128)S(1)}, f32[5,8,128]{2,1,0:T(8,128)S(1)}) custom-call(s32[16]{0:T(128)S(1)} %shard_map.95.info.refs_0_, f32[5,8,8,128]{3,2,1,0:T(8,128)S(1)} %get-tuple-element.88.s, f32[5,8,128]{2,1,0:T(8,128)S(1)} %get-tuple-element.89.rx, f32[5,8,128]{2,1,0:T(8,128)S(1)} %get-tuple-element.90.rz, ...), custom_call_target="tpu_custom_call" | custom-call | tf_op jit(solution)/shard_map/pallas_call | solution.py:715
  93.6 1.9 %collective-permute-start.14 = (f32[5,8,128]{2,1,0:T(8,128)S(1)}, f32[5,8,128]{2,1,0:T(8,128)S(1)}, u32[]{:S(2)}, u32[]{:S(2)}) collective-permute-start(f32[5,8,128]{2,1,0:T(8,128)S(1)} %get-tuple-element.94), channel_id=1, source_target_pairs={{0,8},{16,24},{32,40},{48,56},{64,72},{80,88},{96,104},{112,120},{... | collective-permute-start | bytes 61448 | tf_op jit(solution)/shard_map/ppermute | solution.py:755
  95.5 4.3 %collective-permute-start.15 = (f32[5,8,128]{2,1,0:T(8,128)S(1)}, f32[5,8,128]{2,1,0:T(8,128)S(1)}, u32[]{:S(2)}, u32[]{:S(2)}) collective-permute-start(f32[5,8,128]{2,1,0:T(8,128)S(1)} %get-tuple-element.95), channel_id=1, source_target_pairs={{8,16},{24,32},{40,48},{56,64},{72,80},{88,96},{104,112},{120,0},{... | collective-permute-start | bytes 61448 | tf_op jit(solution)/shard_map/ppermute | solution.py:755
  99.8 5.9 %collective-permute-done.14.ra = f32[5,8,128]{2,1,0:T(8,128)S(1)} collective-permute-done((f32[5,8,128]{2,1,0:T(8,128)S(1)}, f32[5,8,128]{2,1,0:T(8,128)S(1)}, u32[]{:S(2)}, u32[]{:S(2)}) %collective-permute-start.14) | collective-permute-done | bytes 20512 | tf_op jit(solution)/shard_map/ppermute | solution.py:755
  105.7 2.5 %collective-permute-done.15.rb = f32[5,8,128]{2,1,0:T(8,128)S(1)} collective-permute-done((f32[5,8,128]{2,1,0:T(8,128)S(1)}, f32[5,8,128]{2,1,0:T(8,128)S(1)}, u32[]{:S(2)}, u32[]{:S(2)}) %collective-permute-start.15) | collective-permute-done | bytes 20512 | tf_op jit(solution)/shard_map/ppermute | solution.py:755
  108.2 1.7 %all-to-all-done.1.far = f32[16,5,32,128]{3,2,1,0:T(8,128)S(1)} async-done(((f32[16,5,32,128]{3,2,1,0:T(8,128)}), f32[16,5,32,128]{3,2,1,0:T(8,128)S(1)}, u32[]{:S(2)}, u32[]{:S(2)}) %all-to-all-start.1) | async-done | bytes 1310752 | tf_op jit(solution)/shard_map/all_to_all | solution.py:848
  109.9 2.0 %shard_map.114 = (f32[5,8,8,120]{3,2,1,0:T(8,128)}, f32[1,4,5,16,256]{4,3,2,1,0:T(8,128)}) custom-call(s32[16]{0:T(128)S(1)} %shard_map.95.info.refs_0_, f32[16,5,32,128]{3,2,1,0:T(8,128)S(1)} %all-to-all-done.1.far, f32[1,4,5,16,256]{4,3,2,1,0:T(8,128)} %copy-done.3, f32[5,8,8,128]{3,2,1,0:T(8,128)S(1)} %get-tuple-element.93.w, ...), custom_call_target="tpu_custom_call", output_to_operand_aliasing={{1}: (2, {})} | custom-call | tf_op jit(solution)/shard_map/pallas_call | solution.py:715
  (23 shorter events, 0.2 us)
Async XLA Ops:
  1.3 0.7 copy-start
  5.8 30.0 %all-to-all-start = ((f32[16,5,32,128]{3,2,1,0:T(8,128)}), f32[16,5,32,128]{3,2,1,0:T(8,128)S(1)}, u32[]{:S(2)}, u32[]{:S(2)}) async-start(f32[16,5,32,128]{3,2,1,0:T(8,128)} %shard_map.96), calls=%async_computation | async-start | bytes 2621440 | tf_op jit(solution)/shard_map/all_to_all | solution.py:771
  15.2 4.3 %collective-permute-start.2 = (f32[8,128]{1,0:T(8,128)S(1)}, f32[8,128]{1,0:T(8,128)S(1)}, u32[]{:S(2)}, u32[]{:S(2)}) collective-permute-start(f32[8,128]{1,0:T(8,128)S(1)} %get-tuple-element.53), channel_id=1, source_target_pairs={{0,1},{1,2},{2,3},{3,4},{4,5},{5,6},{6,7},{7,0},{8,9},{9,10},{10,1... | collective-permute-start | bytes 12296 | tf_op jit(solution)/shard_map/ppermute | solution.py:746
  15.2 4.3 %collective-permute-start.3 = (f32[8,128]{1,0:T(8,128)S(1)}, f32[8,128]{1,0:T(8,128)S(1)}, u32[]{:S(2)}, u32[]{:S(2)}) collective-permute-start(f32[8,128]{1,0:T(8,128)S(1)} %get-tuple-element.54), channel_id=1, source_target_pairs={{1,0},{2,1},{3,2},{4,3},{5,4},{6,5},{7,6},{0,7},{9,8},{10,9},{11,1... | collective-permute-start | bytes 12296 | tf_op jit(solution)/shard_map/ppermute | solution.py:747
  19.6 18.3 %collective-permute-start.4 = (f32[5,8,8,128]{3,2,1,0:T(8,128)S(1)}, f32[5,8,8,128]{3,2,1,0:T(8,128)S(1)}, u32[]{:S(2)}, u32[]{:S(2)}) collective-permute-start(f32[5,8,8,128]{3,2,1,0:T(8,128)S(1)} %shard_map.99.refs_1_.u.u0), channel_id=1, source_target_pairs={{0,8},{16,24},{32,40},{48,56},{64,72},{80,88},{96,104},{112,120},{... | collective-permute-start | bytes 491528 | tf_op jit(solution)/shard_map/ppermute | solution.py:755
  21.6 16.3 %collective-permute-start.5 = (f32[5,8,8,128]{3,2,1,0:T(8,128)S(1)}, f32[5,8,8,128]{3,2,1,0:T(8,128)S(1)}, u32[]{:S(2)}, u32[]{:S(2)}) collective-permute-start(f32[5,8,8,128]{3,2,1,0:T(8,128)S(1)} %shard_map.99.refs_1_.u.u0), channel_id=1, source_target_pairs={{8,16},{24,32},{40,48},{56,64},{72,80},{88,96},{104,112},{120,0},{... | collective-permute-start | bytes 491528 | tf_op jit(solution)/shard_map/ppermute | solution.py:755
  36.5 6.5 %collective-permute-start = (f32[5,3,4,128]{3,2,1,0:T(4,128)S(1)}, f32[5,3,4,128]{3,2,1,0:T(4,128)S(1)}, u32[]{:S(2)}, u32[]{:S(2)}) collective-permute-start(f32[5,3,4,128]{3,2,1,0:T(4,128)S(1)} %get-tuple-element.50), channel_id=1, source_target_pairs={{0,8},{16,24},{32,40},{48,56},{64,72},{80,88},{96,104},{112,120},{... | collective-permute-start | bytes 92168 | tf_op jit(solution)/shard_map/ppermute | solution.py:755
  36.7 7.2 %collective-permute-start.1 = (f32[5,3,4,128]{3,2,1,0:T(4,128)S(1)}, f32[5,3,4,128]{3,2,1,0:T(4,128)S(1)}, u32[]{:S(2)}, u32[]{:S(2)}) collective-permute-start(f32[5,3,4,128]{3,2,1,0:T(4,128)S(1)} %get-tuple-element.51), channel_id=1, source_target_pairs={{8,16},{24,32},{40,48},{56,64},{72,80},{88,96},{104,112},{120,0},{... | collective-permute-start | bytes 92168 | tf_op jit(solution)/shard_map/ppermute | solution.py:755
  45.2 21.5 %collective-permute-start.6 = (f32[5,3,4,128]{3,2,1,0:T(4,128)S(1)}, f32[5,3,4,128]{3,2,1,0:T(4,128)S(1)}, u32[]{:S(2)}, u32[]{:S(2)}) collective-permute-start(f32[5,3,4,128]{3,2,1,0:T(4,128)S(1)} %get-tuple-element.60), channel_id=1, source_target_pairs={{0,8},{16,24},{32,40},{48,56},{64,72},{80,88},{96,104},{112,120},{... | collective-permute-start | bytes 92168 | tf_op jit(solution)/shard_map/ppermute | solution.py:755
  45.3 21.5 %collective-permute-start.7 = (f32[5,3,4,128]{3,2,1,0:T(4,128)S(1)}, f32[5,3,4,128]{3,2,1,0:T(4,128)S(1)}, u32[]{:S(2)}, u32[]{:S(2)}) collective-permute-start(f32[5,3,4,128]{3,2,1,0:T(4,128)S(1)} %get-tuple-element.61), channel_id=1, source_target_pairs={{8,16},{24,32},{40,48},{56,64},{72,80},{88,96},{104,112},{120,0},{... | collective-permute-start | bytes 92168 | tf_op jit(solution)/shard_map/ppermute | solution.py:755
  53.7 4.3 %collective-permute-start.8 = (f32[8,128]{1,0:T(8,128)S(1)}, f32[8,128]{1,0:T(8,128)S(1)}, u32[]{:S(2)}, u32[]{:S(2)}) collective-permute-start(f32[8,128]{1,0:T(8,128)S(1)} %get-tuple-element.65), channel_id=1, source_target_pairs={{0,1},{1,2},{2,3},{3,4},{4,5},{5,6},{6,7},{7,0},{8,9},{9,10},{10,1... | collective-permute-start | bytes 12296 | tf_op jit(solution)/shard_map/ppermute | solution.py:746
  53.7 4.3 %collective-permute-start.9 = (f32[8,128]{1,0:T(8,128)S(1)}, f32[8,128]{1,0:T(8,128)S(1)}, u32[]{:S(2)}, u32[]{:S(2)}) collective-permute-start(f32[8,128]{1,0:T(8,128)S(1)} %get-tuple-element.66), channel_id=1, source_target_pairs={{1,0},{2,1},{3,2},{4,3},{5,4},{6,5},{7,6},{0,7},{9,8},{10,9},{11,1... | collective-permute-start | bytes 12296 | tf_op jit(solution)/shard_map/ppermute | solution.py:747
  68.0 5.1 %collective-permute-start.10 = (f32[5,3,4,128]{3,2,1,0:T(4,128)S(1)}, f32[5,3,4,128]{3,2,1,0:T(4,128)S(1)}, u32[]{:S(2)}, u32[]{:S(2)}) collective-permute-start(f32[5,3,4,128]{3,2,1,0:T(4,128)S(1)} %get-tuple-element.75), channel_id=1, source_target_pairs={{0,8},{16,24},{32,40},{48,56},{64,72},{80,88},{96,104},{112,120},{... | collective-permute-start | bytes 92168 | tf_op jit(solution)/shard_map/ppermute | solution.py:755
  68.1 7.5 %collective-permute-start.11 = (f32[5,3,4,128]{3,2,1,0:T(4,128)S(1)}, f32[5,3,4,128]{3,2,1,0:T(4,128)S(1)}, u32[]{:S(2)}, u32[]{:S(2)}) collective-permute-start(f32[5,3,4,128]{3,2,1,0:T(4,128)S(1)} %get-tuple-element.76), channel_id=1, source_target_pairs={{8,16},{24,32},{40,48},{56,64},{72,80},{88,96},{104,112},{120,0},{... | collective-permute-start | bytes 92168 | tf_op jit(solution)/shard_map/ppermute | solution.py:755
  76.8 4.9 %collective-permute-start.12 = (f32[5,3,4,128]{3,2,1,0:T(4,128)S(1)}, f32[5,3,4,128]{3,2,1,0:T(4,128)S(1)}, u32[]{:S(2)}, u32[]{:S(2)}) collective-permute-start(f32[5,3,4,128]{3,2,1,0:T(4,128)S(1)} %get-tuple-element.82), channel_id=1, source_target_pairs={{0,8},{16,24},{32,40},{48,56},{64,72},{80,88},{96,104},{112,120},{... | collective-permute-start | bytes 92168 | tf_op jit(solution)/shard_map/ppermute | solution.py:755
  76.9 7.3 %collective-permute-start.13 = (f32[5,3,4,128]{3,2,1,0:T(4,128)S(1)}, f32[5,3,4,128]{3,2,1,0:T(4,128)S(1)}, u32[]{:S(2)}, u32[]{:S(2)}) collective-permute-start(f32[5,3,4,128]{3,2,1,0:T(4,128)S(1)} %get-tuple-element.83), channel_id=1, source_target_pairs={{8,16},{24,32},{40,48},{56,64},{72,80},{88,96},{104,112},{120,0},{... | collective-permute-start | bytes 92168 | tf_op jit(solution)/shard_map/ppermute | solution.py:755
  86.7 3.9 %copy-start.1 = (f32[1,4,16,256]{3,2,1,0:T(8,128)S(1)}, f32[1,4,16,256]{3,2,1,0:T(8,128)}, u32[]{:S(2)}) copy-start(f32[1,4,16,256]{3,2,1,0:T(8,128)} %dens_far.2) | copy-start | bytes 196612
  86.7 3.9 %copy-start.2 = (f32[1,4,3,16,256]{4,3,2,1,0:T(8,128)S(1)}, f32[1,4,3,16,256]{4,3,2,1,0:T(8,128)}, u32[]{:S(2)}) copy-start(f32[1,4,3,16,256]{4,3,2,1,0:T(8,128)} %vel_far.2) | copy-start | bytes 589828
  86.7 23.2 %all-to-all-start.1 = ((f32[16,5,32,128]{3,2,1,0:T(8,128)}), f32[16,5,32,128]{3,2,1,0:T(8,128)S(1)}, u32[]{:S(2)}, u32[]{:S(2)}) async-start(f32[16,5,32,128]{3,2,1,0:T(8,128)} %shard_map.112), calls=%async_computation.1 | async-start | bytes 2621440 | tf_op jit(solution)/shard_map/all_to_all | solution.py:848
  90.6 9.2 %copy-start.4 = (f32[1,4,16,256]{3,2,1,0:T(8,128)S(1)}, f32[1,4,16,256]{3,2,1,0:T(8,128)}, u32[]{:S(2)}) copy-start(f32[1,4,16,256]{3,2,1,0:T(8,128)} %pres_far.2) | copy-start | bytes 196612
  93.6 12.1 %collective-permute-start.14 = (f32[5,8,128]{2,1,0:T(8,128)S(1)}, f32[5,8,128]{2,1,0:T(8,128)S(1)}, u32[]{:S(2)}, u32[]{:S(2)}) collective-permute-start(f32[5,8,128]{2,1,0:T(8,128)S(1)} %get-tuple-element.94), channel_id=1, source_target_pairs={{0,8},{16,24},{32,40},{48,56},{64,72},{80,88},{96,104},{112,120},{... | collective-permute-start | bytes 61448 | tf_op jit(solution)/shard_map/ppermute | solution.py:755
  95.5 12.7 %collective-permute-start.15 = (f32[5,8,128]{2,1,0:T(8,128)S(1)}, f32[5,8,128]{2,1,0:T(8,128)S(1)}, u32[]{:S(2)}, u32[]{:S(2)}) collective-permute-start(f32[5,8,128]{2,1,0:T(8,128)S(1)} %get-tuple-element.95), channel_id=1, source_target_pairs={{8,16},{24,32},{40,48},{56,64},{72,80},{88,96},{104,112},{120,0},{... | collective-permute-start | bytes 61448 | tf_op jit(solution)/shard_map/ppermute | solution.py:755
  99.8 10.1 %copy-start.3 = (f32[1,4,5,16,256]{4,3,2,1,0:T(8,128)}, f32[1,4,5,16,256]{4,3,2,1,0:T(8,128)S(1)}, u32[]{:S(2)}) copy-start(f32[1,4,5,16,256]{4,3,2,1,0:T(8,128)S(1)} %fusion.6.initial) | copy-start | bytes 983044

commit v2 on v1

--- a/solution.py
+++ b/solution.py
@@ -129,21 +129,22 @@
 UNROLL_CELLS, UNROLL_FACES, UNROLL_ROLLS = 2, 9, 4
 
 
+def major_cells(q, sl, sr, m):
+    for c in range(5):
+        l, r = recon(*[q[c, m + k] for k in range(5)])
+        sl[c, m] = l
+        sr[c, m] = r
+
+
+def major_faces(sl, sr, fx, n, f):
+    out = hllc([sl[c, f] for c in range(5)], [sr[c, f + 1] for c in range(5)], n)
+    for c in range(5):
+        fx[c, f] = out[c]
+
+
 def major_pass(q, sl, sr, fx, n, count=10):
-    def cells(m):
-        for c in range(5):
-            l, r = recon(*[q[c, m + k] for k in range(5)])
-            sl[c, m] = l
-            sr[c, m] = r
-
-    repeat(count, UNROLL_CELLS, cells)
-
-    def faces(f):
-        out = hllc([sl[c, f] for c in range(5)], [sr[c, f + 1] for c in range(5)], n)
-        for c in range(5):
-            fx[c, f] = out[c]
-
-    repeat(count - 1, UNROLL_FACES, faces)
+    repeat(count, UNROLL_CELLS, lambda m: major_cells(q, sl, sr, m))
+    repeat(count - 1, UNROLL_FACES, lambda f: major_faces(sl, sr, fx, n, f))
 
 
 def roll_pass(q, d, shift, n, count=8, keep=None, at=3):
@@ -318,7 +319,7 @@
             near_side[c, g], far_side[c, g] = by_parity(info, s[c, g, 0:4, :], s[c, g + 5, 4:8, :])
 
 
-def give_kernel(info, s, far, near, sem):
+def give(info, s, far, near, sem):
     for m in range(8):
         for c in range(5):
             near[c, pl.ds(m, 8, stride=8), :] = s[c, m]
@@ -528,7 +529,7 @@
     theta = THETA[stage]
     refs = list(refs)
     info, s, old, new, reg = split_refs(refs, (1, 1, theta < 1.0, theta > 0.0, stage))
-    pr, d, rz, q, sl, sr, fx = refs
+    pr, d, rz, inner, q, sl, sr, fx = refs
     _, second, upper_z = places_of_rows()
     for m in range(8):
         p = prims_of([s[c, m] for c in range(5)])
@@ -554,16 +555,28 @@
         for m in range(8):
             d[c, m] = t[m]
     roll_pass(pr, d, y_shift, 2, at=0)
+    for c in range(5):
+        for m in range(8):
+            q[c, m + 3] = pr[c, m]
+    repeat(4, 2, lambda m: major_cells(q, sl, sr, m + 3))
+    for f in range(3, 6):
+        major_faces(sl, sr, fx, 1, f)
+    for c in range(5):
+        for f in range(3):
+            inner[c, f] = fx[c, f + 3]
+        inner[c, 3] = sr[c, 3]
+        inner[c, 4] = sl[c, 6]
 
 
 def x_kernel(*refs, stage):
     theta = THETA[stage]
     refs = list(refs)
-    info, s, ra, rb, pr, d, old, new, base, reg = split_refs(
-        refs, (1,) * 6 + (theta < 1.0, theta > 0.0, stage % 2, stage)
-    )
-    out, rx, near_side, far_side = split_refs(refs, (1, 1, stage < 3, stage < 3))
-    q, sl, sr, fx, near = refs
+    info, s, ra, rb, pr, d, inner, old, new, base, reg = split_refs(
+        refs, (1,) * 7 + (theta < 1.0, theta > 0.0, stage % 2, stage)
+    )
+    more = stage < 3
+    out, rx, near_side, far_side, gone = split_refs(refs, (1, 1, more, more, not more))
+    q, sl, sr, fx, near = refs[:5]
     upper_x, second, _ = places_of_rows()
     for c in range(5):
         for g in range(3):
@@ -590,7 +603,15 @@
         for c in range(5):
             q[c, g] = jnp.where(upper_x, roll(pr[c, g + 5], 4, 0), p[c])
             q[c, g + 11] = jnp.where(upper_x, p[c], roll(pr[c, g], 4, 0))
-    major_pass(q, sl, sr, fx, 1)
+    for c in range(5):
+        for f in range(3):
+            fx[c, f + 3] = inner[c, f]
+        sr[c, 3] = inner[c, 3]
+        sl[c, 6] = inner[c, 4]
+    repeat(3, 3, lambda m: major_cells(q, sl, sr, m))
+    repeat(3, 3, lambda m: major_cells(q, sl, sr, m + 7))
+    for f in (0, 1, 2, 6, 7, 8):
+        major_faces(sl, sr, fx, 1, f)
     for c in range(5):
         face = jnp.where(upper_x, fx[c, 8], fx[c, 0])
         rx[c] = face if reg is None else reg[c] + face
@@ -600,8 +621,10 @@
                 out[c, m] = s[c, m] - 0.2 * change
             else:
                 out[c, m] = 0.5 * (base[c, m] + s[c, m]) - 0.1 * change
-    if stage < 3:
+    if more:
         sides(info, out, near_side, far_side)
+    else:
+        give(info, out, gone, *refs[5:])
 
 
 def sync_kernel(info, s, rx, rz, new, mx, mz, out, near_side, far_side):
@@ -822,29 +845,29 @@
         gx = [old[0]] * (theta < 1.0) + [late[0]] * (theta > 0.0)
         gz = [old[1]] * (theta < 1.0) + [late[1]] * (theta > 0.0)
         args = [info, s] + gz + ([rz] if stage else [])
-        pr, d, rz = call(
+        pr, d, rz, inner = call(
             lambda *refs, stage=stage: yz_kernel(*refs, stage=stage),
             [SM] + [VM] * (len(args) - 1),
-            [vm(*FIELD), vm(*FIELD), vm(5, 8, 128)],
+            [vm(*FIELD), vm(*FIELD), vm(5, 8, 128), vm(5, 5, 8, 128)],
             PASS,
             args,
         )
-        args = [info, s, ga, gb, pr, d] + gx
+        args = [info, s, ga, gb, pr, d, inner] + gx
         args += ([base] if stage % 2 else []) + ([rx] if stage else [])
         if stage % 2 == 0:
             base = s
         got = call(
             lambda *refs, stage=stage: x_kernel(*refs, stage=stage),
             [SM] + [VM] * (len(args) - 1),
-            [vm(*FIELD), vm(5, 8, 128)] + ([strip, strip] if stage < 3 else []),
-            PASS + [buf(5, 3, 8, 128)],
+            [vm(*FIELD), vm(5, 8, 128)] + ([strip, strip] if stage < 3 else [(moved, f32, ANY)]),
+            PASS + [buf(5, 3, 8, 128)] + ([] if stage < 3 else [near, dma((4,))]),
             args,
         )
         s, rx = got[:2]
         if stage < 3:
             near_side, far_side = got[2:]
     regs = (rx, rz)
-    (gone,) = call(give_kernel, [SM, VM], [(moved, f32, ANY)], [near, dma((4,))], (info, s))
+    gone = got[2]
     home = lax.all_to_all(gone, "wide", split_axis=0, concat_axis=0, tiled=True)
     plane = vm(5, 8, 128)
     w, near_side, far_side = call(

time: 112 us -> 111 us (level)
    pallas_call x20 -> x19, Pallas kernels: 41.1 us -> 40.3 us  [call(): pl.pallas_call(kernel, in_specs=ins, out_specs=[spec for _, _, spec in ou...]
  transfers between devices with their start and end apart: 18 -> 18, of which waited for: 9 -> 9; matrix products, arithmetic and copies ran while one was open for 0% -> 0% of each run, Pallas kernels for 26% -> 27%
where the time goes in v2:
time: 111 us
  Pallas kernels  40.3 us (36%)
  starting transfers between devices  39.6 us (36%)
  waiting for transfers between devices  28.3 us (25%)
  between operations  1.73 us (2%)
    pallas_call x19, Pallas kernels, call(): pl.pallas_call(kernel, in_specs=ins, out_specs=[spec for _, _, spec in ou...  40.3 us
    ppermute x12, starting transfers between devices, trade(): got.append(lax.ppermute(value, 'wide', pairs + [(j, i) for i, j in pairs]))  21.6 us
    ppermute x12, waiting for transfers between devices, trade(): got.append(lax.ppermute(value, 'wide', pairs + [(j, i) for i, j in pairs]))  13.9 us
    all_to_all x1, waiting for transfers between devices, local(): came = lax.all_to_all(sent, 'wide', split_axis=0, concat_axis=0, tiled=True)  10 us
    all_to_all x1, starting transfers between devices, local(): came = lax.all_to_all(sent, 'wide', split_axis=0, concat_axis=0, tiled=True)  8.22 us
    ppermute x2, starting transfers between devices, swap(): return (below, lax.ppermute(lo, axis, ring(axis, False)))  5.89 us
    all_to_all x1, starting transfers between devices, local(): home = lax.all_to_all(gone, 'wide', split_axis=0, concat_axis=0, tiled=True)  3.84 us
    ppermute x2, waiting for transfers between devices, swap(): below = lax.ppermute(hi, axis, ring(axis, True))  2.57 us
  transfers between devices with their start and end apart: 18, of which 9 were waited for; matrix products, arithmetic and copies ran while one was open for 0% of the time, Pallas kernels for 27%

profile of v2, /device:TPU:0, one launch (start us, length us, event | category | flops | bytes accessed | tf_op | source)
XLA Modules:
  0.0 110.7 jit_solution(17780443513584211611)
XLA Ops:
  1.3 0.6 copy-done
  1.9 1.3 %shard_map.95.info.refs_0_ = s32[16]{0:T(128)S(1)} custom-call(s32[1,16]{1,0:T(1,128)S(1)} %copy-done, s32[1]{0:T(128)S(6)} %copy.25.start, s32[1]{0:T(128)} %bitcast.here), custom_call_target="tpu_custom_call" | custom-call | tf_op jit(solution)/shard_map/pallas_call | solution.py:738
  3.2 2.6 %shard_map.96 = f32[16,5,32,128]{3,2,1,0:T(8,128)} custom-call(s32[16]{0:T(128)S(1)} %shard_map.95.info.refs_0_, f32[1,4,16,256]{3,2,1,0:T(8,128)} %dens_far.2, f32[1,4,3,16,256]{4,3,2,1,0:T(8,128)} %vel_far.2, f32[1,4,16,256]{3,2,1,0:T(8,128)} %pres_far.2), custom_call_target="tpu_custom_call" | custom-call | tf_op jit(solution)/shard_map/pallas_call | solution.py:738
  5.8 8.2 %all-to-all-start = ((f32[16,5,32,128]{3,2,1,0:T(8,128)}), f32[16,5,32,128]{3,2,1,0:T(8,128)S(1)}, u32[]{:S(2)}, u32[]{:S(2)}) async-start(f32[16,5,32,128]{3,2,1,0:T(8,128)} %shard_map.96), calls=%async_computation | async-start | bytes 2621440 | tf_op jit(solution)/shard_map/all_to_all | solution.py:794
  14.1 1.1 %shard_map.98 = (f32[5,8,8,128]{3,2,1,0:T(8,128)S(1)}, f32[8,128]{1,0:T(8,128)S(1)}, f32[8,128]{1,0:T(8,128)S(1)}) custom-call(f32[8,8,120]{2,1,0:T(8,128)} %dens_far.3, f32[3,8,8,120]{3,2,1,0:T(8,128)} %vel_far.3, f32[8,8,120]{2,1,0:T(8,128)} %pres_far.3), custom_call_target="tpu_custom_call" | custom-call | tf_op jit(solution)/shard_map/pallas_call | solution.py:738
  15.2 0.0 collective-permute-start.2
  15.2 2.9 %collective-permute-start.3 = (f32[8,128]{1,0:T(8,128)S(1)}, f32[8,128]{1,0:T(8,128)S(1)}, u32[]{:S(2)}, u32[]{:S(2)}) collective-permute-start(f32[8,128]{1,0:T(8,128)S(1)} %get-tuple-element.59), channel_id=1, source_target_pairs={{1,0},{2,1},{3,2},{4,3},{5,4},{6,5},{7,6},{0,7},{9,8},{10,9},{11,1... | collective-permute-start | bytes 12296 | tf_op jit(solution)/shard_map/ppermute | solution.py:770
  18.1 1.3 %collective-permute-done.2.zl = f32[8,128]{1,0:T(8,128)S(1)} collective-permute-done((f32[8,128]{1,0:T(8,128)S(1)}, f32[8,128]{1,0:T(8,128)S(1)}, u32[]{:S(2)}, u32[]{:S(2)}) %collective-permute-start.2) | collective-permute-done | bytes 4128 | tf_op jit(solution)/shard_map/ppermute | solution.py:769
  19.4 0.0 collective-permute-done.3.zh
  19.5 0.1 shard_map.99.refs_1_.u.u0
  19.6 2.0 %collective-permute-start.4 = (f32[5,8,8,128]{3,2,1,0:T(8,128)S(1)}, f32[5,8,8,128]{3,2,1,0:T(8,128)S(1)}, u32[]{:S(2)}, u32[]{:S(2)}) collective-permute-start(f32[5,8,8,128]{3,2,1,0:T(8,128)S(1)} %shard_map.99.refs_1_.u.u0), channel_id=1, source_target_pairs={{0,8},{16,24},{32,40},{48,56},{64,72},{80,88},{96,104},{112,120},{... | collective-permute-start | bytes 491528 | tf_op jit(solution)/shard_map/ppermute | solution.py:778
  21.6 4.2 %collective-permute-start.5 = (f32[5,8,8,128]{3,2,1,0:T(8,128)S(1)}, f32[5,8,8,128]{3,2,1,0:T(8,128)S(1)}, u32[]{:S(2)}, u32[]{:S(2)}) collective-permute-start(f32[5,8,8,128]{3,2,1,0:T(8,128)S(1)} %shard_map.99.refs_1_.u.u0), channel_id=1, source_target_pairs={{8,16},{24,32},{40,48},{56,64},{72,80},{88,96},{104,112},{120,0},{... | collective-permute-start | bytes 491528 | tf_op jit(solution)/shard_map/ppermute | solution.py:778
  25.8 10.0 %all-to-all-done.far = f32[16,5,32,128]{3,2,1,0:T(8,128)S(1)} async-done(((f32[16,5,32,128]{3,2,1,0:T(8,128)}), f32[16,5,32,128]{3,2,1,0:T(8,128)S(1)}, u32[]{:S(2)}, u32[]{:S(2)}) %all-to-all-start) | async-done | bytes 1310752 | tf_op jit(solution)/shard_map/all_to_all | solution.py:794
  35.8 0.7 shard_map.97
  36.5 0.2 collective-permute-start
  36.7 1.2 %collective-permute-start.1 = (f32[5,3,4,128]{3,2,1,0:T(4,128)S(1)}, f32[5,3,4,128]{3,2,1,0:T(4,128)S(1)}, u32[]{:S(2)}, u32[]{:S(2)}) collective-permute-start(f32[5,3,4,128]{3,2,1,0:T(4,128)S(1)} %get-tuple-element.56), channel_id=1, source_target_pairs={{8,16},{24,32},{40,48},{56,64},{72,80},{88,96},{104,112},{120,0},{... | collective-permute-start | bytes 92168 | tf_op jit(solution)/shard_map/ppermute | solution.py:778
  38.0 2.4 %shard_map.100 = (f32[5,3,8,128]{3,2,1,0:T(8,128)S(1)}, f32[5,3,8,128]{3,2,1,0:T(8,128)S(1)}) custom-call(s32[16]{0:T(128)S(1)} %shard_map.95.info.refs_0_, f32[5,8,8,128]{3,2,1,0:T(8,128)S(1)} %shard_map.99.refs_1_.u.u0, f32[5,8,8,128]{3,2,1,0:T(8,128)S(1)} %collective-permute-done.4.refs_2_.ra, f32[5,8,8,128]{3,2,1,0:T(8,128)S(1)} %collective-permute-done.5.refs_3_.rb), custom_call_target="tpu_custom_call" | custom-call | tf_op jit(solution)/shard_map/pallas_call | solution.py:738
  40.4 2.9 %shard_map.101 = (f32[5,8,8,128]{3,2,1,0:T(8,128)S(1)}, f32[5,8,8,128]{3,2,1,0:T(8,128)S(1)}, f32[5,8,128]{2,1,0:T(8,128)S(1)}, f32[5,5,8,128]{3,2,1,0:T(8,128)S(1)}) custom-call(s32[16]{0:T(128)S(1)} %shard_map.95.info.refs_0_, f32[5,8,8,128]{3,2,1,0:T(8,128)S(1)} %get-tuple-element.54.refs_1_.refs_9_, f32[5,3,8,128]{3,2,1,0:T(8,128)S(1)} %get-tuple-element.60.refs_2_), custom_call_target="tpu_custom_call" | custom-call | tf_op jit(solution)/shard_map/pallas_call | solution.py:738
  43.3 0.6 collective-permute-done.1.refs_3_
  43.9 0.9 shard_map.102
  44.9 0.2 collective-permute-start.6
  45.0 3.5 %collective-permute-start.7 = (f32[5,3,4,128]{3,2,1,0:T(4,128)S(1)}, f32[5,3,4,128]{3,2,1,0:T(4,128)S(1)}, u32[]{:S(2)}, u32[]{:S(2)}) collective-permute-start(f32[5,3,4,128]{3,2,1,0:T(4,128)S(1)} %get-tuple-element.67), channel_id=1, source_target_pairs={{8,16},{24,32},{40,48},{56,64},{72,80},{88,96},{104,112},{120,0},{... | collective-permute-start | bytes 92168 | tf_op jit(solution)/shard_map/ppermute | solution.py:778
  48.5 5.1 %shard_map.103 = (f32[5,18,8,128]{3,2,1,0:T(8,128)S(1)}, f32[8,128]{1,0:T(8,128)S(1)}, f32[8,128]{1,0:T(8,128)S(1)}, f32[5,2,8,128]{3,2,1,0:T(8,128)S(1)}, f32[5,8,8,128]{3,2,1,0:T(8,128)S(1)}) custom-call(s32[16]{0:T(128)S(1)} %shard_map.95.info.refs_0_, f32[5,8,8,128]{3,2,1,0:T(8,128)S(1)} %shard_map.99.refs_1_.u.u0, ...), custom_call_target="tpu_custom_call" | custom-call | tf_op jit(solution)/shard_map/pallas_call | solution.py:738
  53.6 2.9 %collective-permute-start.9 = (f32[8,128]{1,0:T(8,128)S(1)}, f32[8,128]{1,0:T(8,128)S(1)}, u32[]{:S(2)}, u32[]{:S(2)}) collective-permute-start(f32[8,128]{1,0:T(8,128)S(1)} %get-tuple-element.72), channel_id=1, source_target_pairs={{1,0},{2,1},{3,2},{4,3},{5,4},{6,5},{7,6},{0,7},{9,8},{10,9},{11,1... | collective-permute-start | bytes 12296 | tf_op jit(solution)/shard_map/ppermute | solution.py:770
  56.6 1.3 %collective-permute-done.8.zl = f32[8,128]{1,0:T(8,128)S(1)} collective-permute-done((f32[8,128]{1,0:T(8,128)S(1)}, f32[8,128]{1,0:T(8,128)S(1)}, u32[]{:S(2)}, u32[]{:S(2)}) %collective-permute-start.8) | collective-permute-done | bytes 4128 | tf_op jit(solution)/shard_map/ppermute | solution.py:769
  57.9 0.0 collective-permute-done.9.zh
  57.9 3.7 %shard_map.104 = (f32[5,12,8,128]{3,2,1,0:T(8,128)S(1)}, f32[5,2,8,128]{3,2,1,0:T(8,128)S(1)}, f32[5,8,8,128]{3,2,1,0:T(8,128)S(1)}) custom-call(s32[16]{0:T(128)S(1)} %shard_map.95.info.refs_0_, f32[5,8,8,128]{3,2,1,0:T(8,128)S(1)} %shard_map.99.refs_1_.u.u0, f32[5,8,8,128]{3,2,1,0:T(8,128)S(1)} %collective-permute-done.4.refs_2_.ra, ...), custom_call_target="tpu_custom_call" | custom-call | tf_op jit(solution)/shard_map/pallas_call | solution.py:738
  61.6 2.4 %shard_map.105 = (f32[5,3,8,128]{3,2,1,0:T(8,128)S(1)}, f32[5,3,8,128]{3,2,1,0:T(8,128)S(1)}) custom-call(s32[16]{0:T(128)S(1)} %shard_map.95.info.refs_0_, f32[5,12,8,128]{3,2,1,0:T(8,128)S(1)} %get-tuple-element.73.refs_1_.new), custom_call_target="tpu_custom_call" | custom-call | tf_op jit(solution)/shard_map/pallas_call | solution.py:738
  64.0 2.9 %shard_map.106 = (f32[5,8,8,128]{3,2,1,0:T(8,128)S(1)}, f32[5,8,8,128]{3,2,1,0:T(8,128)S(1)}, f32[5,8,128]{2,1,0:T(8,128)S(1)}, f32[5,5,8,128]{3,2,1,0:T(8,128)S(1)}) custom-call(s32[16]{0:T(128)S(1)} %shard_map.95.info.refs_0_, f32[5,8,8,128]{3,2,1,0:T(8,128)S(1)} %get-tuple-element.65.refs_1_, f32[5,3,8,128]{3,2,1,0:T(8,128)S(1)} %get-tuple-element.60.refs_2_, ...), custom_call_target="tpu_custom_call" | custom-call | tf_op jit(solution)/shard_map/pallas_call | solution.py:738
  66.9 0.9 shard_map.107
  67.9 0.1 collective-permute-start.10
  68.0 2.1 %collective-permute-start.11 = (f32[5,3,4,128]{3,2,1,0:T(4,128)S(1)}, f32[5,3,4,128]{3,2,1,0:T(4,128)S(1)}, u32[]{:S(2)}, u32[]{:S(2)}) collective-permute-start(f32[5,3,4,128]{3,2,1,0:T(4,128)S(1)} %get-tuple-element.83), channel_id=1, source_target_pairs={{8,16},{24,32},{40,48},{56,64},{72,80},{88,96},{104,112},{120,0},{... | collective-permute-start | bytes 92168 | tf_op jit(solution)/shard_map/ppermute | solution.py:778
  70.1 2.9 %shard_map.108 = (f32[5,8,8,128]{3,2,1,0:T(8,128)S(1)}, f32[5,8,8,128]{3,2,1,0:T(8,128)S(1)}, f32[5,8,128]{2,1,0:T(8,128)S(1)}, f32[5,5,8,128]{3,2,1,0:T(8,128)S(1)}) custom-call(s32[16]{0:T(128)S(1)} %shard_map.95.info.refs_0_, f32[5,8,8,128]{3,2,1,0:T(8,128)S(1)} %get-tuple-element.81.refs_1_.refs_8_, f32[5,3,8,128]{3,2,1,0:T(8,128)S(1)} %get-tuple-element.60.refs_2_, ...), custom_call_target="tpu_custom_call" | custom-call | tf_op jit(solution)/shard_map/pallas_call | solution.py:738
  73.0 2.5 %collective-permute-done.11.refs_3_ = f32[5,3,4,128]{3,2,1,0:T(4,128)S(1)} collective-permute-done((f32[5,3,4,128]{3,2,1,0:T(4,128)S(1)}, f32[5,3,4,128]{3,2,1,0:T(4,128)S(1)}, u32[]{:S(2)}, u32[]{:S(2)}) %collective-permute-start.11) | collective-permute-done | bytes 30752 | tf_op jit(solution)/shard_map/ppermute | solution.py:778
  75.4 0.9 shard_map.109
  76.4 0.1 collective-permute-start.12
  76.5 1.9 %collective-permute-start.13 = (f32[5,3,4,128]{3,2,1,0:T(4,128)S(1)}, f32[5,3,4,128]{3,2,1,0:T(4,128)S(1)}, u32[]{:S(2)}, u32[]{:S(2)}) collective-permute-start(f32[5,3,4,128]{3,2,1,0:T(4,128)S(1)} %get-tuple-element.91), channel_id=1, source_target_pairs={{8,16},{24,32},{40,48},{56,64},{72,80},{88,96},{104,112},{120,0},{... | collective-permute-start | bytes 92168 | tf_op jit(solution)/shard_map/ppermute | solution.py:778
  78.4 2.9 %shard_map.110 = (f32[5,8,8,128]{3,2,1,0:T(8,128)S(1)}, f32[5,8,8,128]{3,2,1,0:T(8,128)S(1)}, f32[5,8,128]{2,1,0:T(8,128)S(1)}, f32[5,5,8,128]{3,2,1,0:T(8,128)S(1)}) custom-call(s32[16]{0:T(128)S(1)} %shard_map.95.info.refs_0_, f32[5,8,8,128]{3,2,1,0:T(8,128)S(1)} %get-tuple-element.89.refs_1_, f32[5,3,8,128]{3,2,1,0:T(8,128)S(1)} %get-tuple-element.74.refs_3_.refs_2_, ...), custom_call_target="tpu_custom_call" | custom-call | tf_op jit(solution)/shard_map/pallas_call | solution.py:738
  81.3 2.5 %collective-permute-done.13.refs_3_ = f32[5,3,4,128]{3,2,1,0:T(4,128)S(1)} collective-permute-done((f32[5,3,4,128]{3,2,1,0:T(4,128)S(1)}, f32[5,3,4,128]{3,2,1,0:T(4,128)S(1)}, u32[]{:S(2)}, u32[]{:S(2)}) %collective-permute-start.13) | collective-permute-done | bytes 30752 | tf_op jit(solution)/shard_map/ppermute | solution.py:778
  83.8 1.6 %shard_map.111 = (f32[5,8,8,128]{3,2,1,0:T(8,128)S(1)}, f32[5,8,128]{2,1,0:T(8,128)S(1)}, f32[16,5,32,128]{3,2,1,0:T(8,128)}) custom-call(s32[16]{0:T(128)S(1)} %shard_map.95.info.refs_0_, f32[5,8,8,128]{3,2,1,0:T(8,128)S(1)} %get-tuple-element.89.refs_1_, f32[5,3,4,128]{3,2,1,0:T(4,128)S(1)} %collective-permute-done.12.refs_2_, ...), custom_call_target="tpu_custom_call" | custom-call | tf_op jit(solution)/shard_map/pallas_call | solution.py:738
  85.4 3.8 %all-to-all-start.1 = ((f32[16,5,32,128]{3,2,1,0:T(8,128)}), f32[16,5,32,128]{3,2,1,0:T(8,128)S(1)}, u32[]{:S(2)}, u32[]{:S(2)}) async-start(f32[16,5,32,128]{3,2,1,0:T(8,128)} %get-tuple-element.97), calls=%async_computation.1 | async-start | bytes 2621440 | tf_op jit(solution)/shard_map/all_to_all | solution.py:871
  89.4 2.9 %shard_map.112 = (f32[5,8,8,128]{3,2,1,0:T(8,128)S(1)}, f32[5,8,128]{2,1,0:T(8,128)S(1)}, f32[5,8,128]{2,1,0:T(8,128)S(1)}) custom-call(s32[16]{0:T(128)S(1)} %shard_map.95.info.refs_0_, f32[5,8,8,128]{3,2,1,0:T(8,128)S(1)} %get-tuple-element.98.s, f32[5,8,128]{2,1,0:T(8,128)S(1)} %get-tuple-element.99.rx, f32[5,8,128]{2,1,0:T(8,128)S(1)} %get-tuple-element.100.rz, ...), custom_call_target="tpu_custom_call" | custom-call | tf_op jit(solution)/shard_map/pallas_call | solution.py:738
  92.3 1.9 %collective-permute-start.14 = (f32[5,8,128]{2,1,0:T(8,128)S(1)}, f32[5,8,128]{2,1,0:T(8,128)S(1)}, u32[]{:S(2)}, u32[]{:S(2)}) collective-permute-start(f32[5,8,128]{2,1,0:T(8,128)S(1)} %get-tuple-element.104), channel_id=1, source_target_pairs={{0,8},{16,24},{32,40},{48,56},{64,72},{80,88},{96,104},{112,120},{... | collective-permute-start | bytes 61448 | tf_op jit(solution)/shard_map/ppermute | solution.py:778
  94.2 4.3 %collective-permute-start.15 = (f32[5,8,128]{2,1,0:T(8,128)S(1)}, f32[5,8,128]{2,1,0:T(8,128)S(1)}, u32[]{:S(2)}, u32[]{:S(2)}) collective-permute-start(f32[5,8,128]{2,1,0:T(8,128)S(1)} %get-tuple-element.105), channel_id=1, source_target_pairs={{8,16},{24,32},{40,48},{56,64},{72,80},{88,96},{104,112},{120,0},{... | collective-permute-start | bytes 61448 | tf_op jit(solution)/shard_map/ppermute | solution.py:778
  98.5 5.9 %collective-permute-done.14.ra = f32[5,8,128]{2,1,0:T(8,128)S(1)} collective-permute-done((f32[5,8,128]{2,1,0:T(8,128)S(1)}, f32[5,8,128]{2,1,0:T(8,128)S(1)}, u32[]{:S(2)}, u32[]{:S(2)}) %collective-permute-start.14) | collective-permute-done | bytes 20512 | tf_op jit(solution)/shard_map/ppermute | solution.py:778
  104.4 2.5 %collective-permute-done.15.rb = f32[5,8,128]{2,1,0:T(8,128)S(1)} collective-permute-done((f32[5,8,128]{2,1,0:T(8,128)S(1)}, f32[5,8,128]{2,1,0:T(8,128)S(1)}, u32[]{:S(2)}, u32[]{:S(2)}) %collective-permute-start.15) | collective-permute-done | bytes 20512 | tf_op jit(solution)/shard_map/ppermute | solution.py:778
  106.9 1.7 %all-to-all-done.1.far = f32[16,5,32,128]{3,2,1,0:T(8,128)S(1)} async-done(((f32[16,5,32,128]{3,2,1,0:T(8,128)}), f32[16,5,32,128]{3,2,1,0:T(8,128)S(1)}, u32[]{:S(2)}, u32[]{:S(2)}) %all-to-all-start.1) | async-done | bytes 1310752 | tf_op jit(solution)/shard_map/all_to_all | solution.py:871
  108.6 2.0 %shard_map.113 = (f32[5,8,8,120]{3,2,1,0:T(8,128)}, f32[1,4,5,16,256]{4,3,2,1,0:T(8,128)}) custom-call(s32[16]{0:T(128)S(1)} %shard_map.95.info.refs_0_, f32[16,5,32,128]{3,2,1,0:T(8,128)S(1)} %all-to-all-done.1.far, f32[1,4,5,16,256]{4,3,2,1,0:T(8,128)} %copy-done.3, f32[5,8,8,128]{3,2,1,0:T(8,128)S(1)} %get-tuple-element.103.w, ...), custom_call_target="tpu_custom_call", output_to_operand_aliasing={{1}: (2, {})} | custom-call | tf_op jit(solution)/shard_map/pallas_call | solution.py:738
  (22 shorter events, 0.1 us)
Async XLA Ops:
  1.3 0.7 copy-start
  5.8 30.0 %all-to-all-start = ((f32[16,5,32,128]{3,2,1,0:T(8,128)}), f32[16,5,32,128]{3,2,1,0:T(8,128)S(1)}, u32[]{:S(2)}, u32[]{:S(2)}) async-start(f32[16,5,32,128]{3,2,1,0:T(8,128)} %shard_map.96), calls=%async_computation | async-start | bytes 2621440 | tf_op jit(solution)/shard_map/all_to_all | solution.py:794
  15.2 4.3 %collective-permute-start.2 = (f32[8,128]{1,0:T(8,128)S(1)}, f32[8,128]{1,0:T(8,128)S(1)}, u32[]{:S(2)}, u32[]{:S(2)}) collective-permute-start(f32[8,128]{1,0:T(8,128)S(1)} %get-tuple-element.58), channel_id=1, source_target_pairs={{0,1},{1,2},{2,3},{3,4},{4,5},{5,6},{6,7},{7,0},{8,9},{9,10},{10,1... | collective-permute-start | bytes 12296 | tf_op jit(solution)/shard_map/ppermute | solution.py:769
  15.2 4.3 %collective-permute-start.3 = (f32[8,128]{1,0:T(8,128)S(1)}, f32[8,128]{1,0:T(8,128)S(1)}, u32[]{:S(2)}, u32[]{:S(2)}) collective-permute-start(f32[8,128]{1,0:T(8,128)S(1)} %get-tuple-element.59), channel_id=1, source_target_pairs={{1,0},{2,1},{3,2},{4,3},{5,4},{6,5},{7,6},{0,7},{9,8},{10,9},{11,1... | collective-permute-start | bytes 12296 | tf_op jit(solution)/shard_map/ppermute | solution.py:770
  19.6 18.3 %collective-permute-start.4 = (f32[5,8,8,128]{3,2,1,0:T(8,128)S(1)}, f32[5,8,8,128]{3,2,1,0:T(8,128)S(1)}, u32[]{:S(2)}, u32[]{:S(2)}) collective-permute-start(f32[5,8,8,128]{3,2,1,0:T(8,128)S(1)} %shard_map.99.refs_1_.u.u0), channel_id=1, source_target_pairs={{0,8},{16,24},{32,40},{48,56},{64,72},{80,88},{96,104},{112,120},{... | collective-permute-start | bytes 491528 | tf_op jit(solution)/shard_map/ppermute | solution.py:778
  21.6 16.3 %collective-permute-start.5 = (f32[5,8,8,128]{3,2,1,0:T(8,128)S(1)}, f32[5,8,8,128]{3,2,1,0:T(8,128)S(1)}, u32[]{:S(2)}, u32[]{:S(2)}) collective-permute-start(f32[5,8,8,128]{3,2,1,0:T(8,128)S(1)} %shard_map.99.refs_1_.u.u0), channel_id=1, source_target_pairs={{8,16},{24,32},{40,48},{56,64},{72,80},{88,96},{104,112},{120,0},{... | collective-permute-start | bytes 491528 | tf_op jit(solution)/shard_map/ppermute | solution.py:778
  36.5 6.8 %collective-permute-start = (f32[5,3,4,128]{3,2,1,0:T(4,128)S(1)}, f32[5,3,4,128]{3,2,1,0:T(4,128)S(1)}, u32[]{:S(2)}, u32[]{:S(2)}) collective-permute-start(f32[5,3,4,128]{3,2,1,0:T(4,128)S(1)} %get-tuple-element.55), channel_id=1, source_target_pairs={{0,8},{16,24},{32,40},{48,56},{64,72},{80,88},{96,104},{112,120},{... | collective-permute-start | bytes 92168 | tf_op jit(solution)/shard_map/ppermute | solution.py:778
  36.7 7.2 %collective-permute-start.1 = (f32[5,3,4,128]{3,2,1,0:T(4,128)S(1)}, f32[5,3,4,128]{3,2,1,0:T(4,128)S(1)}, u32[]{:S(2)}, u32[]{:S(2)}) collective-permute-start(f32[5,3,4,128]{3,2,1,0:T(4,128)S(1)} %get-tuple-element.56), channel_id=1, source_target_pairs={{8,16},{24,32},{40,48},{56,64},{72,80},{88,96},{104,112},{120,0},{... | collective-permute-start | bytes 92168 | tf_op jit(solution)/shard_map/ppermute | solution.py:778
  44.9 22.1 %collective-permute-start.6 = (f32[5,3,4,128]{3,2,1,0:T(4,128)S(1)}, f32[5,3,4,128]{3,2,1,0:T(4,128)S(1)}, u32[]{:S(2)}, u32[]{:S(2)}) collective-permute-start(f32[5,3,4,128]{3,2,1,0:T(4,128)S(1)} %get-tuple-element.66), channel_id=1, source_target_pairs={{0,8},{16,24},{32,40},{48,56},{64,72},{80,88},{96,104},{112,120},{... | collective-permute-start | bytes 92168 | tf_op jit(solution)/shard_map/ppermute | solution.py:778
  45.0 21.9 %collective-permute-start.7 = (f32[5,3,4,128]{3,2,1,0:T(4,128)S(1)}, f32[5,3,4,128]{3,2,1,0:T(4,128)S(1)}, u32[]{:S(2)}, u32[]{:S(2)}) collective-permute-start(f32[5,3,4,128]{3,2,1,0:T(4,128)S(1)} %get-tuple-element.67), channel_id=1, source_target_pairs={{8,16},{24,32},{40,48},{56,64},{72,80},{88,96},{104,112},{120,0},{... | collective-permute-start | bytes 92168 | tf_op jit(solution)/shard_map/ppermute | solution.py:778
  53.6 4.3 %collective-permute-start.8 = (f32[8,128]{1,0:T(8,128)S(1)}, f32[8,128]{1,0:T(8,128)S(1)}, u32[]{:S(2)}, u32[]{:S(2)}) collective-permute-start(f32[8,128]{1,0:T(8,128)S(1)} %get-tuple-element.71), channel_id=1, source_target_pairs={{0,1},{1,2},{2,3},{3,4},{4,5},{5,6},{6,7},{7,0},{8,9},{9,10},{10,1... | collective-permute-start | bytes 12296 | tf_op jit(solution)/shard_map/ppermute | solution.py:769
  53.6 4.3 %collective-permute-start.9 = (f32[8,128]{1,0:T(8,128)S(1)}, f32[8,128]{1,0:T(8,128)S(1)}, u32[]{:S(2)}, u32[]{:S(2)}) collective-permute-start(f32[8,128]{1,0:T(8,128)S(1)} %get-tuple-element.72), channel_id=1, source_target_pairs={{1,0},{2,1},{3,2},{4,3},{5,4},{6,5},{7,6},{0,7},{9,8},{10,9},{11,1... | collective-permute-start | bytes 12296 | tf_op jit(solution)/shard_map/ppermute | solution.py:770
  67.9 5.1 %collective-permute-start.10 = (f32[5,3,4,128]{3,2,1,0:T(4,128)S(1)}, f32[5,3,4,128]{3,2,1,0:T(4,128)S(1)}, u32[]{:S(2)}, u32[]{:S(2)}) collective-permute-start(f32[5,3,4,128]{3,2,1,0:T(4,128)S(1)} %get-tuple-element.82), channel_id=1, source_target_pairs={{0,8},{16,24},{32,40},{48,56},{64,72},{80,88},{96,104},{112,120},{... | collective-permute-start | bytes 92168 | tf_op jit(solution)/shard_map/ppermute | solution.py:778
  68.0 7.5 %collective-permute-start.11 = (f32[5,3,4,128]{3,2,1,0:T(4,128)S(1)}, f32[5,3,4,128]{3,2,1,0:T(4,128)S(1)}, u32[]{:S(2)}, u32[]{:S(2)}) collective-permute-start(f32[5,3,4,128]{3,2,1,0:T(4,128)S(1)} %get-tuple-element.83), channel_id=1, source_target_pairs={{8,16},{24,32},{40,48},{56,64},{72,80},{88,96},{104,112},{120,0},{... | collective-permute-start | bytes 92168 | tf_op jit(solution)/shard_map/ppermute | solution.py:778
  76.4 4.9 %collective-permute-start.12 = (f32[5,3,4,128]{3,2,1,0:T(4,128)S(1)}, f32[5,3,4,128]{3,2,1,0:T(4,128)S(1)}, u32[]{:S(2)}, u32[]{:S(2)}) collective-permute-start(f32[5,3,4,128]{3,2,1,0:T(4,128)S(1)} %get-tuple-element.90), channel_id=1, source_target_pairs={{0,8},{16,24},{32,40},{48,56},{64,72},{80,88},{96,104},{112,120},{... | collective-permute-start | bytes 92168 | tf_op jit(solution)/shard_map/ppermute | solution.py:778
  76.5 7.3 %collective-permute-start.13 = (f32[5,3,4,128]{3,2,1,0:T(4,128)S(1)}, f32[5,3,4,128]{3,2,1,0:T(4,128)S(1)}, u32[]{:S(2)}, u32[]{:S(2)}) collective-permute-start(f32[5,3,4,128]{3,2,1,0:T(4,128)S(1)} %get-tuple-element.91), channel_id=1, source_target_pairs={{8,16},{24,32},{40,48},{56,64},{72,80},{88,96},{104,112},{120,0},{... | collective-permute-start | bytes 92168 | tf_op jit(solution)/shard_map/ppermute | solution.py:778
  85.4 3.9 %copy-start.1 = (f32[1,4,16,256]{3,2,1,0:T(8,128)S(1)}, f32[1,4,16,256]{3,2,1,0:T(8,128)}, u32[]{:S(2)}) copy-start(f32[1,4,16,256]{3,2,1,0:T(8,128)} %dens_far.2) | copy-start | bytes 196612
  85.4 3.9 %copy-start.2 = (f32[1,4,3,16,256]{4,3,2,1,0:T(8,128)S(1)}, f32[1,4,3,16,256]{4,3,2,1,0:T(8,128)}, u32[]{:S(2)}) copy-start(f32[1,4,3,16,256]{4,3,2,1,0:T(8,128)} %vel_far.2) | copy-start | bytes 589828
  85.4 23.2 %all-to-all-start.1 = ((f32[16,5,32,128]{3,2,1,0:T(8,128)}), f32[16,5,32,128]{3,2,1,0:T(8,128)S(1)}, u32[]{:S(2)}, u32[]{:S(2)}) async-start(f32[16,5,32,128]{3,2,1,0:T(8,128)} %get-tuple-element.97), calls=%async_computation.1 | async-start | bytes 2621440 | tf_op jit(solution)/shard_map/all_to_all | solution.py:871
  89.3 9.2 %copy-start.4 = (f32[1,4,16,256]{3,2,1,0:T(8,128)S(1)}, f32[1,4,16,256]{3,2,1,0:T(8,128)}, u32[]{:S(2)}) copy-start(f32[1,4,16,256]{3,2,1,0:T(8,128)} %pres_far.2) | copy-start | bytes 196612
  92.3 12.1 %collective-permute-start.14 = (f32[5,8,128]{2,1,0:T(8,128)S(1)}, f32[5,8,128]{2,1,0:T(8,128)S(1)}, u32[]{:S(2)}, u32[]{:S(2)}) collective-permute-start(f32[5,8,128]{2,1,0:T(8,128)S(1)} %get-tuple-element.104), channel_id=1, source_target_pairs={{0,8},{16,24},{32,40},{48,56},{64,72},{80,88},{96,104},{112,120},{... | collective-permute-start | bytes 61448 | tf_op jit(solution)/shard_map/ppermute | solution.py:778
  94.2 12.7 %collective-permute-start.15 = (f32[5,8,128]{2,1,0:T(8,128)S(1)}, f32[5,8,128]{2,1,0:T(8,128)S(1)}, u32[]{:S(2)}, u32[]{:S(2)}) collective-permute-start(f32[5,8,128]{2,1,0:T(8,128)S(1)} %get-tuple-element.105), channel_id=1, source_target_pairs={{8,16},{24,32},{40,48},{56,64},{72,80},{88,96},{104,112},{120,0},{... | collective-permute-start | bytes 61448 | tf_op jit(solution)/shard_map/ppermute | solution.py:778
  98.5 10.1 %copy-start.3 = (f32[1,4,5,16,256]{4,3,2,1,0:T(8,128)}, f32[1,4,5,16,256]{4,3,2,1,0:T(8,128)S(1)}, u32[]{:S(2)}) copy-start(f32[1,4,5,16,256]{4,3,2,1,0:T(8,128)S(1)} %fusion.6.initial) | copy-start | bytes 983044

commit v3 on v2

--- a/solution.py
+++ b/solution.py
@@ -697,7 +697,7 @@
             out[c, x] = jnp.where(covered, 0.125 * mean[at : at + 8], w)
 
 
-def last_kernel(info, far, initial, w, ra, rb, coarse, fine, sem):
+def home_kernel(info, far, initial, fine, sem):
     for s in range(4):
 
         @pl.when(s < info[COUNT])
@@ -705,6 +705,15 @@
             for cp in home_copies(info, far, fine, sem, s):
                 cp.start()
 
+    for s in range(4):
+
+        @pl.when(s < info[COUNT])
+        def _():
+            for cp in home_copies(info, far, fine, sem, s):
+                cp.wait()
+
+
+def last_kernel(info, w, ra, rb, coarse):
     lane = lanes()
     z0 = [info[Z0], info[Z0 + 1]]
     inside = [(lane >= z0[p]) & (lane < z0[p] + 8) for p in range(2)]
@@ -717,13 +726,6 @@
         coarse[c, 7] = final[:, :LIVE_Z]
         for x in range(1, 7):
             coarse[c, x] = w[c, x, :, pl.ds(0, LIVE_Z)]
-
-    for s in range(4):
-
-        @pl.when(s < info[COUNT])
-        def _():
-            for cp in home_copies(info, far, fine, sem, s):
-                cp.wait()
 
 
 VM = pl.BlockSpec(memory_space=pltpu.VMEM)
@@ -881,13 +883,14 @@
     initial = jnp.stack(
         cons_of([fdens, fvel[:, :, 0], fvel[:, :, 1], fvel[:, :, 2], fpres]), axis=2
     )
-    coarse_out, fine_out = call(
-        last_kernel,
-        [SM, ANY, ANY] + [VM] * 3,
-        [vm(5, 8, 8, LIVE_Z), (initial.shape, f32, ANY)],
+    (coarse_out,) = call(last_kernel, [SM] + [VM] * 3, [vm(5, 8, 8, LIVE_Z)], [], (info, w, ra, rb))
+    (fine_out,) = call(
+        home_kernel,
+        [SM, ANY, ANY],
+        [(initial.shape, f32, ANY)],
         [dma((4, 4))],
-        (info, home, initial, w, ra, rb),
-        alias={2: 1},
+        (info, home, initial),
+        alias={2: 0},
     )
     return coarse_out, fine_out
 

time: 111 us -> 111 us (level)
  waiting for transfers between devices: 28.3 us -> 27.1 us
    all_to_all x1, waiting for transfers between devices: 1.67 us -> 0.45 us  [local(): home = lax.all_to_all(gone, 'wide', split_axis=0, concat_axis=0, tiled=True)]
    pallas_call x19 -> x20, Pallas kernels: 40.3 us -> 40.9 us  [call(): pl.pallas_call(kernel, in_specs=ins, out_specs=[spec for _, _, spec in ou...]
  transfers between devices with their start and end apart: 18 -> 18, of which waited for: 9 -> 9; matrix products, arithmetic and copies ran while one was open for 0% -> 0% of each run, Pallas kernels for 27% -> 28%
where the time goes in v3:
time: 111 us; the launch traced here: 110 us
  Pallas kernels  40.9 us (37%)
  starting transfers between devices  39.6 us (36%)
  waiting for transfers between devices  27.1 us (24%)
  between operations  1.73 us (2%)
    pallas_call x20, Pallas kernels, call(): pl.pallas_call(kernel, in_specs=ins, out_specs=[spec for _, _, spec in ou...  40.9 us
    ppermute x12, starting transfers between devices, trade(): got.append(lax.ppermute(value, 'wide', pairs + [(j, i) for i, j in pairs]))  21.6 us
    ppermute x12, waiting for transfers between devices, trade(): got.append(lax.ppermute(value, 'wide', pairs + [(j, i) for i, j in pairs]))  13.9 us
    all_to_all x1, waiting for transfers between devices, local(): came = lax.all_to_all(sent, 'wide', split_axis=0, concat_axis=0, tiled=True)  10 us
    all_to_all x1, starting transfers between devices, local(): came = lax.all_to_all(sent, 'wide', split_axis=0, concat_axis=0, tiled=True)  8.22 us
    ppermute x2, starting transfers between devices, swap(): return (below, lax.ppermute(lo, axis, ring(axis, False)))  5.89 us
    all_to_all x1, starting transfers between devices, local(): home = lax.all_to_all(gone, 'wide', split_axis=0, concat_axis=0, tiled=True)  3.84 us
    ppermute x2, waiting for transfers between devices, swap(): below = lax.ppermute(hi, axis, ring(axis, True))  2.57 us
  transfers between devices with their start and end apart: 18, of which 9 were waited for; matrix products, arithmetic and copies ran while one was open for 0% of the time, Pallas kernels for 28%

profile of v3, /device:TPU:0, one launch (start us, length us, event | category | flops | bytes accessed | tf_op | source)
XLA Modules:
  0.0 110.1 jit_solution(5871608501355029216)
XLA Ops:
  1.3 0.6 copy-done
  1.9 1.3 %shard_map.95.info.refs_0_ = s32[16]{0:T(128)S(1)} custom-call(s32[1,16]{1,0:T(1,128)S(1)} %copy-done, s32[1]{0:T(128)S(6)} %copy.25.start, s32[1]{0:T(128)} %bitcast.here), custom_call_target="tpu_custom_call" | custom-call | tf_op jit(solution)/shard_map/pallas_call | solution.py:740
  3.2 2.6 %shard_map.96 = f32[16,5,32,128]{3,2,1,0:T(8,128)} custom-call(s32[16]{0:T(128)S(1)} %shard_map.95.info.refs_0_, f32[1,4,16,256]{3,2,1,0:T(8,128)} %dens_far.2, f32[1,4,3,16,256]{4,3,2,1,0:T(8,128)} %vel_far.2, f32[1,4,16,256]{3,2,1,0:T(8,128)} %pres_far.2), custom_call_target="tpu_custom_call" | custom-call | tf_op jit(solution)/shard_map/pallas_call | solution.py:740
  5.8 8.2 %all-to-all-start = ((f32[16,5,32,128]{3,2,1,0:T(8,128)}), f32[16,5,32,128]{3,2,1,0:T(8,128)S(1)}, u32[]{:S(2)}, u32[]{:S(2)}) async-start(f32[16,5,32,128]{3,2,1,0:T(8,128)} %shard_map.96), calls=%async_computation | async-start | bytes 2621440 | tf_op jit(solution)/shard_map/all_to_all | solution.py:796
  14.1 1.1 %shard_map.98 = (f32[5,8,8,128]{3,2,1,0:T(8,128)S(1)}, f32[8,128]{1,0:T(8,128)S(1)}, f32[8,128]{1,0:T(8,128)S(1)}) custom-call(f32[8,8,120]{2,1,0:T(8,128)} %dens_far.3, f32[3,8,8,120]{3,2,1,0:T(8,128)} %vel_far.3, f32[8,8,120]{2,1,0:T(8,128)} %pres_far.3), custom_call_target="tpu_custom_call" | custom-call | tf_op jit(solution)/shard_map/pallas_call | solution.py:740
  15.2 2.9 %collective-permute-start.3 = (f32[8,128]{1,0:T(8,128)S(1)}, f32[8,128]{1,0:T(8,128)S(1)}, u32[]{:S(2)}, u32[]{:S(2)}) collective-permute-start(f32[8,128]{1,0:T(8,128)S(1)} %get-tuple-element.59), channel_id=1, source_target_pairs={{1,0},{2,1},{3,2},{4,3},{5,4},{6,5},{7,6},{0,7},{9,8},{10,9},{11,1... | collective-permute-start | bytes 12296 | tf_op jit(solution)/shard_map/ppermute | solution.py:772
  18.1 1.3 %collective-permute-done.2.zl = f32[8,128]{1,0:T(8,128)S(1)} collective-permute-done((f32[8,128]{1,0:T(8,128)S(1)}, f32[8,128]{1,0:T(8,128)S(1)}, u32[]{:S(2)}, u32[]{:S(2)}) %collective-permute-start.2) | collective-permute-done | bytes 4128 | tf_op jit(solution)/shard_map/ppermute | solution.py:771
  19.4 0.0 collective-permute-done.3.zh
  19.5 0.1 shard_map.99.refs_1_.u.u0
  19.6 2.0 %collective-permute-start.4 = (f32[5,8,8,128]{3,2,1,0:T(8,128)S(1)}, f32[5,8,8,128]{3,2,1,0:T(8,128)S(1)}, u32[]{:S(2)}, u32[]{:S(2)}) collective-permute-start(f32[5,8,8,128]{3,2,1,0:T(8,128)S(1)} %shard_map.99.refs_1_.u.u0), channel_id=1, source_target_pairs={{0,8},{16,24},{32,40},{48,56},{64,72},{80,88},{96,104},{112,120},{... | collective-permute-start | bytes 491528 | tf_op jit(solution)/shard_map/ppermute | solution.py:780
  21.6 4.2 %collective-permute-start.5 = (f32[5,8,8,128]{3,2,1,0:T(8,128)S(1)}, f32[5,8,8,128]{3,2,1,0:T(8,128)S(1)}, u32[]{:S(2)}, u32[]{:S(2)}) collective-permute-start(f32[5,8,8,128]{3,2,1,0:T(8,128)S(1)} %shard_map.99.refs_1_.u.u0), channel_id=1, source_target_pairs={{8,16},{24,32},{40,48},{56,64},{72,80},{88,96},{104,112},{120,0},{... | collective-permute-start | bytes 491528 | tf_op jit(solution)/shard_map/ppermute | solution.py:780
  25.8 10.0 %all-to-all-done.far = f32[16,5,32,128]{3,2,1,0:T(8,128)S(1)} async-done(((f32[16,5,32,128]{3,2,1,0:T(8,128)}), f32[16,5,32,128]{3,2,1,0:T(8,128)S(1)}, u32[]{:S(2)}, u32[]{:S(2)}) %all-to-all-start) | async-done | bytes 1310752 | tf_op jit(solution)/shard_map/all_to_all | solution.py:796
  35.8 0.7 shard_map.97
  36.5 0.2 collective-permute-start
  36.7 1.2 %collective-permute-start.1 = (f32[5,3,4,128]{3,2,1,0:T(4,128)S(1)}, f32[5,3,4,128]{3,2,1,0:T(4,128)S(1)}, u32[]{:S(2)}, u32[]{:S(2)}) collective-permute-start(f32[5,3,4,128]{3,2,1,0:T(4,128)S(1)} %get-tuple-element.56), channel_id=1, source_target_pairs={{8,16},{24,32},{40,48},{56,64},{72,80},{88,96},{104,112},{120,0},{... | collective-permute-start | bytes 92168 | tf_op jit(solution)/shard_map/ppermute | solution.py:780
  38.0 2.4 %shard_map.100 = (f32[5,3,8,128]{3,2,1,0:T(8,128)S(1)}, f32[5,3,8,128]{3,2,1,0:T(8,128)S(1)}) custom-call(s32[16]{0:T(128)S(1)} %shard_map.95.info.refs_0_, f32[5,8,8,128]{3,2,1,0:T(8,128)S(1)} %shard_map.99.refs_1_.u.u0, f32[5,8,8,128]{3,2,1,0:T(8,128)S(1)} %collective-permute-done.4.refs_2_.ra, f32[5,8,8,128]{3,2,1,0:T(8,128)S(1)} %collective-permute-done.5.refs_3_.rb), custom_call_target="tpu_custom_call" | custom-call | tf_op jit(solution)/shard_map/pallas_call | solution.py:740
  40.4 2.9 %shard_map.101 = (f32[5,8,8,128]{3,2,1,0:T(8,128)S(1)}, f32[5,8,8,128]{3,2,1,0:T(8,128)S(1)}, f32[5,8,128]{2,1,0:T(8,128)S(1)}, f32[5,5,8,128]{3,2,1,0:T(8,128)S(1)}) custom-call(s32[16]{0:T(128)S(1)} %shard_map.95.info.refs_0_, f32[5,8,8,128]{3,2,1,0:T(8,128)S(1)} %get-tuple-element.54.refs_1_.refs_9_, f32[5,3,8,128]{3,2,1,0:T(8,128)S(1)} %get-tuple-element.60.refs_2_), custom_call_target="tpu_custom_call" | custom-call | tf_op jit(solution)/shard_map/pallas_call | solution.py:740
  43.3 0.6 collective-permute-done.1.refs_3_
  43.9 0.9 shard_map.102
  44.9 0.2 collective-permute-start.6
  45.0 3.5 %collective-permute-start.7 = (f32[5,3,4,128]{3,2,1,0:T(4,128)S(1)}, f32[5,3,4,128]{3,2,1,0:T(4,128)S(1)}, u32[]{:S(2)}, u32[]{:S(2)}) collective-permute-start(f32[5,3,4,128]{3,2,1,0:T(4,128)S(1)} %get-tuple-element.67), channel_id=1, source_target_pairs={{8,16},{24,32},{40,48},{56,64},{72,80},{88,96},{104,112},{120,0},{... | collective-permute-start | bytes 92168 | tf_op jit(solution)/shard_map/ppermute | solution.py:780
  48.5 5.1 %shard_map.103 = (f32[5,18,8,128]{3,2,1,0:T(8,128)S(1)}, f32[8,128]{1,0:T(8,128)S(1)}, f32[8,128]{1,0:T(8,128)S(1)}, f32[5,2,8,128]{3,2,1,0:T(8,128)S(1)}, f32[5,8,8,128]{3,2,1,0:T(8,128)S(1)}) custom-call(s32[16]{0:T(128)S(1)} %shard_map.95.info.refs_0_, f32[5,8,8,128]{3,2,1,0:T(8,128)S(1)} %shard_map.99.refs_1_.u.u0, ...), custom_call_target="tpu_custom_call" | custom-call | tf_op jit(solution)/shard_map/pallas_call | solution.py:740
  53.6 2.9 %collective-permute-start.9 = (f32[8,128]{1,0:T(8,128)S(1)}, f32[8,128]{1,0:T(8,128)S(1)}, u32[]{:S(2)}, u32[]{:S(2)}) collective-permute-start(f32[8,128]{1,0:T(8,128)S(1)} %get-tuple-element.72), channel_id=1, source_target_pairs={{1,0},{2,1},{3,2},{4,3},{5,4},{6,5},{7,6},{0,7},{9,8},{10,9},{11,1... | collective-permute-start | bytes 12296 | tf_op jit(solution)/shard_map/ppermute | solution.py:772
  56.6 1.3 %collective-permute-done.8.zl = f32[8,128]{1,0:T(8,128)S(1)} collective-permute-done((f32[8,128]{1,0:T(8,128)S(1)}, f32[8,128]{1,0:T(8,128)S(1)}, u32[]{:S(2)}, u32[]{:S(2)}) %collective-permute-start.8) | collective-permute-done | bytes 4128 | tf_op jit(solution)/shard_map/ppermute | solution.py:771
  57.9 0.0 collective-permute-done.9.zh
  57.9 3.7 %shard_map.104 = (f32[5,12,8,128]{3,2,1,0:T(8,128)S(1)}, f32[5,2,8,128]{3,2,1,0:T(8,128)S(1)}, f32[5,8,8,128]{3,2,1,0:T(8,128)S(1)}) custom-call(s32[16]{0:T(128)S(1)} %shard_map.95.info.refs_0_, f32[5,8,8,128]{3,2,1,0:T(8,128)S(1)} %shard_map.99.refs_1_.u.u0, f32[5,8,8,128]{3,2,1,0:T(8,128)S(1)} %collective-permute-done.4.refs_2_.ra, ...), custom_call_target="tpu_custom_call" | custom-call | tf_op jit(solution)/shard_map/pallas_call | solution.py:740
  61.6 2.4 %shard_map.105 = (f32[5,3,8,128]{3,2,1,0:T(8,128)S(1)}, f32[5,3,8,128]{3,2,1,0:T(8,128)S(1)}) custom-call(s32[16]{0:T(128)S(1)} %shard_map.95.info.refs_0_, f32[5,12,8,128]{3,2,1,0:T(8,128)S(1)} %get-tuple-element.73.refs_1_.new), custom_call_target="tpu_custom_call" | custom-call | tf_op jit(solution)/shard_map/pallas_call | solution.py:740
  64.0 2.9 %shard_map.106 = (f32[5,8,8,128]{3,2,1,0:T(8,128)S(1)}, f32[5,8,8,128]{3,2,1,0:T(8,128)S(1)}, f32[5,8,128]{2,1,0:T(8,128)S(1)}, f32[5,5,8,128]{3,2,1,0:T(8,128)S(1)}) custom-call(s32[16]{0:T(128)S(1)} %shard_map.95.info.refs_0_, f32[5,8,8,128]{3,2,1,0:T(8,128)S(1)} %get-tuple-element.65.refs_1_, f32[5,3,8,128]{3,2,1,0:T(8,128)S(1)} %get-tuple-element.60.refs_2_, ...), custom_call_target="tpu_custom_call" | custom-call | tf_op jit(solution)/shard_map/pallas_call | solution.py:740
  66.9 0.9 shard_map.107
  67.9 0.1 collective-permute-start.10
  68.0 2.1 %collective-permute-start.11 = (f32[5,3,4,128]{3,2,1,0:T(4,128)S(1)}, f32[5,3,4,128]{3,2,1,0:T(4,128)S(1)}, u32[]{:S(2)}, u32[]{:S(2)}) collective-permute-start(f32[5,3,4,128]{3,2,1,0:T(4,128)S(1)} %get-tuple-element.83), channel_id=1, source_target_pairs={{8,16},{24,32},{40,48},{56,64},{72,80},{88,96},{104,112},{120,0},{... | collective-permute-start | bytes 92168 | tf_op jit(solution)/shard_map/ppermute | solution.py:780
  70.1 2.9 %shard_map.108 = (f32[5,8,8,128]{3,2,1,0:T(8,128)S(1)}, f32[5,8,8,128]{3,2,1,0:T(8,128)S(1)}, f32[5,8,128]{2,1,0:T(8,128)S(1)}, f32[5,5,8,128]{3,2,1,0:T(8,128)S(1)}) custom-call(s32[16]{0:T(128)S(1)} %shard_map.95.info.refs_0_, f32[5,8,8,128]{3,2,1,0:T(8,128)S(1)} %get-tuple-element.81.refs_1_.refs_8_, f32[5,3,8,128]{3,2,1,0:T(8,128)S(1)} %get-tuple-element.60.refs_2_, ...), custom_call_target="tpu_custom_call" | custom-call | tf_op jit(solution)/shard_map/pallas_call | solution.py:740
  73.0 2.5 %collective-permute-done.11.refs_3_ = f32[5,3,4,128]{3,2,1,0:T(4,128)S(1)} collective-permute-done((f32[5,3,4,128]{3,2,1,0:T(4,128)S(1)}, f32[5,3,4,128]{3,2,1,0:T(4,128)S(1)}, u32[]{:S(2)}, u32[]{:S(2)}) %collective-permute-start.11) | collective-permute-done | bytes 30752 | tf_op jit(solution)/shard_map/ppermute | solution.py:780
  75.4 0.9 shard_map.109
  76.4 0.1 collective-permute-start.12
  76.5 1.9 %collective-permute-start.13 = (f32[5,3,4,128]{3,2,1,0:T(4,128)S(1)}, f32[5,3,4,128]{3,2,1,0:T(4,128)S(1)}, u32[]{:S(2)}, u32[]{:S(2)}) collective-permute-start(f32[5,3,4,128]{3,2,1,0:T(4,128)S(1)} %get-tuple-element.91), channel_id=1, source_target_pairs={{8,16},{24,32},{40,48},{56,64},{72,80},{88,96},{104,112},{120,0},{... | collective-permute-start | bytes 92168 | tf_op jit(solution)/shard_map/ppermute | solution.py:780
  78.4 2.9 %shard_map.110 = (f32[5,8,8,128]{3,2,1,0:T(8,128)S(1)}, f32[5,8,8,128]{3,2,1,0:T(8,128)S(1)}, f32[5,8,128]{2,1,0:T(8,128)S(1)}, f32[5,5,8,128]{3,2,1,0:T(8,128)S(1)}) custom-call(s32[16]{0:T(128)S(1)} %shard_map.95.info.refs_0_, f32[5,8,8,128]{3,2,1,0:T(8,128)S(1)} %get-tuple-element.89.refs_1_, f32[5,3,8,128]{3,2,1,0:T(8,128)S(1)} %get-tuple-element.74.refs_3_.refs_2_, ...), custom_call_target="tpu_custom_call" | custom-call | tf_op jit(solution)/shard_map/pallas_call | solution.py:740
  81.3 2.5 %collective-permute-done.13.refs_3_ = f32[5,3,4,128]{3,2,1,0:T(4,128)S(1)} collective-permute-done((f32[5,3,4,128]{3,2,1,0:T(4,128)S(1)}, f32[5,3,4,128]{3,2,1,0:T(4,128)S(1)}, u32[]{:S(2)}, u32[]{:S(2)}) %collective-permute-start.13) | collective-permute-done | bytes 30752 | tf_op jit(solution)/shard_map/ppermute | solution.py:780
  83.8 1.6 %shard_map.111 = (f32[5,8,8,128]{3,2,1,0:T(8,128)S(1)}, f32[5,8,128]{2,1,0:T(8,128)S(1)}, f32[16,5,32,128]{3,2,1,0:T(8,128)}) custom-call(s32[16]{0:T(128)S(1)} %shard_map.95.info.refs_0_, f32[5,8,8,128]{3,2,1,0:T(8,128)S(1)} %get-tuple-element.89.refs_1_, f32[5,3,4,128]{3,2,1,0:T(4,128)S(1)} %collective-permute-done.12.refs_2_, ...), custom_call_target="tpu_custom_call" | custom-call | tf_op jit(solution)/shard_map/pallas_call | solution.py:740
  85.4 3.8 %all-to-all-start.1 = ((f32[16,5,32,128]{3,2,1,0:T(8,128)}), f32[16,5,32,128]{3,2,1,0:T(8,128)S(1)}, u32[]{:S(2)}, u32[]{:S(2)}) async-start(f32[16,5,32,128]{3,2,1,0:T(8,128)} %get-tuple-element.105), calls=%async_computation.1 | async-start | bytes 2621440 | tf_op jit(solution)/shard_map/all_to_all | solution.py:873
  89.4 2.9 %shard_map.112 = (f32[5,8,8,128]{3,2,1,0:T(8,128)S(1)}, f32[5,8,128]{2,1,0:T(8,128)S(1)}, f32[5,8,128]{2,1,0:T(8,128)S(1)}) custom-call(s32[16]{0:T(128)S(1)} %shard_map.95.info.refs_0_, f32[5,8,8,128]{3,2,1,0:T(8,128)S(1)} %get-tuple-element.97.s, f32[5,8,128]{2,1,0:T(8,128)S(1)} %get-tuple-element.98.rx, f32[5,8,128]{2,1,0:T(8,128)S(1)} %get-tuple-element.99.rz, ...), custom_call_target="tpu_custom_call" | custom-call | tf_op jit(solution)/shard_map/pallas_call | solution.py:740
  92.3 1.9 %collective-permute-start.14 = (f32[5,8,128]{2,1,0:T(8,128)S(1)}, f32[5,8,128]{2,1,0:T(8,128)S(1)}, u32[]{:S(2)}, u32[]{:S(2)}) collective-permute-start(f32[5,8,128]{2,1,0:T(8,128)S(1)} %get-tuple-element.103), channel_id=1, source_target_pairs={{0,8},{16,24},{32,40},{48,56},{64,72},{80,88},{96,104},{112,120},{... | collective-permute-start | bytes 61448 | tf_op jit(solution)/shard_map/ppermute | solution.py:780
  94.2 4.3 %collective-permute-start.15 = (f32[5,8,128]{2,1,0:T(8,128)S(1)}, f32[5,8,128]{2,1,0:T(8,128)S(1)}, u32[]{:S(2)}, u32[]{:S(2)}) collective-permute-start(f32[5,8,128]{2,1,0:T(8,128)S(1)} %get-tuple-element.104), channel_id=1, source_target_pairs={{8,16},{24,32},{40,48},{56,64},{72,80},{88,96},{104,112},{120,0},{... | collective-permute-start | bytes 61448 | tf_op jit(solution)/shard_map/ppermute | solution.py:780
  98.5 5.9 %collective-permute-done.14.ra = f32[5,8,128]{2,1,0:T(8,128)S(1)} collective-permute-done((f32[5,8,128]{2,1,0:T(8,128)S(1)}, f32[5,8,128]{2,1,0:T(8,128)S(1)}, u32[]{:S(2)}, u32[]{:S(2)}) %collective-permute-start.14) | collective-permute-done | bytes 20512 | tf_op jit(solution)/shard_map/ppermute | solution.py:780
  104.4 2.5 %collective-permute-done.15.rb = f32[5,8,128]{2,1,0:T(8,128)S(1)} collective-permute-done((f32[5,8,128]{2,1,0:T(8,128)S(1)}, f32[5,8,128]{2,1,0:T(8,128)S(1)}, u32[]{:S(2)}, u32[]{:S(2)}) %collective-permute-start.15) | collective-permute-done | bytes 20512 | tf_op jit(solution)/shard_map/ppermute | solution.py:780
  106.9 1.2 %shard_map.113 = f32[5,8,8,120]{3,2,1,0:T(8,128)} custom-call(s32[16]{0:T(128)S(1)} %shard_map.95.info.refs_0_, f32[5,8,8,128]{3,2,1,0:T(8,128)S(1)} %get-tuple-element.102.w, f32[5,8,128]{2,1,0:T(8,128)S(1)} %collective-permute-done.14.ra, f32[5,8,128]{2,1,0:T(8,128)S(1)} %collective-permute-done.15.rb), custom_call_target="tpu_custom_call" | custom-call | tf_op jit(solution)/shard_map/pallas_call | solution.py:740
  108.1 0.4 all-to-all-done.1.far
  108.6 1.3 %shard_map.114 = f32[1,4,5,16,256]{4,3,2,1,0:T(8,128)} custom-call(s32[16]{0:T(128)S(1)} %shard_map.95.info.refs_0_, f32[16,5,32,128]{3,2,1,0:T(8,128)S(1)} %all-to-all-done.1.far, f32[1,4,5,16,256]{4,3,2,1,0:T(8,128)} %copy-done.3), custom_call_target="tpu_custom_call", output_to_operand_aliasing={{}: (2, {})} | custom-call | tf_op jit(solution)/shard_map/pallas_call | solution.py:740
  (23 shorter events, 0.2 us)
Async XLA Ops:
  1.3 0.7 copy-start
  5.8 30.0 %all-to-all-start = ((f32[16,5,32,128]{3,2,1,0:T(8,128)}), f32[16,5,32,128]{3,2,1,0:T(8,128)S(1)}, u32[]{:S(2)}, u32[]{:S(2)}) async-start(f32[16,5,32,128]{3,2,1,0:T(8,128)} %shard_map.96), calls=%async_computation | async-start | bytes 2621440 | tf_op jit(solution)/shard_map/all_to_all | solution.py:796
  15.2 4.3 %collective-permute-start.2 = (f32[8,128]{1,0:T(8,128)S(1)}, f32[8,128]{1,0:T(8,128)S(1)}, u32[]{:S(2)}, u32[]{:S(2)}) collective-permute-start(f32[8,128]{1,0:T(8,128)S(1)} %get-tuple-element.58), channel_id=1, source_target_pairs={{0,1},{1,2},{2,3},{3,4},{4,5},{5,6},{6,7},{7,0},{8,9},{9,10},{10,1... | collective-permute-start | bytes 12296 | tf_op jit(solution)/shard_map/ppermute | solution.py:771
  15.2 4.3 %collective-permute-start.3 = (f32[8,128]{1,0:T(8,128)S(1)}, f32[8,128]{1,0:T(8,128)S(1)}, u32[]{:S(2)}, u32[]{:S(2)}) collective-permute-start(f32[8,128]{1,0:T(8,128)S(1)} %get-tuple-element.59), channel_id=1, source_target_pairs={{1,0},{2,1},{3,2},{4,3},{5,4},{6,5},{7,6},{0,7},{9,8},{10,9},{11,1... | collective-permute-start | bytes 12296 | tf_op jit(solution)/shard_map/ppermute | solution.py:772
  19.6 18.3 %collective-permute-start.4 = (f32[5,8,8,128]{3,2,1,0:T(8,128)S(1)}, f32[5,8,8,128]{3,2,1,0:T(8,128)S(1)}, u32[]{:S(2)}, u32[]{:S(2)}) collective-permute-start(f32[5,8,8,128]{3,2,1,0:T(8,128)S(1)} %shard_map.99.refs_1_.u.u0), channel_id=1, source_target_pairs={{0,8},{16,24},{32,40},{48,56},{64,72},{80,88},{96,104},{112,120},{... | collective-permute-start | bytes 491528 | tf_op jit(solution)/shard_map/ppermute | solution.py:780
  21.6 16.3 %collective-permute-start.5 = (f32[5,8,8,128]{3,2,1,0:T(8,128)S(1)}, f32[5,8,8,128]{3,2,1,0:T(8,128)S(1)}, u32[]{:S(2)}, u32[]{:S(2)}) collective-permute-start(f32[5,8,8,128]{3,2,1,0:T(8,128)S(1)} %shard_map.99.refs_1_.u.u0), channel_id=1, source_target_pairs={{8,16},{24,32},{40,48},{56,64},{72,80},{88,96},{104,112},{120,0},{... | collective-permute-start | bytes 491528 | tf_op jit(solution)/shard_map/ppermute | solution.py:780
  36.5 6.8 %collective-permute-start = (f32[5,3,4,128]{3,2,1,0:T(4,128)S(1)}, f32[5,3,4,128]{3,2,1,0:T(4,128)S(1)}, u32[]{:S(2)}, u32[]{:S(2)}) collective-permute-start(f32[5,3,4,128]{3,2,1,0:T(4,128)S(1)} %get-tuple-element.55), channel_id=1, source_target_pairs={{0,8},{16,24},{32,40},{48,56},{64,72},{80,88},{96,104},{112,120},{... | collective-permute-start | bytes 92168 | tf_op jit(solution)/shard_map/ppermute | solution.py:780
  36.7 7.2 %collective-permute-start.1 = (f32[5,3,4,128]{3,2,1,0:T(4,128)S(1)}, f32[5,3,4,128]{3,2,1,0:T(4,128)S(1)}, u32[]{:S(2)}, u32[]{:S(2)}) collective-permute-start(f32[5,3,4,128]{3,2,1,0:T(4,128)S(1)} %get-tuple-element.56), channel_id=1, source_target_pairs={{8,16},{24,32},{40,48},{56,64},{72,80},{88,96},{104,112},{120,0},{... | collective-permute-start | bytes 92168 | tf_op jit(solution)/shard_map/ppermute | solution.py:780
  44.9 22.1 %collective-permute-start.6 = (f32[5,3,4,128]{3,2,1,0:T(4,128)S(1)}, f32[5,3,4,128]{3,2,1,0:T(4,128)S(1)}, u32[]{:S(2)}, u32[]{:S(2)}) collective-permute-start(f32[5,3,4,128]{3,2,1,0:T(4,128)S(1)} %get-tuple-element.66), channel_id=1, source_target_pairs={{0,8},{16,24},{32,40},{48,56},{64,72},{80,88},{96,104},{112,120},{... | collective-permute-start | bytes 92168 | tf_op jit(solution)/shard_map/ppermute | solution.py:780
  45.0 21.9 %collective-permute-start.7 = (f32[5,3,4,128]{3,2,1,0:T(4,128)S(1)}, f32[5,3,4,128]{3,2,1,0:T(4,128)S(1)}, u32[]{:S(2)}, u32[]{:S(2)}) collective-permute-start(f32[5,3,4,128]{3,2,1,0:T(4,128)S(1)} %get-tuple-element.67), channel_id=1, source_target_pairs={{8,16},{24,32},{40,48},{56,64},{72,80},{88,96},{104,112},{120,0},{... | collective-permute-start | bytes 92168 | tf_op jit(solution)/shard_map/ppermute | solution.py:780
  53.6 4.3 %collective-permute-start.8 = (f32[8,128]{1,0:T(8,128)S(1)}, f32[8,128]{1,0:T(8,128)S(1)}, u32[]{:S(2)}, u32[]{:S(2)}) collective-permute-start(f32[8,128]{1,0:T(8,128)S(1)} %get-tuple-element.71), channel_id=1, source_target_pairs={{0,1},{1,2},{2,3},{3,4},{4,5},{5,6},{6,7},{7,0},{8,9},{9,10},{10,1... | collective-permute-start | bytes 12296 | tf_op jit(solution)/shard_map/ppermute | solution.py:771
  53.6 4.3 %collective-permute-start.9 = (f32[8,128]{1,0:T(8,128)S(1)}, f32[8,128]{1,0:T(8,128)S(1)}, u32[]{:S(2)}, u32[]{:S(2)}) collective-permute-start(f32[8,128]{1,0:T(8,128)S(1)} %get-tuple-element.72), channel_id=1, source_target_pairs={{1,0},{2,1},{3,2},{4,3},{5,4},{6,5},{7,6},{0,7},{9,8},{10,9},{11,1... | collective-permute-start | bytes 12296 | tf_op jit(solution)/shard_map/ppermute | solution.py:772
  67.9 5.1 %collective-permute-start.10 = (f32[5,3,4,128]{3,2,1,0:T(4,128)S(1)}, f32[5,3,4,128]{3,2,1,0:T(4,128)S(1)}, u32[]{:S(2)}, u32[]{:S(2)}) collective-permute-start(f32[5,3,4,128]{3,2,1,0:T(4,128)S(1)} %get-tuple-element.82), channel_id=1, source_target_pairs={{0,8},{16,24},{32,40},{48,56},{64,72},{80,88},{96,104},{112,120},{... | collective-permute-start | bytes 92168 | tf_op jit(solution)/shard_map/ppermute | solution.py:780
  68.0 7.5 %collective-permute-start.11 = (f32[5,3,4,128]{3,2,1,0:T(4,128)S(1)}, f32[5,3,4,128]{3,2,1,0:T(4,128)S(1)}, u32[]{:S(2)}, u32[]{:S(2)}) collective-permute-start(f32[5,3,4,128]{3,2,1,0:T(4,128)S(1)} %get-tuple-element.83), channel_id=1, source_target_pairs={{8,16},{24,32},{40,48},{56,64},{72,80},{88,96},{104,112},{120,0},{... | collective-permute-start | bytes 92168 | tf_op jit(solution)/shard_map/ppermute | solution.py:780
  76.4 4.9 %collective-permute-start.12 = (f32[5,3,4,128]{3,2,1,0:T(4,128)S(1)}, f32[5,3,4,128]{3,2,1,0:T(4,128)S(1)}, u32[]{:S(2)}, u32[]{:S(2)}) collective-permute-start(f32[5,3,4,128]{3,2,1,0:T(4,128)S(1)} %get-tuple-element.90), channel_id=1, source_target_pairs={{0,8},{16,24},{32,40},{48,56},{64,72},{80,88},{96,104},{112,120},{... | collective-permute-start | bytes 92168 | tf_op jit(solution)/shard_map/ppermute | solution.py:780
  76.5 7.3 %collective-permute-start.13 = (f32[5,3,4,128]{3,2,1,0:T(4,128)S(1)}, f32[5,3,4,128]{3,2,1,0:T(4,128)S(1)}, u32[]{:S(2)}, u32[]{:S(2)}) collective-permute-start(f32[5,3,4,128]{3,2,1,0:T(4,128)S(1)} %get-tuple-element.91), channel_id=1, source_target_pairs={{8,16},{24,32},{40,48},{56,64},{72,80},{88,96},{104,112},{120,0},{... | collective-permute-start | bytes 92168 | tf_op jit(solution)/shard_map/ppermute | solution.py:780
  85.4 3.9 %copy-start.1 = (f32[1,4,16,256]{3,2,1,0:T(8,128)S(1)}, f32[1,4,16,256]{3,2,1,0:T(8,128)}, u32[]{:S(2)}) copy-start(f32[1,4,16,256]{3,2,1,0:T(8,128)} %dens_far.2) | copy-start | bytes 196612
  85.4 3.9 %copy-start.2 = (f32[1,4,3,16,256]{4,3,2,1,0:T(8,128)S(1)}, f32[1,4,3,16,256]{4,3,2,1,0:T(8,128)}, u32[]{:S(2)}) copy-start(f32[1,4,3,16,256]{4,3,2,1,0:T(8,128)} %vel_far.2) | copy-start | bytes 589828
  85.4 23.2 %all-to-all-start.1 = ((f32[16,5,32,128]{3,2,1,0:T(8,128)}), f32[16,5,32,128]{3,2,1,0:T(8,128)S(1)}, u32[]{:S(2)}, u32[]{:S(2)}) async-start(f32[16,5,32,128]{3,2,1,0:T(8,128)} %get-tuple-element.105), calls=%async_computation.1 | async-start | bytes 2621440 | tf_op jit(solution)/shard_map/all_to_all | solution.py:873
  89.3 9.2 %copy-start.4 = (f32[1,4,16,256]{3,2,1,0:T(8,128)S(1)}, f32[1,4,16,256]{3,2,1,0:T(8,128)}, u32[]{:S(2)}) copy-start(f32[1,4,16,256]{3,2,1,0:T(8,128)} %pres_far.2) | copy-start | bytes 196612
  92.3 12.1 %collective-permute-start.14 = (f32[5,8,128]{2,1,0:T(8,128)S(1)}, f32[5,8,128]{2,1,0:T(8,128)S(1)}, u32[]{:S(2)}, u32[]{:S(2)}) collective-permute-start(f32[5,8,128]{2,1,0:T(8,128)S(1)} %get-tuple-element.103), channel_id=1, source_target_pairs={{0,8},{16,24},{32,40},{48,56},{64,72},{80,88},{96,104},{112,120},{... | collective-permute-start | bytes 61448 | tf_op jit(solution)/shard_map/ppermute | solution.py:780
  94.2 12.7 %collective-permute-start.15 = (f32[5,8,128]{2,1,0:T(8,128)S(1)}, f32[5,8,128]{2,1,0:T(8,128)S(1)}, u32[]{:S(2)}, u32[]{:S(2)}) collective-permute-start(f32[5,8,128]{2,1,0:T(8,128)S(1)} %get-tuple-element.104), channel_id=1, source_target_pairs={{8,16},{24,32},{40,48},{56,64},{72,80},{88,96},{104,112},{120,0},{... | collective-permute-start | bytes 61448 | tf_op jit(solution)/shard_map/ppermute | solution.py:780
  98.5 10.1 %copy-start.3 = (f32[1,4,5,16,256]{4,3,2,1,0:T(8,128)}, f32[1,4,5,16,256]{4,3,2,1,0:T(8,128)S(1)}, u32[]{:S(2)}) copy-start(f32[1,4,5,16,256]{4,3,2,1,0:T(8,128)S(1)} %fusion.6.initial) | copy-start | bytes 983044
